TPU v7x, 512 devices: a 8x2x16 block of a 8x8x16 slice. The times are simulated.
512 devices in a mesh: group: 2 (over y), blk: 32 (over z, core), uly: 8 (over x).
Axes of the slice: x: 8, y: 2, z: 16, core: 2. Of those that a mesh axis runs over, the one named last changes fastest.
The devices are a block of a 8x8x16 slice.
Arguments:
- query: bfloat16 [12288, 3072], P(('group', 'blk', 'uly')), parts along dimension 0, may hold values from -16 to 16
- keys: bfloat16 [12288, 3072], P(('group', 'blk', 'uly')), parts along dimension 0, may hold values from -16 to 16
- values: bfloat16 [12288, 3072], P(('group', 'blk', 'uly')), parts along dimension 0, may hold values from -6 to 6
- out_weight: bfloat16 [3072, 3072], P('uly', 'blk'), may hold values from -1 to 1
- out_gain: float32 [3072], replicated, may hold values from 0.1 to 1.9
Outputs:
- gated_out: bfloat16 [12288, 3072], P(('group', 'blk', 'uly')), parts along dimension 0
There are 2 independent parts, one for each index of `group`. A program takes and returns all parts, laid end to end along the dimension named above; an argument that names none is the same for every part. Nothing has to cross between parts.
All inputs are finite; a program needn't handle non-finite values.
Results may differ from a plain program's by a relative error of at most 0.015.
Values may be sent and summed in bfloat16 or wider, within the bound.
No kernel may reach another device: no remote copies, remote signals or barrier semaphores. Data moves between devices by JAX's collectives and lax.ppermute only.
A program may use at most 128 MiB of HBM per device.

v0:
```python
import functools
import math

import jax
import jax.numpy as jnp
from jax import lax
from jax.experimental import pallas as pl
from jax.experimental.pallas import tpu as pltpu
from jax.sharding import PartitionSpec as P


HEAD = 64
PAIR = 2 * HEAD
STATS = 8
VMEM_LIMIT = 16 * 1024 * 1024
LOG2E = math.log2(math.e)


def nt_dot(a, b):
    return lax.dot_general(a, b, (((1,), (1,)), ((), ())), preferred_element_type=jnp.float32)


def fold_kernel(first, q_ref, *refs):
    state_ref, new_ref = (None, refs[-1]) if first else refs[-2:]
    kv_refs = refs[:-1] if first else refs[:-2]
    features = q_ref.shape[1]
    for pair in range(features // PAIR):
        cols = slice(pair * PAIR, (pair + 1) * PAIR)
        q_pair = q_ref[:, cols]
        lane = lax.broadcasted_iota(jnp.int32, q_pair.shape, 1)
        k_parts = [ref[:, cols] for ref in kv_refs]
        v_parts = [ref[:, slice(features + cols.start, features + cols.stop)].T for ref in kv_refs]
        for half in range(2):
            head = 2 * pair + half
            rows = slice(head * HEAD, (head + 1) * HEAD)
            max_row = slice(features + head, features + head + 1)
            den_row = slice(features + STATS + head, features + STATS + head + 1)
            mine = (lane < HEAD) if half == 0 else (lane >= HEAD)
            q_head = jnp.where(mine, q_pair, jnp.zeros_like(q_pair))
            scores = [nt_dot(k, q_head) for k in k_parts]
            top = jnp.max(scores[0], axis=0, keepdims=True)
            for s in scores[1:]:
                top = jnp.maximum(top, jnp.max(s, axis=0, keepdims=True))
            if not first:
                old_max = state_ref[max_row, :]
                top = jnp.maximum(top, old_max)
                shrink = jnp.exp2((old_max - top) * LOG2E)
            den, acc = 0.0, 0.0
            for s, v in zip(scores, v_parts):
                weights = jnp.exp2((s - top) * LOG2E)
                den = den + jnp.sum(weights, axis=0, keepdims=True)
                acc = acc + jnp.dot(
                    v[half * HEAD : (half + 1) * HEAD, :],
                    weights.astype(jnp.bfloat16),
                    preferred_element_type=jnp.float32,
                )
            if not first:
                den = den + state_ref[den_row, :] * shrink
                acc = acc + state_ref[rows, :] * shrink
            new_ref[max_row, :] = top
            new_ref[den_row, :] = den
            new_ref[rows, :] = acc


def fold(query_rows, blocks, state):
    row_count, features = query_rows.shape
    vmem = pl.BlockSpec(memory_space=pltpu.VMEM)
    operands = (query_rows, *blocks) if state is None else (query_rows, *blocks, state)
    key_count = sum(b.shape[0] for b in blocks)
    return pl.pallas_call(
        functools.partial(fold_kernel, state is None),
        out_shape=jax.ShapeDtypeStruct((features + 2 * STATS, row_count), jnp.float32),
        in_specs=[vmem] * len(operands),
        out_specs=vmem,
        compiler_params=pltpu.CompilerParams(vmem_limit_bytes=VMEM_LIMIT),
        cost_estimate=pl.CostEstimate(
            flops=4 * row_count * key_count * features,
            bytes_accessed=4 * key_count * features,
            transcendentals=row_count * key_count * (features // HEAD),
        ),
    )(*operands)


def merge_kernel(one_ref, two_ref, out_ref):
    features = out_ref.shape[1]
    heads = features // HEAD
    max_rows, den_rows = (slice(features + i, features + i + heads) for i in (0, STATS))
    one_max, two_max = one_ref[max_rows, :], two_ref[max_rows, :]
    top = jnp.maximum(one_max, two_max)
    one, two = (jnp.exp2((m - top) * LOG2E) for m in (one_max, two_max))
    den = one_ref[den_rows, :] * one + two_ref[den_rows, :] * two
    one, two = one / den, two / den
    parts = []
    for head in range(heads):
        rows, row = slice(head * HEAD, (head + 1) * HEAD), slice(head, head + 1)
        parts.append(one_ref[rows, :] * one[row, :] + two_ref[rows, :] * two[row, :])
    out_ref[...] = jnp.concatenate(parts, axis=0).astype(out_ref.dtype).T


def merge(one, two, features):
    vmem = pl.BlockSpec(memory_space=pltpu.VMEM)
    return pl.pallas_call(
        merge_kernel,
        out_shape=jax.ShapeDtypeStruct((one.shape[1], features), jnp.bfloat16),
        in_specs=[vmem] * 2,
        out_specs=vmem,
        compiler_params=pltpu.CompilerParams(vmem_limit_bytes=VMEM_LIMIT),
    )(one, two)


def on_device(query, keys, values, out_weight, out_gain):
    tokens, width = query.shape
    blk, uly = lax.axis_size("blk"), lax.axis_size("uly")
    depth, quad = blk // 2, uly // 2
    features = width // uly
    rows = tokens * uly
    core = lax.axis_index("blk") % 2
    side = lax.axis_index("uly") // quad
    swap = [(i, i ^ 1) for i in range(blk)]
    ring = [
        (2 * z + c, 2 * ((z + (1 if c == 0 else -1)) % depth) + c)
        for z in range(depth)
        for c in range(2)
    ]
    across = [(i, (i + quad) % uly) for i in range(uly)]
    quads = [[h * quad + i for i in range(quad)] for h in range(2)]

    far_weight = lax.ppermute(out_weight, "uly", across)
    both = jnp.concatenate([out_weight, far_weight], axis=0)
    weight = lax.all_gather(both, "blk", axis=1, tiled=True)

    cut = [a.reshape(tokens, uly, features) for a in (query, keys, values)]
    packed = jnp.concatenate(cut, axis=2).transpose(1, 0, 2)
    own = lax.all_to_all(packed, "uly", 0, 0, tiled=True).reshape(rows, 3 * features)
    other = lax.ppermute(own, "blk", swap)
    q_own, q_other = own[:, :features], other[:, :features]
    q_all = jnp.concatenate(
        [jnp.where(core == 0, q_own, q_other), jnp.where(core == 0, q_other, q_own)], axis=0
    ) * jnp.bfloat16(1.0 / math.sqrt(HEAD))

    a, b = own[:, features:], other[:, features:]
    state = fold(q_all, (a,), None)
    last = depth // 2
    for step in range(1, last + 1):
        a = lax.ppermute(a, "blk", ring)
        if step < last:
            b = lax.ppermute(b, "blk", ring)
        state = fold(q_all, (a, b) if step < last else (a,), state)
    theirs = lax.ppermute(state, "blk", swap)
    attended = merge(state, theirs, features)

    half = quad * tokens
    near = lax.dynamic_slice_in_dim(attended, core * rows + side * half, half, axis=0)
    far = lax.dynamic_slice_in_dim(attended, core * rows + (1 - side) * half, half, axis=0)
    far = lax.ppermute(far, "uly", across)
    joined = jnp.concatenate([near, far], axis=1)
    partial = jnp.dot(joined, weight, preferred_element_type=jnp.float32).astype(jnp.bfloat16)
    blocks = lax.all_to_all(
        partial.reshape(quad, tokens, width), "uly", 0, 0, tiled=True, axis_index_groups=quads
    )
    summed = jnp.sum(blocks.astype(jnp.float32), axis=0)
    return (out_gain * summed).astype(jnp.bfloat16)


def solution(mesh):
    in_specs = (
        P(("group", "blk", "uly"), None),
        P(("group", "blk", "uly"), None),
        P(("group", "blk", "uly"), None),
        P("uly", "blk"),
        P(),
    )
    out_specs = P(("group", "blk", "uly"), None)
    return jax.shard_map(
        on_device, mesh=mesh, in_specs=in_specs, out_specs=out_specs, check_vma=False
    )
```

profile of v0, /device:TPU:65, one launch (start us, length us, event | category | flops | bytes accessed | tf_op | source)
XLA Modules:
  0.0 237.1 jit_solution(1691407616615614058)
XLA Ops:
  6.6 8.5 %collective-permute-start.18 = (bf16[384,96]{0,1:T(8,128)(2,1)}, bf16[384,96]{0,1:T(8,128)(2,1)S(1)}, u32[]{:S(2)}, u32[]{:S(2)}) collective-permute-start(bf16[384,96]{0,1:T(8,128)(2,1)} %param.8), channel_id=1, source_target_pairs={{0,4},{1,5},{2,6},{3,7},{4,0},{5,1},{6,2},{7,3},{8,12},{9,13},{10,... | collective-permute-start | bytes 221192 | tf_op jit(solution)/shard_map/ppermute | solution.py:128
  15.0 2.0 collective-permute-done.18
  20.7 19.0 %all_to_all.10 = bf16[8,24,1152]{2,1,0:T(8,128)(2,1)S(1)} all-to-all(bf16[8,24,1152]{2,1,0:T(8,128)(2,1)S(1)} %maximum_bitcast_fusion), channel_id=1, replica_groups=mesh['group'=2,'blk'=32,'uly'=8] {'uly'}, dimensions={0} | all-to-all | bytes 884736 | tf_op jit(solution)/shard_map/all_to_all | solution.py:134
  39.7 39.0 %collective-permute-start = (bf16[192,1152]{1,0:T(8,128)(2,1)S(1)}, bf16[192,1152]{1,0:T(8,128)(2,1)S(1)}, u32[]{:S(2)}, u32[]{:S(2)}) collective-permute-start(bf16[192,1152]{1,0:T(8,128)(2,1)S(1)} %bitcast.16), channel_id=1, source_target_pairs={{0,8},{8,0},{16,24},{24,16},{32,40},{40,32},{48,56},{56,48},{64,72... | collective-permute-start | bytes 1327112 | tf_op jit(solution)/shard_map/ppermute | solution.py:135
  78.8 10.8 %collective-permute-start.1 = (bf16[192,768]{1,0:T(8,128)(2,1)S(1)}, bf16[192,768]{1,0:T(8,128)(2,1)S(1)}, u32[]{:S(2)}, u32[]{:S(2)}) collective-permute-start(bf16[192,768]{1,0:T(8,128)(2,1)S(1)} %slice.18.refs_0_), channel_id=1, source_target_pairs={{0,16},{8,248},{16,32},{24,8},{32,48},{40,24},{48,64},{56,40},{64,... | collective-permute-start | bytes 884744 | tf_op jit(solution)/shard_map/ppermute | solution.py:145
  89.6 5.4 %collective-permute-done.1.refs_0_ = bf16[192,768]{1,0:T(8,128)(2,1)S(1)} collective-permute-done((bf16[192,768]{1,0:T(8,128)(2,1)S(1)}, bf16[192,768]{1,0:T(8,128)(2,1)S(1)}, u32[]{:S(2)}, u32[]{:S(2)}) %collective-permute-start.1) | collective-permute-done | bytes 294944 | tf_op jit(solution)/shard_map/ppermute | solution.py:145
  95.0 5.2 %collective-permute-start.2 = (bf16[192,768]{1,0:T(8,128)(2,1)S(1)}, bf16[192,768]{1,0:T(8,128)(2,1)S(1)}, u32[]{:S(2)}, u32[]{:S(2)}) collective-permute-start(bf16[192,768]{1,0:T(8,128)(2,1)S(1)} %collective-permute-done.1.refs_0_), channel_id=1, source_target_pairs={{0,16},{8,248},{16,32},{24,8},{32,48},{40,24},{48,64},{56,40},{64,... | collective-permute-start | bytes 884744 | tf_op jit(solution)/shard_map/ppermute | solution.py:145
  102.2 4.6 %collective-permute-done.2.refs_0_ = bf16[192,768]{1,0:T(8,128)(2,1)S(1)} collective-permute-done((bf16[192,768]{1,0:T(8,128)(2,1)S(1)}, bf16[192,768]{1,0:T(8,128)(2,1)S(1)}, u32[]{:S(2)}, u32[]{:S(2)}) %collective-permute-start.2) | collective-permute-done | bytes 294944 | tf_op jit(solution)/shard_map/ppermute | solution.py:145
  106.8 5.0 %collective-permute-start.3 = (bf16[192,768]{1,0:T(8,128)(2,1)S(1)}, bf16[192,768]{1,0:T(8,128)(2,1)S(1)}, u32[]{:S(2)}, u32[]{:S(2)}) collective-permute-start(bf16[192,768]{1,0:T(8,128)(2,1)S(1)} %collective-permute-done.2.refs_0_), channel_id=1, source_target_pairs={{0,16},{8,248},{16,32},{24,8},{32,48},{40,24},{48,64},{56,40},{64,... | collective-permute-start | bytes 884744 | tf_op jit(solution)/shard_map/ppermute | solution.py:145
  112.8 5.5 %collective-permute-start.10 = (bf16[192,768]{1,0:T(8,128)(2,1)S(1)}, bf16[192,768]{1,0:T(8,128)(2,1)S(1)}, u32[]{:S(2)}, u32[]{:S(2)}) collective-permute-start(bf16[192,768]{1,0:T(8,128)(2,1)S(1)} %collective-permute-done.9.refs_1_), channel_id=1, source_target_pairs={{0,16},{8,248},{16,32},{24,8},{32,48},{40,24},{48,64},{56,40},{64,... | collective-permute-start | bytes 884744 | tf_op jit(solution)/shard_map/ppermute | solution.py:147
  118.9 5.3 %collective-permute-start.4 = (bf16[192,768]{1,0:T(8,128)(2,1)S(1)}, bf16[192,768]{1,0:T(8,128)(2,1)S(1)}, u32[]{:S(2)}, u32[]{:S(2)}) collective-permute-start(bf16[192,768]{1,0:T(8,128)(2,1)S(1)} %collective-permute-done.3.refs_0_), channel_id=1, source_target_pairs={{0,16},{8,248},{16,32},{24,8},{32,48},{40,24},{48,64},{56,40},{64,... | collective-permute-start | bytes 884744 | tf_op jit(solution)/shard_map/ppermute | solution.py:145
  124.2 4.8 %collective-permute-start.11 = (bf16[192,768]{1,0:T(8,128)(2,1)S(1)}, bf16[192,768]{1,0:T(8,128)(2,1)S(1)}, u32[]{:S(2)}, u32[]{:S(2)}) collective-permute-start(bf16[192,768]{1,0:T(8,128)(2,1)S(1)} %collective-permute-done.10.refs_1_), channel_id=1, source_target_pairs={{0,16},{8,248},{16,32},{24,8},{32,48},{40,24},{48,64},{56,40},{64,... | collective-permute-start | bytes 884744 | tf_op jit(solution)/shard_map/ppermute | solution.py:147
  129.1 5.2 %collective-permute-start.5 = (bf16[192,768]{1,0:T(8,128)(2,1)S(1)}, bf16[192,768]{1,0:T(8,128)(2,1)S(1)}, u32[]{:S(2)}, u32[]{:S(2)}) collective-permute-start(bf16[192,768]{1,0:T(8,128)(2,1)S(1)} %collective-permute-done.4.refs_0_), channel_id=1, source_target_pairs={{0,16},{8,248},{16,32},{24,8},{32,48},{40,24},{48,64},{56,40},{64,... | collective-permute-start | bytes 884744 | tf_op jit(solution)/shard_map/ppermute | solution.py:145
  134.3 3.9 %collective-permute-start.12 = (bf16[192,768]{1,0:T(8,128)(2,1)S(1)}, bf16[192,768]{1,0:T(8,128)(2,1)S(1)}, u32[]{:S(2)}, u32[]{:S(2)}) collective-permute-start(bf16[192,768]{1,0:T(8,128)(2,1)S(1)} %collective-permute-done.11.refs_1_), channel_id=1, source_target_pairs={{0,16},{8,248},{16,32},{24,8},{32,48},{40,24},{48,64},{56,40},{64,... | collective-permute-start | bytes 884744 | tf_op jit(solution)/shard_map/ppermute | solution.py:147
  138.1 4.8 %collective-permute-start.6 = (bf16[192,768]{1,0:T(8,128)(2,1)S(1)}, bf16[192,768]{1,0:T(8,128)(2,1)S(1)}, u32[]{:S(2)}, u32[]{:S(2)}) collective-permute-start(bf16[192,768]{1,0:T(8,128)(2,1)S(1)} %collective-permute-done.5.refs_0_), channel_id=1, source_target_pairs={{0,16},{8,248},{16,32},{24,8},{32,48},{40,24},{48,64},{56,40},{64,... | collective-permute-start | bytes 884744 | tf_op jit(solution)/shard_map/ppermute | solution.py:145
  143.0 3.9 %collective-permute-start.13 = (bf16[192,768]{1,0:T(8,128)(2,1)S(1)}, bf16[192,768]{1,0:T(8,128)(2,1)}, u32[]{:S(2)}, u32[]{:S(2)}) collective-permute-start(bf16[192,768]{1,0:T(8,128)(2,1)S(1)} %collective-permute-done.12.refs_1_), channel_id=1, source_target_pairs={{0,16},{8,248},{16,32},{24,8},{32,48},{40,24},{48,64},{56,40},{64,... | collective-permute-start | bytes 884744 | tf_op jit(solution)/shard_map/ppermute | solution.py:147
  146.8 4.8 %collective-permute-start.7 = (bf16[192,768]{1,0:T(8,128)(2,1)S(1)}, bf16[192,768]{1,0:T(8,128)(2,1)S(1)}, u32[]{:S(2)}, u32[]{:S(2)}) collective-permute-start(bf16[192,768]{1,0:T(8,128)(2,1)S(1)} %collective-permute-done.6.refs_0_), channel_id=1, source_target_pairs={{0,16},{8,248},{16,32},{24,8},{32,48},{40,24},{48,64},{56,40},{64,... | collective-permute-start | bytes 884744 | tf_op jit(solution)/shard_map/ppermute | solution.py:145
  151.7 4.0 %collective-permute-start.14 = (bf16[192,768]{1,0:T(8,128)(2,1)}, bf16[192,768]{1,0:T(8,128)(2,1)}, u32[]{:S(2)}, u32[]{:S(2)}) collective-permute-start(bf16[192,768]{1,0:T(8,128)(2,1)} %collective-permute-done.13.refs_1_), channel_id=1, source_target_pairs={{0,16},{8,248},{16,32},{24,8},{32,48},{40,24},{48,64},{56,40},{64,... | collective-permute-start | bytes 884744 | tf_op jit(solution)/shard_map/ppermute | solution.py:147
  155.7 4.7 %collective-permute-start.8 = (bf16[192,768]{1,0:T(8,128)(2,1)S(1)}, bf16[192,768]{1,0:T(8,128)(2,1)S(1)}, u32[]{:S(2)}, u32[]{:S(2)}) collective-permute-start(bf16[192,768]{1,0:T(8,128)(2,1)S(1)} %collective-permute-done.7.refs_0_), channel_id=1, source_target_pairs={{0,16},{8,248},{16,32},{24,8},{32,48},{40,24},{48,64},{56,40},{64,... | collective-permute-start | bytes 884744 | tf_op jit(solution)/shard_map/ppermute | solution.py:145
  160.4 4.5 %collective-permute-start.15 = (bf16[192,768]{1,0:T(8,128)(2,1)}, bf16[192,768]{1,0:T(8,128)(2,1)S(1)}, u32[]{:S(2)}, u32[]{:S(2)}) collective-permute-start(bf16[192,768]{1,0:T(8,128)(2,1)} %collective-permute-done.14.refs_1_), channel_id=1, source_target_pairs={{0,16},{8,248},{16,32},{24,8},{32,48},{40,24},{48,64},{56,40},{64,... | collective-permute-start | bytes 884744 | tf_op jit(solution)/shard_map/ppermute | solution.py:147
  167.7 2.5 %shard_map.56.refs_2_ = f32[400,384]{1,0:T(8,128)S(1)} custom-call(bf16[384,384]{1,0:T(8,128)(2,1)S(1)} %maximum_multiply_fusion.q_ref, bf16[192,768]{1,0:T(8,128)(2,1)S(1)} %collective-permute-done.1.refs_0_, bf16[192,768]{1,0:T(8,128)(2,1)S(1)} %collective-permute-done.9.refs_1_, f32[400,384]{1,0:T(8,128)S(1)} %shard_map.55.refs_2_), custom_call_target="tpu_custom_call" | custom-call | flops 226492416 | bytes 589824 | tf_op jit(solution)/shard_map/pallas_call | solution.py:70
  170.1 2.5 %shard_map.57.refs_2_ = f32[400,384]{1,0:T(8,128)S(1)} custom-call(bf16[384,384]{1,0:T(8,128)(2,1)S(1)} %maximum_multiply_fusion.q_ref, bf16[192,768]{1,0:T(8,128)(2,1)S(1)} %collective-permute-done.2.refs_0_, bf16[192,768]{1,0:T(8,128)(2,1)S(1)} %collective-permute-done.10.refs_1_, f32[400,384]{1,0:T(8,128)S(1)} %shard_map.56.refs_2_), custom_call_target="tpu_custom_call" | custom-call | flops 226492416 | bytes 589824 | tf_op jit(solution)/shard_map/pallas_call | solution.py:70
  172.6 2.5 %shard_map.58.refs_2_ = f32[400,384]{1,0:T(8,128)S(1)} custom-call(bf16[384,384]{1,0:T(8,128)(2,1)S(1)} %maximum_multiply_fusion.q_ref, bf16[192,768]{1,0:T(8,128)(2,1)S(1)} %collective-permute-done.3.refs_0_, bf16[192,768]{1,0:T(8,128)(2,1)S(1)} %collective-permute-done.11.refs_1_, f32[400,384]{1,0:T(8,128)S(1)} %shard_map.57.refs_2_), custom_call_target="tpu_custom_call" | custom-call | flops 226492416 | bytes 589824 | tf_op jit(solution)/shard_map/pallas_call | solution.py:70
  175.1 2.5 %shard_map.59.refs_2_ = f32[400,384]{1,0:T(8,128)S(1)} custom-call(bf16[384,384]{1,0:T(8,128)(2,1)S(1)} %maximum_multiply_fusion.q_ref, bf16[192,768]{1,0:T(8,128)(2,1)S(1)} %collective-permute-done.4.refs_0_, bf16[192,768]{1,0:T(8,128)(2,1)S(1)} %collective-permute-done.12.refs_1_, f32[400,384]{1,0:T(8,128)S(1)} %shard_map.58.refs_2_), custom_call_target="tpu_custom_call" | custom-call | flops 226492416 | bytes 589824 | tf_op jit(solution)/shard_map/pallas_call | solution.py:70
  177.6 3.4 %shard_map.60.refs_2_ = f32[400,384]{1,0:T(8,128)S(1)} custom-call(bf16[384,384]{1,0:T(8,128)(2,1)S(1)} %maximum_multiply_fusion.q_ref, bf16[192,768]{1,0:T(8,128)(2,1)S(1)} %collective-permute-done.5.refs_0_, bf16[192,768]{1,0:T(8,128)(2,1)} %collective-permute-done.13.refs_1_, f32[400,384]{1,0:T(8,128)S(1)} %shard_map.59.refs_2_), custom_call_target="tpu_custom_call" | custom-call | flops 226492416 | bytes 589824 | tf_op jit(solution)/shard_map/pallas_call | solution.py:70
  181.1 3.7 %shard_map.61.refs_2_ = f32[400,384]{1,0:T(8,128)S(1)} custom-call(bf16[384,384]{1,0:T(8,128)(2,1)S(1)} %maximum_multiply_fusion.q_ref, bf16[192,768]{1,0:T(8,128)(2,1)S(1)} %collective-permute-done.6.refs_0_, bf16[192,768]{1,0:T(8,128)(2,1)} %collective-permute-done.14.refs_1_, f32[400,384]{1,0:T(8,128)S(1)} %shard_map.60.refs_2_), custom_call_target="tpu_custom_call" | custom-call | flops 226492416 | bytes 589824 | tf_op jit(solution)/shard_map/pallas_call | solution.py:70
  184.7 2.5 %shard_map.62.refs_1_ = f32[400,384]{1,0:T(8,128)S(1)} custom-call(bf16[384,384]{1,0:T(8,128)(2,1)S(1)} %maximum_multiply_fusion.q_ref, bf16[192,768]{1,0:T(8,128)(2,1)S(1)} %collective-permute-done.7.refs_0_, bf16[192,768]{1,0:T(8,128)(2,1)S(1)} %collective-permute-done.15.refs_1_, f32[400,384]{1,0:T(8,128)S(1)} %shard_map.61.refs_2_), custom_call_target="tpu_custom_call" | custom-call | flops 226492416 | bytes 589824 | tf_op jit(solution)/shard_map/pallas_call | solution.py:70
  189.0 5.1 %collective-permute-start.16 = (f32[400,384]{1,0:T(8,128)S(1)}, f32[400,384]{1,0:T(8,128)S(1)}, u32[]{:S(2)}, u32[]{:S(2)}) collective-permute-start(f32[400,384]{1,0:T(8,128)S(1)} %shard_map.63.one_ref), channel_id=1, source_target_pairs={{0,8},{8,0},{16,24},{24,16},{32,40},{40,32},{48,56},{56,48},{64,72... | collective-permute-start | bytes 1843208 | tf_op jit(solution)/shard_map/ppermute | solution.py:149
  195.9 5.0 %collective-permute-start.17 = (bf16[96,384]{1,0:T(8,128)(2,1)S(1)}, bf16[96,384]{1,0:T(8,128)(2,1)S(1)}, u32[]{:S(2)}, u32[]{:S(2)}) collective-permute-start(bf16[96,384]{1,0:T(8,128)(2,1)S(1)} %get-tuple-element.8), channel_id=1, source_target_pairs={{0,4},{1,5},{2,6},{3,7},{4,0},{5,1},{6,2},{7,3},{8,12},{9,13},{10,... | collective-permute-start | bytes 221192 | tf_op jit(solution)/shard_map/ppermute | solution.py:155
  200.9 4.1 %collective-permute-done.17 = bf16[96,384]{1,0:T(8,128)(2,1)S(1)} collective-permute-done((bf16[96,384]{1,0:T(8,128)(2,1)S(1)}, bf16[96,384]{1,0:T(8,128)(2,1)S(1)}, u32[]{:S(2)}, u32[]{:S(2)}) %collective-permute-start.17) | collective-permute-done | bytes 73760 | tf_op jit(solution)/shard_map/ppermute | solution.py:155
  205.1 3.9 %convolution_convert_fusion = bf16[96,3072]{1,0:T(8,128)(2,1)S(1)} fusion(bf16[768,3072]{0,1:T(8,128)(2,1)} %all-gather.2.cloned.1.call-done, bf16[96,384]{1,0:T(8,128)(2,1)S(1)} %collective-permute-done.17, bf16[96,384]{1,0:T(8,128)(2,1)S(1)} %get-tuple-element.7), kind=kOutput, calls=%fused_computation | convolution fusion | flops 453574656 | bytes 5455872 | tf_op jit(solution)/shard_map/dot_general | solution.py:157
  209.0 20.4 %all_to_all.11 = bf16[4,24,3072]{2,1,0:T(8,128)(2,1)S(1)} all-to-all(bf16[4,24,3072]{2,1,0:T(8,128)(2,1)S(1)} %bitcast.15), channel_id=1, replica_groups={{0,1,2,3},{4,5,6,7},{8,9,10,11},{12,13,14,15},{16,17,18,19},{20,21,22,2..., dimensions={0} | all-to-all | bytes 1179648 | tf_op jit(solution)/shard_map/all_to_all | solution.py:158
  (39 shorter events, 14.4 us)
Async XLA Ops:
  6.5 198.5 %all-gather.2.cloned.1.call-start = ((), (), s32[]{:S(2)}) async-start(), calls=%async_computation.2 | async-start | bytes 4866048 | tf_op jit(solution)/shard_map/all_gather | solution.py:130
  6.6 10.5 %collective-permute-start.18 = (bf16[384,96]{0,1:T(8,128)(2,1)}, bf16[384,96]{0,1:T(8,128)(2,1)S(1)}, u32[]{:S(2)}, u32[]{:S(2)}) collective-permute-start(bf16[384,96]{0,1:T(8,128)(2,1)} %param.8), channel_id=1, source_target_pairs={{0,4},{1,5},{2,6},{3,7},{4,0},{5,1},{6,2},{7,3},{8,12},{9,13},{10,... | collective-permute-start | bytes 221192 | tf_op jit(solution)/shard_map/ppermute | solution.py:128
  39.7 111.9 %copy-start = (bf16[8,24,1152]{2,1,0:T(8,128)(2,1)}, bf16[8,24,1152]{2,1,0:T(8,128)(2,1)S(1)}, u32[]{:S(2)}) copy-start(bf16[8,24,1152]{2,1,0:T(8,128)(2,1)S(1)} %all_to_all.10) | copy-start | bytes 1327108
  39.7 60.5 %collective-permute-start = (bf16[192,1152]{1,0:T(8,128)(2,1)S(1)}, bf16[192,1152]{1,0:T(8,128)(2,1)S(1)}, u32[]{:S(2)}, u32[]{:S(2)}) collective-permute-start(bf16[192,1152]{1,0:T(8,128)(2,1)S(1)} %bitcast.16), channel_id=1, source_target_pairs={{0,8},{8,0},{16,24},{24,16},{32,40},{40,32},{48,56},{56,48},{64,72... | collective-permute-start | bytes 1327112 | tf_op jit(solution)/shard_map/ppermute | solution.py:135
  78.8 16.2 %collective-permute-start.1 = (bf16[192,768]{1,0:T(8,128)(2,1)S(1)}, bf16[192,768]{1,0:T(8,128)(2,1)S(1)}, u32[]{:S(2)}, u32[]{:S(2)}) collective-permute-start(bf16[192,768]{1,0:T(8,128)(2,1)S(1)} %slice.18.refs_0_), channel_id=1, source_target_pairs={{0,16},{8,248},{16,32},{24,8},{32,48},{40,24},{48,64},{56,40},{64,... | collective-permute-start | bytes 884744 | tf_op jit(solution)/shard_map/ppermute | solution.py:145
  95.0 11.8 %collective-permute-start.2 = (bf16[192,768]{1,0:T(8,128)(2,1)S(1)}, bf16[192,768]{1,0:T(8,128)(2,1)S(1)}, u32[]{:S(2)}, u32[]{:S(2)}) collective-permute-start(bf16[192,768]{1,0:T(8,128)(2,1)S(1)} %collective-permute-done.1.refs_0_), channel_id=1, source_target_pairs={{0,16},{8,248},{16,32},{24,8},{32,48},{40,24},{48,64},{56,40},{64,... | collective-permute-start | bytes 884744 | tf_op jit(solution)/shard_map/ppermute | solution.py:145
  100.2 55.4 %copy-start.1 = (bf16[192,1152]{1,0:T(8,128)(2,1)}, bf16[192,1152]{1,0:T(8,128)(2,1)S(1)}, u32[]{:S(2)}) copy-start(bf16[192,1152]{1,0:T(8,128)(2,1)S(1)} %collective-permute-done) | copy-start | bytes 1327108
  100.3 12.5 %collective-permute-start.9 = (bf16[192,768]{1,0:T(8,128)(2,1)S(1)}, bf16[192,768]{1,0:T(8,128)(2,1)S(1)}, u32[]{:S(2)}, u32[]{:S(2)}) collective-permute-start(bf16[192,768]{1,0:T(8,128)(2,1)S(1)} %slice.19), channel_id=1, source_target_pairs={{0,16},{8,248},{16,32},{24,8},{32,48},{40,24},{48,64},{56,40},{64,... | collective-permute-start | bytes 884744 | tf_op jit(solution)/shard_map/ppermute | solution.py:147
  106.8 12.0 %collective-permute-start.3 = (bf16[192,768]{1,0:T(8,128)(2,1)S(1)}, bf16[192,768]{1,0:T(8,128)(2,1)S(1)}, u32[]{:S(2)}, u32[]{:S(2)}) collective-permute-start(bf16[192,768]{1,0:T(8,128)(2,1)S(1)} %collective-permute-done.2.refs_0_), channel_id=1, source_target_pairs={{0,16},{8,248},{16,32},{24,8},{32,48},{40,24},{48,64},{56,40},{64,... | collective-permute-start | bytes 884744 | tf_op jit(solution)/shard_map/ppermute | solution.py:145
  112.8 11.4 %collective-permute-start.10 = (bf16[192,768]{1,0:T(8,128)(2,1)S(1)}, bf16[192,768]{1,0:T(8,128)(2,1)S(1)}, u32[]{:S(2)}, u32[]{:S(2)}) collective-permute-start(bf16[192,768]{1,0:T(8,128)(2,1)S(1)} %collective-permute-done.9.refs_1_), channel_id=1, source_target_pairs={{0,16},{8,248},{16,32},{24,8},{32,48},{40,24},{48,64},{56,40},{64,... | collective-permute-start | bytes 884744 | tf_op jit(solution)/shard_map/ppermute | solution.py:147
  118.9 10.2 %collective-permute-start.4 = (bf16[192,768]{1,0:T(8,128)(2,1)S(1)}, bf16[192,768]{1,0:T(8,128)(2,1)S(1)}, u32[]{:S(2)}, u32[]{:S(2)}) collective-permute-start(bf16[192,768]{1,0:T(8,128)(2,1)S(1)} %collective-permute-done.3.refs_0_), channel_id=1, source_target_pairs={{0,16},{8,248},{16,32},{24,8},{32,48},{40,24},{48,64},{56,40},{64,... | collective-permute-start | bytes 884744 | tf_op jit(solution)/shard_map/ppermute | solution.py:145
  124.2 10.1 %collective-permute-start.11 = (bf16[192,768]{1,0:T(8,128)(2,1)S(1)}, bf16[192,768]{1,0:T(8,128)(2,1)S(1)}, u32[]{:S(2)}, u32[]{:S(2)}) collective-permute-start(bf16[192,768]{1,0:T(8,128)(2,1)S(1)} %collective-permute-done.10.refs_1_), channel_id=1, source_target_pairs={{0,16},{8,248},{16,32},{24,8},{32,48},{40,24},{48,64},{56,40},{64,... | collective-permute-start | bytes 884744 | tf_op jit(solution)/shard_map/ppermute | solution.py:147
  129.1 9.1 %collective-permute-start.5 = (bf16[192,768]{1,0:T(8,128)(2,1)S(1)}, bf16[192,768]{1,0:T(8,128)(2,1)S(1)}, u32[]{:S(2)}, u32[]{:S(2)}) collective-permute-start(bf16[192,768]{1,0:T(8,128)(2,1)S(1)} %collective-permute-done.4.refs_0_), channel_id=1, source_target_pairs={{0,16},{8,248},{16,32},{24,8},{32,48},{40,24},{48,64},{56,40},{64,... | collective-permute-start | bytes 884744 | tf_op jit(solution)/shard_map/ppermute | solution.py:145
  134.3 8.7 %collective-permute-start.12 = (bf16[192,768]{1,0:T(8,128)(2,1)S(1)}, bf16[192,768]{1,0:T(8,128)(2,1)S(1)}, u32[]{:S(2)}, u32[]{:S(2)}) collective-permute-start(bf16[192,768]{1,0:T(8,128)(2,1)S(1)} %collective-permute-done.11.refs_1_), channel_id=1, source_target_pairs={{0,16},{8,248},{16,32},{24,8},{32,48},{40,24},{48,64},{56,40},{64,... | collective-permute-start | bytes 884744 | tf_op jit(solution)/shard_map/ppermute | solution.py:147
  138.1 8.7 %collective-permute-start.6 = (bf16[192,768]{1,0:T(8,128)(2,1)S(1)}, bf16[192,768]{1,0:T(8,128)(2,1)S(1)}, u32[]{:S(2)}, u32[]{:S(2)}) collective-permute-start(bf16[192,768]{1,0:T(8,128)(2,1)S(1)} %collective-permute-done.5.refs_0_), channel_id=1, source_target_pairs={{0,16},{8,248},{16,32},{24,8},{32,48},{40,24},{48,64},{56,40},{64,... | collective-permute-start | bytes 884744 | tf_op jit(solution)/shard_map/ppermute | solution.py:145
  143.0 8.7 %collective-permute-start.13 = (bf16[192,768]{1,0:T(8,128)(2,1)S(1)}, bf16[192,768]{1,0:T(8,128)(2,1)}, u32[]{:S(2)}, u32[]{:S(2)}) collective-permute-start(bf16[192,768]{1,0:T(8,128)(2,1)S(1)} %collective-permute-done.12.refs_1_), channel_id=1, source_target_pairs={{0,16},{8,248},{16,32},{24,8},{32,48},{40,24},{48,64},{56,40},{64,... | collective-permute-start | bytes 884744 | tf_op jit(solution)/shard_map/ppermute | solution.py:147
  146.8 8.8 %collective-permute-start.7 = (bf16[192,768]{1,0:T(8,128)(2,1)S(1)}, bf16[192,768]{1,0:T(8,128)(2,1)S(1)}, u32[]{:S(2)}, u32[]{:S(2)}) collective-permute-start(bf16[192,768]{1,0:T(8,128)(2,1)S(1)} %collective-permute-done.6.refs_0_), channel_id=1, source_target_pairs={{0,16},{8,248},{16,32},{24,8},{32,48},{40,24},{48,64},{56,40},{64,... | collective-permute-start | bytes 884744 | tf_op jit(solution)/shard_map/ppermute | solution.py:145
  151.7 8.7 %collective-permute-start.14 = (bf16[192,768]{1,0:T(8,128)(2,1)}, bf16[192,768]{1,0:T(8,128)(2,1)}, u32[]{:S(2)}, u32[]{:S(2)}) collective-permute-start(bf16[192,768]{1,0:T(8,128)(2,1)} %collective-permute-done.13.refs_1_), channel_id=1, source_target_pairs={{0,16},{8,248},{16,32},{24,8},{32,48},{40,24},{48,64},{56,40},{64,... | collective-permute-start | bytes 884744 | tf_op jit(solution)/shard_map/ppermute | solution.py:147
  155.7 31.5 %collective-permute-start.8 = (bf16[192,768]{1,0:T(8,128)(2,1)S(1)}, bf16[192,768]{1,0:T(8,128)(2,1)S(1)}, u32[]{:S(2)}, u32[]{:S(2)}) collective-permute-start(bf16[192,768]{1,0:T(8,128)(2,1)S(1)} %collective-permute-done.7.refs_0_), channel_id=1, source_target_pairs={{0,16},{8,248},{16,32},{24,8},{32,48},{40,24},{48,64},{56,40},{64,... | collective-permute-start | bytes 884744 | tf_op jit(solution)/shard_map/ppermute | solution.py:145
  160.4 24.4 %collective-permute-start.15 = (bf16[192,768]{1,0:T(8,128)(2,1)}, bf16[192,768]{1,0:T(8,128)(2,1)S(1)}, u32[]{:S(2)}, u32[]{:S(2)}) collective-permute-start(bf16[192,768]{1,0:T(8,128)(2,1)} %collective-permute-done.14.refs_1_), channel_id=1, source_target_pairs={{0,16},{8,248},{16,32},{24,8},{32,48},{40,24},{48,64},{56,40},{64,... | collective-permute-start | bytes 884744 | tf_op jit(solution)/shard_map/ppermute | solution.py:147
  189.0 40.5 %copy-start.2 = (f32[3072]{0:T(1024)S(1)}, f32[3072]{0:T(1024)}, u32[]{:S(2)}) copy-start(f32[3072]{0:T(1024)} %param.9) | copy-start | bytes 36868
  189.0 6.7 %collective-permute-start.16 = (f32[400,384]{1,0:T(8,128)S(1)}, f32[400,384]{1,0:T(8,128)S(1)}, u32[]{:S(2)}, u32[]{:S(2)}) collective-permute-start(f32[400,384]{1,0:T(8,128)S(1)} %shard_map.63.one_ref), channel_id=1, source_target_pairs={{0,8},{8,0},{16,24},{24,16},{32,40},{40,32},{48,56},{56,48},{64,72... | collective-permute-start | bytes 1843208 | tf_op jit(solution)/shard_map/ppermute | solution.py:149
  195.9 9.1 %collective-permute-start.17 = (bf16[96,384]{1,0:T(8,128)(2,1)S(1)}, bf16[96,384]{1,0:T(8,128)(2,1)S(1)}, u32[]{:S(2)}, u32[]{:S(2)}) collective-permute-start(bf16[96,384]{1,0:T(8,128)(2,1)S(1)} %get-tuple-element.8), channel_id=1, source_target_pairs={{0,4},{1,5},{2,6},{3,7},{4,0},{5,1},{6,2},{7,3},{8,12},{9,13},{10,... | collective-permute-start | bytes 221192 | tf_op jit(solution)/shard_map/ppermute | solution.py:155
Sparse Core Ops, SparseCore 0:
  18.8 115.3 all-gather.1
where the time goes:
time: 238 us; the launch traced here: 237 us
  starting transfers between devices  132 us (55%)
  blocking collectives  39.5 us (17%)
  Pallas kernels  23.2 us (10%)
  waiting for transfers between devices  19.5 us (8%)
  between operations  13.8 us (6%)
  matrix products  3.89 us (2%)
  other arithmetic  3.45 us (1%)
    ppermute x8, starting transfers between devices, on_device(): a = lax.ppermute(a, 'blk', ring)  45.7 us
    ppermute x1, starting transfers between devices, on_device(): other = lax.ppermute(own, 'blk', swap)  39 us
    ppermute x7, starting transfers between devices, on_device(): b = lax.ppermute(b, 'blk', ring)  28.4 us
    pallas_call x9, Pallas kernels, fold(): pl.pallas_call(functools.partial(fold_kernel, state is None), out_shape=j...  23 us
    all_to_all x1, blocking collectives, on_device(): lax.all_to_all(partial.reshape(quad, tokens, width), 'uly', 0, 0, tiled=T...  20.4 us
    all_to_all x1, blocking collectives, on_device(): lax.all_to_all(packed, 'uly', 0, 0, tiled=True).reshape(rows, 3 * features)  19 us
    ppermute x8, waiting for transfers between devices, on_device(): a = lax.ppermute(a, 'blk', ring)  10.6 us
    ppermute x1, starting transfers between devices, on_device(): far_weight = lax.ppermute(out_weight, 'uly', across)  8.49 us
  transfers between devices with their start and end apart: 20, of which 7 were waited for; matrix products, arithmetic and copies ran while one was open for 1% of the time, Pallas kernels for 10%

commit v1 on v0

--- a/solution.py
+++ b/solution.py
@@ -81,8 +81,7 @@
     )(*operands)
 
 
-def merge_kernel(one_ref, two_ref, out_ref):
-    features = out_ref.shape[1]
+def merged(one_ref, two_ref, features):
     heads = features // HEAD
     max_rows, den_rows = (slice(features + i, features + i + heads) for i in (0, STATS))
     one_max, two_max = one_ref[max_rows, :], two_ref[max_rows, :]
@@ -94,70 +93,111 @@
     for head in range(heads):
         rows, row = slice(head * HEAD, (head + 1) * HEAD), slice(head, head + 1)
         parts.append(one_ref[rows, :] * one[row, :] + two_ref[rows, :] * two[row, :])
-    out_ref[...] = jnp.concatenate(parts, axis=0).astype(out_ref.dtype).T
-
-
-def merge(one, two, features):
+    return jnp.concatenate(parts, axis=0).astype(jnp.bfloat16).T
+
+
+def project_kernel(
+    depth, place_ref, one_ref, two_ref, self_ref, mine_ref, theirs_ref, out_ref, attended, weight
+):
+    z, core = place_ref[0], place_ref[1]
+    rows, width = out_ref.shape
+    features = attended.shape[1]
+    pair = self_ref.shape[0]
+    cols = pair // 2
+    last = depth // 2
+
+    def put(chip, offset, block):
+        at = pl.multiple_of(lax.rem(chip, depth) * pair + offset, 16)
+        weight[pl.ds(at, block.shape[0]), :] = block
+
+    put(z, 0, self_ref[...])
+    for step in range(1, last):
+        block = slice((step - 1) * pair, step * pair)
+        ahead, behind = z + step, z + depth - step
+        put(jnp.where(core == 0, ahead, behind), 0, mine_ref[block, :])
+        put(jnp.where(core == 0, behind, ahead), 0, theirs_ref[block, :])
+    block = slice((last - 1) * pair, (last - 1) * pair + cols)
+    put(z + last, core * cols, mine_ref[block, :])
+    put(z + last, (1 - core) * cols, theirs_ref[block, :])
+
+    attended[...] = merged(one_ref, two_ref, features)
+    mine = attended[pl.ds(pl.multiple_of(core * rows, 16), rows), :]
+    chunk = width // 4
+    for i in range(4):
+        part = slice(i * chunk, (i + 1) * chunk)
+        out_ref[:, part] = nt_dot(mine, weight[part, :]).astype(out_ref.dtype)
+
+
+def project(depth, place, one, two, weights):
+    row_count = one.shape[1]
+    features = weights[0].shape[1]
+    width = weights[0].shape[0] * depth
     vmem = pl.BlockSpec(memory_space=pltpu.VMEM)
     return pl.pallas_call(
-        merge_kernel,
-        out_shape=jax.ShapeDtypeStruct((one.shape[1], features), jnp.bfloat16),
-        in_specs=[vmem] * 2,
+        functools.partial(project_kernel, depth),
+        out_shape=jax.ShapeDtypeStruct((row_count // 2, width), jnp.bfloat16),
+        in_specs=[pl.BlockSpec(memory_space=pltpu.SMEM)] + [vmem] * 5,
         out_specs=vmem,
+        scratch_shapes=[
+            pltpu.VMEM((row_count, features), jnp.bfloat16),
+            pltpu.VMEM((width, features), jnp.bfloat16),
+        ],
         compiler_params=pltpu.CompilerParams(vmem_limit_bytes=VMEM_LIMIT),
-    )(one, two)
+    )(place, one, two, *weights)
 
 
 def on_device(query, keys, values, out_weight, out_gain):
     tokens, width = query.shape
     blk, uly = lax.axis_size("blk"), lax.axis_size("uly")
-    depth, quad = blk // 2, uly // 2
+    depth = blk // 2
+    last = depth // 2
     features = width // uly
     rows = tokens * uly
-    core = lax.axis_index("blk") % 2
-    side = lax.axis_index("uly") // quad
+    z, core = lax.axis_index("blk") // 2, lax.axis_index("blk") % 2
     swap = [(i, i ^ 1) for i in range(blk)]
-    ring = [
-        (2 * z + c, 2 * ((z + (1 if c == 0 else -1)) % depth) + c)
-        for z in range(depth)
-        for c in range(2)
-    ]
-    across = [(i, (i + quad) % uly) for i in range(uly)]
-    quads = [[h * quad + i for i in range(quad)] for h in range(2)]
-
-    far_weight = lax.ppermute(out_weight, "uly", across)
-    both = jnp.concatenate([out_weight, far_weight], axis=0)
-    weight = lax.all_gather(both, "blk", axis=1, tiled=True)
+    ring, against = (
+        [
+            (2 * z + c, 2 * ((z + (way if c == 0 else -way)) % depth) + c)
+            for z in range(depth)
+            for c in range(2)
+        ]
+        for way in (1, -1)
+    )
+
+    def by_core(own, other):
+        return jnp.concatenate(
+            [jnp.where(core == 0, own, other), jnp.where(core == 0, other, own)], axis=0
+        )
+
+    columns = out_weight.T
+    w_self = by_core(columns, lax.ppermute(columns, "blk", swap))
 
     cut = [a.reshape(tokens, uly, features) for a in (query, keys, values)]
     packed = jnp.concatenate(cut, axis=2).transpose(1, 0, 2)
     own = lax.all_to_all(packed, "uly", 0, 0, tiled=True).reshape(rows, 3 * features)
     other = lax.ppermute(own, "blk", swap)
-    q_own, q_other = own[:, :features], other[:, :features]
-    q_all = jnp.concatenate(
-        [jnp.where(core == 0, q_own, q_other), jnp.where(core == 0, q_other, q_own)], axis=0
-    ) * jnp.bfloat16(1.0 / math.sqrt(HEAD))
-
-    a, b = own[:, features:], other[:, features:]
+    q_all = by_core(own[:, :features], other[:, :features])
+    q_all = q_all * jnp.bfloat16(1.0 / math.sqrt(HEAD))
+
+    a, b, w = own[:, features:], other[:, features:], w_self
+    w_blocks = []
     state = fold(q_all, (a,), None)
-    last = depth // 2
     for step in range(1, last + 1):
         a = lax.ppermute(a, "blk", ring)
         if step < last:
             b = lax.ppermute(b, "blk", ring)
+        else:
+            half = w.shape[0] // 2
+            w = lax.dynamic_slice_in_dim(w, core * half, half, axis=0)
+        w = lax.ppermute(w, "blk", against)
+        w_blocks.append(w)
         state = fold(q_all, (a, b) if step < last else (a,), state)
+    w_mine = jnp.concatenate(w_blocks, axis=0)
+    w_theirs = lax.ppermute(w_mine, "blk", swap)
     theirs = lax.ppermute(state, "blk", swap)
-    attended = merge(state, theirs, features)
-
-    half = quad * tokens
-    near = lax.dynamic_slice_in_dim(attended, core * rows + side * half, half, axis=0)
-    far = lax.dynamic_slice_in_dim(attended, core * rows + (1 - side) * half, half, axis=0)
-    far = lax.ppermute(far, "uly", across)
-    joined = jnp.concatenate([near, far], axis=1)
-    partial = jnp.dot(joined, weight, preferred_element_type=jnp.float32).astype(jnp.bfloat16)
-    blocks = lax.all_to_all(
-        partial.reshape(quad, tokens, width), "uly", 0, 0, tiled=True, axis_index_groups=quads
-    )
+    place = jnp.stack([z, core]).astype(jnp.int32)
+    partial = project(depth, place, state, theirs, (w_self, w_mine, w_theirs))
+    blocks = lax.all_to_all(partial.reshape(uly, tokens, width), "uly", 0, 0, tiled=True)
     summed = jnp.sum(blocks.astype(jnp.float32), axis=0)
     return (out_gain * summed).astype(jnp.bfloat16)
 

time: 238 us -> 236 us (level)
  blocking collectives: 39.5 us -> 53.4 us
  between operations: 13.8 us -> 0.68 us
  local copies, waits for them, and re-layouts: 2.03 us -> 6.66 us
  matrix products: 3.89 us -> 0 us
  starting transfers between devices: 132 us -> 129 us
    ppermute x2 -> x10, starting transfers between devices: 13.5 us -> 29.4 us  [the longest x8 21.5 us: on_device(): w = lax.ppermute(w, 'blk', against)]
    all_to_all x1, blocking collectives: 20.4 us -> 34.4 us  [on_device(): lax.all_to_all(partial.reshape(uly, tokens, width), 'uly', 0, 0, tiled=True)]
    ppermute x7, starting transfers between devices: 28.4 us -> 16.5 us  [on_device(): b = lax.ppermute(b, 'blk', ring)]
    ppermute x2 -> x10, waiting for transfers between devices: 6.19 us -> 15.8 us  [the longest x8 15.8 us: on_device(): w = lax.ppermute(w, 'blk', against)]
    ppermute x8, waiting for transfers between devices: 10.6 us -> 1.68 us  [on_device(): a = lax.ppermute(a, 'blk', ring)]
    unnamed x6 -> x35, local copies, waits for them, and re-layouts: 0.01 us -> 4.65 us
    dot_general x1 -> x0, matrix products: 3.89 us -> none  [on_device(): jnp.dot(joined, weight, preferred_element_type=jnp.float32)]
    ppermute x8, starting transfers between devices: 45.7 us -> 42.2 us  [on_device(): a = lax.ppermute(a, 'blk', ring)]
  transfers between devices with their start and end apart: 20 -> 27, of which waited for: 7 -> 7; matrix products, arithmetic and copies ran while one was open for 1% -> 1% of each run, Pallas kernels for 10% -> 9%
where the time goes in v1:
time: 236 us; the launch traced here: 235 us
  starting transfers between devices  129 us (55%)
  blocking collectives  53.4 us (23%)
  Pallas kernels  23 us (10%)
  waiting for transfers between devices  19.5 us (8%)
  local copies, waits for them, and re-layouts  6.66 us (3%)
    ppermute x8, starting transfers between devices, on_device(): a = lax.ppermute(a, 'blk', ring)  42.2 us
    ppermute x1, starting transfers between devices, on_device(): other = lax.ppermute(own, 'blk', swap)  39.3 us
    all_to_all x1, blocking collectives, on_device(): lax.all_to_all(partial.reshape(uly, tokens, width), 'uly', 0, 0, tiled=True)  34.4 us
    ppermute x8, starting transfers between devices, on_device(): w = lax.ppermute(w, 'blk', against)  21.5 us
    pallas_call x9, Pallas kernels, fold(): pl.pallas_call(functools.partial(fold_kernel, state is None), out_shape=j...  21.2 us
    all_to_all x1, blocking collectives, on_device(): lax.all_to_all(packed, 'uly', 0, 0, tiled=True).reshape(rows, 3 * features)  18.9 us
    ppermute x7, starting transfers between devices, on_device(): b = lax.ppermute(b, 'blk', ring)  16.5 us
    ppermute x8, waiting for transfers between devices, on_device(): w = lax.ppermute(w, 'blk', against)  15.8 us
  transfers between devices with their start and end apart: 27, of which 7 were waited for; matrix products, arithmetic and copies ran while one was open for 1% of the time, Pallas kernels for 9%

profile of v1, /device:TPU:65, one launch (start us, length us, event | category | flops | bytes accessed | tf_op | source)
XLA Modules:
  0.0 234.5 jit_solution(6346788236278034952)
XLA Ops:
  2.0 18.9 %all_to_all.10 = bf16[8,24,1152]{2,1,0:T(8,128)(2,1)S(1)} all-to-all(bf16[8,24,1152]{2,1,0:T(8,128)(2,1)S(1)} %maximum_bitcast_fusion), channel_id=1, replica_groups=mesh['group'=2,'blk'=32,'uly'=8] {'uly'}, dimensions={0} | all-to-all | bytes 884736 | tf_op jit(solution)/shard_map/all_to_all | solution.py:177
  20.9 39.3 %collective-permute-start = (bf16[192,1152]{1,0:T(8,128)(2,1)S(1)}, bf16[192,1152]{1,0:T(8,128)(2,1)S(1)}, u32[]{:S(2)}, u32[]{:S(2)}) collective-permute-start(bf16[192,1152]{1,0:T(8,128)(2,1)S(1)} %bitcast.20), channel_id=1, source_target_pairs={{0,8},{8,0},{16,24},{24,16},{32,40},{40,32},{48,56},{56,48},{64,72... | collective-permute-start | bytes 1327112 | tf_op jit(solution)/shard_map/ppermute | solution.py:178
  60.2 11.8 %collective-permute-start.1 = (bf16[192,768]{1,0:T(8,128)(2,1)S(1)}, bf16[192,768]{1,0:T(8,128)(2,1)S(1)}, u32[]{:S(2)}, u32[]{:S(2)}) collective-permute-start(bf16[192,768]{1,0:T(8,128)(2,1)S(1)} %slice.18.refs_0_), channel_id=1, source_target_pairs={{0,16},{8,248},{16,32},{24,8},{32,48},{40,24},{48,64},{56,40},{64,... | collective-permute-start | bytes 884744 | tf_op jit(solution)/shard_map/ppermute | solution.py:186
  75.7 5.0 %collective-permute-start.2 = (bf16[192,768]{1,0:T(8,128)(2,1)S(1)}, bf16[192,768]{1,0:T(8,128)(2,1)S(1)}, u32[]{:S(2)}, u32[]{:S(2)}) collective-permute-start(bf16[192,768]{1,0:T(8,128)(2,1)S(1)} %collective-permute-done.1.refs_0_), channel_id=1, source_target_pairs={{0,16},{8,248},{16,32},{24,8},{32,48},{40,24},{48,64},{56,40},{64,... | collective-permute-start | bytes 884744 | tf_op jit(solution)/shard_map/ppermute | solution.py:186
  82.8 3.4 %collective-permute-start.18 = (bf16[192,384]{1,0:T(8,128)(2,1)S(1)}, bf16[192,384]{1,0:T(8,128)(2,1)S(1)}, u32[]{:S(2)}, u32[]{:S(2)}) collective-permute-start(bf16[192,384]{1,0:T(8,128)(2,1)S(1)} %pad_maximum_fusion.self_ref), channel_id=1, source_target_pairs={{0,240},{8,24},{16,0},{24,40},{32,16},{40,56},{48,32},{56,72},{64,... | collective-permute-start | bytes 442376 | tf_op jit(solution)/shard_map/ppermute | solution.py:192
  86.9 3.2 %collective-permute-start.3 = (bf16[192,768]{1,0:T(8,128)(2,1)S(1)}, bf16[192,768]{1,0:T(8,128)(2,1)S(1)}, u32[]{:S(2)}, u32[]{:S(2)}) collective-permute-start(bf16[192,768]{1,0:T(8,128)(2,1)S(1)} %collective-permute-done.2.refs_0_), channel_id=1, source_target_pairs={{0,16},{8,248},{16,32},{24,8},{32,48},{40,24},{48,64},{56,40},{64,... | collective-permute-start | bytes 884744 | tf_op jit(solution)/shard_map/ppermute | solution.py:186
  90.2 3.4 %collective-permute-start.10 = (bf16[192,768]{1,0:T(8,128)(2,1)S(1)}, bf16[192,768]{1,0:T(8,128)(2,1)S(1)}, u32[]{:S(2)}, u32[]{:S(2)}) collective-permute-start(bf16[192,768]{1,0:T(8,128)(2,1)S(1)} %collective-permute-done.9.refs_1_), channel_id=1, source_target_pairs={{0,16},{8,248},{16,32},{24,8},{32,48},{40,24},{48,64},{56,40},{64,... | collective-permute-start | bytes 884744 | tf_op jit(solution)/shard_map/ppermute | solution.py:188
  93.6 2.0 collective-permute-start.19
  95.6 6.2 %collective-permute-done.19 = bf16[192,384]{1,0:T(8,128)(2,1)S(1)} collective-permute-done((bf16[192,384]{1,0:T(8,128)(2,1)S(1)}, bf16[192,384]{1,0:T(8,128)(2,1)S(1)}, u32[]{:S(2)}, u32[]{:S(2)}) %collective-permute-start.19) | collective-permute-done | bytes 147488 | tf_op jit(solution)/shard_map/ppermute | solution.py:192
  103.7 4.6 %collective-permute-start.4 = (bf16[192,768]{1,0:T(8,128)(2,1)S(1)}, bf16[192,768]{1,0:T(8,128)(2,1)S(1)}, u32[]{:S(2)}, u32[]{:S(2)}) collective-permute-start(bf16[192,768]{1,0:T(8,128)(2,1)S(1)} %collective-permute-done.3.refs_0_), channel_id=1, source_target_pairs={{0,16},{8,248},{16,32},{24,8},{32,48},{40,24},{48,64},{56,40},{64,... | collective-permute-start | bytes 884744 | tf_op jit(solution)/shard_map/ppermute | solution.py:186
  111.7 3.4 %collective-permute-start.21 = (bf16[192,384]{1,0:T(8,128)(2,1)S(1)}, bf16[192,384]{1,0:T(8,128)(2,1)}, u32[]{:S(2)}, u32[]{:S(2)}) collective-permute-start(bf16[192,384]{1,0:T(8,128)(2,1)S(1)} %collective-permute-done.20), channel_id=1, source_target_pairs={{0,240},{8,24},{16,0},{24,40},{32,16},{40,56},{48,32},{56,72},{64,... | collective-permute-start | bytes 442376 | tf_op jit(solution)/shard_map/ppermute | solution.py:192
  115.1 5.4 %collective-permute-done.21 = bf16[192,384]{1,0:T(8,128)(2,1)} collective-permute-done((bf16[192,384]{1,0:T(8,128)(2,1)S(1)}, bf16[192,384]{1,0:T(8,128)(2,1)}, u32[]{:S(2)}, u32[]{:S(2)}) %collective-permute-start.21) | collective-permute-done | bytes 147488 | tf_op jit(solution)/shard_map/ppermute | solution.py:192
  122.5 4.6 %collective-permute-start.5 = (bf16[192,768]{1,0:T(8,128)(2,1)S(1)}, bf16[192,768]{1,0:T(8,128)(2,1)S(1)}, u32[]{:S(2)}, u32[]{:S(2)}) collective-permute-start(bf16[192,768]{1,0:T(8,128)(2,1)S(1)} %collective-permute-done.4.refs_0_), channel_id=1, source_target_pairs={{0,16},{8,248},{16,32},{24,8},{32,48},{40,24},{48,64},{56,40},{64,... | collective-permute-start | bytes 884744 | tf_op jit(solution)/shard_map/ppermute | solution.py:186
  129.2 3.4 %collective-permute-start.23 = (bf16[192,384]{1,0:T(8,128)(2,1)S(1)}, bf16[192,384]{1,0:T(8,128)(2,1)S(1)}, u32[]{:S(2)}, u32[]{:S(2)}) collective-permute-start(bf16[192,384]{1,0:T(8,128)(2,1)S(1)} %collective-permute-done.22), channel_id=1, source_target_pairs={{0,240},{8,24},{16,0},{24,40},{32,16},{40,56},{48,32},{56,72},{64,... | collective-permute-start | bytes 442376 | tf_op jit(solution)/shard_map/ppermute | solution.py:192
  132.6 3.3 %collective-permute-start.6 = (bf16[192,768]{1,0:T(8,128)(2,1)S(1)}, bf16[192,768]{1,0:T(8,128)(2,1)S(1)}, u32[]{:S(2)}, u32[]{:S(2)}) collective-permute-start(bf16[192,768]{1,0:T(8,128)(2,1)S(1)} %collective-permute-done.5.refs_0_), channel_id=1, source_target_pairs={{0,16},{8,248},{16,32},{24,8},{32,48},{40,24},{48,64},{56,40},{64,... | collective-permute-start | bytes 884744 | tf_op jit(solution)/shard_map/ppermute | solution.py:186
  136.0 3.1 %collective-permute-start.13 = (bf16[192,768]{1,0:T(8,128)(2,1)S(1)}, bf16[192,768]{1,0:T(8,128)(2,1)S(1)}, u32[]{:S(2)}, u32[]{:S(2)}) collective-permute-start(bf16[192,768]{1,0:T(8,128)(2,1)S(1)} %collective-permute-done.12.refs_1_), channel_id=1, source_target_pairs={{0,16},{8,248},{16,32},{24,8},{32,48},{40,24},{48,64},{56,40},{64,... | collective-permute-start | bytes 884744 | tf_op jit(solution)/shard_map/ppermute | solution.py:188
  140.1 2.2 collective-permute-start.24
  142.4 4.4 %collective-permute-start.7 = (bf16[192,768]{1,0:T(8,128)(2,1)S(1)}, bf16[192,768]{1,0:T(8,128)(2,1)S(1)}, u32[]{:S(2)}, u32[]{:S(2)}) collective-permute-start(bf16[192,768]{1,0:T(8,128)(2,1)S(1)} %collective-permute-done.6.refs_0_), channel_id=1, source_target_pairs={{0,16},{8,248},{16,32},{24,8},{32,48},{40,24},{48,64},{56,40},{64,... | collective-permute-start | bytes 884744 | tf_op jit(solution)/shard_map/ppermute | solution.py:186
  146.8 2.0 collective-permute-start.14
  148.8 3.3 %collective-permute-start.25 = (bf16[96,384]{1,0:T(8,128)(2,1)S(1)}, bf16[96,384]{1,0:T(8,128)(2,1)S(1)}, u32[]{:S(2)}, u32[]{:S(2)}) collective-permute-start(bf16[96,384]{1,0:T(8,128)(2,1)S(1)} %constant_dynamic-slice_fusion), channel_id=1, source_target_pairs={{0,240},{8,24},{16,0},{24,40},{32,16},{40,56},{48,32},{56,72},{64,... | collective-permute-start | bytes 221192 | tf_op jit(solution)/shard_map/ppermute | solution.py:192
  152.2 4.0 %collective-permute-done.25 = bf16[96,384]{1,0:T(8,128)(2,1)S(1)} collective-permute-done((bf16[96,384]{1,0:T(8,128)(2,1)S(1)}, bf16[96,384]{1,0:T(8,128)(2,1)S(1)}, u32[]{:S(2)}, u32[]{:S(2)}) %collective-permute-start.25) | collective-permute-done | bytes 73760 | tf_op jit(solution)/shard_map/ppermute | solution.py:192
  156.3 5.9 %collective-permute-start.26 = (bf16[1440,384]{1,0:T(8,128)(2,1)S(1)}, bf16[1440,384]{1,0:T(8,128)(2,1)S(1)}, u32[]{:S(2)}, u32[]{:S(2)}) collective-permute-start(bf16[1440,384]{1,0:T(8,128)(2,1)S(1)} %constant_dynamic-update-slice_fusion.mine_ref), channel_id=1, source_target_pairs={{0,8},{8,0},{16,24},{24,16},{32,40},{40,32},{48,56},{56,48},{64,72... | collective-permute-start | bytes 3317768 | tf_op jit(solution)/shard_map/ppermute | solution.py:196
  162.2 5.2 %collective-permute-start.8 = (bf16[192,768]{1,0:T(8,128)(2,1)S(1)}, bf16[192,768]{1,0:T(8,128)(2,1)S(1)}, u32[]{:S(2)}, u32[]{:S(2)}) collective-permute-start(bf16[192,768]{1,0:T(8,128)(2,1)S(1)} %collective-permute-done.7.refs_0_), channel_id=1, source_target_pairs={{0,16},{8,248},{16,32},{24,8},{32,48},{40,24},{48,64},{56,40},{64,... | collective-permute-start | bytes 884744 | tf_op jit(solution)/shard_map/ppermute | solution.py:186
  167.4 2.1 collective-permute-start.15
  172.4 2.5 %shard_map.56.refs_2_ = f32[400,384]{1,0:T(8,128)S(1)} custom-call(bf16[384,384]{1,0:T(8,128)(2,1)S(1)} %maximum_multiply_fusion.q_ref, bf16[192,768]{1,0:T(8,128)(2,1)S(1)} %collective-permute-done.1.refs_0_, bf16[192,768]{1,0:T(8,128)(2,1)S(1)} %collective-permute-done.9.refs_1_, f32[400,384]{1,0:T(8,128)S(1)} %shard_map.55.refs_2_), custom_call_target="tpu_custom_call" | custom-call | flops 226492416 | bytes 589824 | tf_op jit(solution)/shard_map/pallas_call | solution.py:70
  174.9 2.5 %shard_map.57.refs_2_ = f32[400,384]{1,0:T(8,128)S(1)} custom-call(bf16[384,384]{1,0:T(8,128)(2,1)S(1)} %maximum_multiply_fusion.q_ref, bf16[192,768]{1,0:T(8,128)(2,1)S(1)} %collective-permute-done.2.refs_0_, bf16[192,768]{1,0:T(8,128)(2,1)S(1)} %copy-done.5, f32[400,384]{1,0:T(8,128)S(1)} %shard_map.56.refs_2_), custom_call_target="tpu_custom_call" | custom-call | flops 226492416 | bytes 589824 | tf_op jit(solution)/shard_map/pallas_call | solution.py:70
  177.5 2.5 %shard_map.58.refs_2_ = f32[400,384]{1,0:T(8,128)S(1)} custom-call(bf16[384,384]{1,0:T(8,128)(2,1)S(1)} %maximum_multiply_fusion.q_ref, bf16[192,768]{1,0:T(8,128)(2,1)S(1)} %copy-done.3, bf16[192,768]{1,0:T(8,128)(2,1)S(1)} %copy-done.9, f32[400,384]{1,0:T(8,128)S(1)} %shard_map.57.refs_2_), custom_call_target="tpu_custom_call" | custom-call | flops 226492416 | bytes 589824 | tf_op jit(solution)/shard_map/pallas_call | solution.py:70
  180.0 2.5 %shard_map.59.refs_2_ = f32[400,384]{1,0:T(8,128)S(1)} custom-call(bf16[384,384]{1,0:T(8,128)(2,1)S(1)} %maximum_multiply_fusion.q_ref, bf16[192,768]{1,0:T(8,128)(2,1)S(1)} %copy-done.7, bf16[192,768]{1,0:T(8,128)(2,1)S(1)} %collective-permute-done.12.refs_1_, f32[400,384]{1,0:T(8,128)S(1)} %shard_map.58.refs_2_), custom_call_target="tpu_custom_call" | custom-call | flops 226492416 | bytes 589824 | tf_op jit(solution)/shard_map/pallas_call | solution.py:70
  182.5 2.5 %shard_map.60.refs_2_ = f32[400,384]{1,0:T(8,128)S(1)} custom-call(bf16[384,384]{1,0:T(8,128)(2,1)S(1)} %maximum_multiply_fusion.q_ref, bf16[192,768]{1,0:T(8,128)(2,1)S(1)} %collective-permute-done.5.refs_0_, bf16[192,768]{1,0:T(8,128)(2,1)S(1)} %collective-permute-done.13.refs_1_, f32[400,384]{1,0:T(8,128)S(1)} %shard_map.59.refs_2_), custom_call_target="tpu_custom_call" | custom-call | flops 226492416 | bytes 589824 | tf_op jit(solution)/shard_map/pallas_call | solution.py:70
  185.0 2.7 %shard_map.61.refs_2_ = f32[400,384]{1,0:T(8,128)S(1)} custom-call(bf16[384,384]{1,0:T(8,128)(2,1)S(1)} %maximum_multiply_fusion.q_ref, bf16[192,768]{1,0:T(8,128)(2,1)S(1)} %collective-permute-done.6.refs_0_, bf16[192,768]{1,0:T(8,128)(2,1)S(1)} %collective-permute-done.14.refs_1_, f32[400,384]{1,0:T(8,128)S(1)} %shard_map.60.refs_2_), custom_call_target="tpu_custom_call" | custom-call | flops 226492416 | bytes 589824 | tf_op jit(solution)/shard_map/pallas_call | solution.py:70
  187.7 2.5 %shard_map.62.refs_1_ = f32[400,384]{1,0:T(8,128)S(1)} custom-call(bf16[384,384]{1,0:T(8,128)(2,1)S(1)} %maximum_multiply_fusion.q_ref, bf16[192,768]{1,0:T(8,128)(2,1)S(1)} %collective-permute-done.7.refs_0_, bf16[192,768]{1,0:T(8,128)(2,1)S(1)} %collective-permute-done.15.refs_1_, f32[400,384]{1,0:T(8,128)S(1)} %shard_map.61.refs_2_), custom_call_target="tpu_custom_call" | custom-call | flops 226492416 | bytes 589824 | tf_op jit(solution)/shard_map/pallas_call | solution.py:70
  198.7 34.4 %all_to_all.11 = bf16[8,24,3072]{2,1,0:T(8,128)(2,1)S(1)} all-to-all(bf16[8,24,3072]{2,1,0:T(8,128)(2,1)S(1)} %bitcast.19), channel_id=1, replica_groups=mesh['group'=2,'blk'=32,'uly'=8] {'uly'}, dimensions={0} | all-to-all | bytes 2359296 | tf_op jit(solution)/shard_map/all_to_all | solution.py:200
  (83 shorter events, 31.5 us)
Async XLA Ops:
  1.9 70.1 %copy-start.12 = (bf16[384,96]{0,1:T(8,128)(2,1)S(1)}, bf16[384,96]{0,1:T(8,128)(2,1)}, u32[]{:S(2)}) copy-start(bf16[384,96]{0,1:T(8,128)(2,1)} %param.8) | copy-start | bytes 221188
  20.9 65.3 %copy-start.10 = (bf16[8,24,1152]{2,1,0:T(8,128)(2,1)}, bf16[8,24,1152]{2,1,0:T(8,128)(2,1)S(1)}, u32[]{:S(2)}) copy-start(bf16[8,24,1152]{2,1,0:T(8,128)(2,1)S(1)} %all_to_all.10) | copy-start | bytes 1327108
  20.9 59.8 %collective-permute-start = (bf16[192,1152]{1,0:T(8,128)(2,1)S(1)}, bf16[192,1152]{1,0:T(8,128)(2,1)S(1)}, u32[]{:S(2)}, u32[]{:S(2)}) collective-permute-start(bf16[192,1152]{1,0:T(8,128)(2,1)S(1)} %bitcast.20), channel_id=1, source_target_pairs={{0,8},{8,0},{16,24},{24,16},{32,40},{40,32},{48,56},{56,48},{64,72... | collective-permute-start | bytes 1327112 | tf_op jit(solution)/shard_map/ppermute | solution.py:178
  60.2 15.5 %collective-permute-start.1 = (bf16[192,768]{1,0:T(8,128)(2,1)S(1)}, bf16[192,768]{1,0:T(8,128)(2,1)S(1)}, u32[]{:S(2)}, u32[]{:S(2)}) collective-permute-start(bf16[192,768]{1,0:T(8,128)(2,1)S(1)} %slice.18.refs_0_), channel_id=1, source_target_pairs={{0,16},{8,248},{16,32},{24,8},{32,48},{40,24},{48,64},{56,40},{64,... | collective-permute-start | bytes 884744 | tf_op jit(solution)/shard_map/ppermute | solution.py:186
  72.1 10.7 %collective-permute-start.17 = (bf16[96,384]{1,0:T(8,128)(2,1)S(1)}, bf16[96,384]{1,0:T(8,128)(2,1)S(1)}, u32[]{:S(2)}, u32[]{:S(2)}) collective-permute-start(bf16[96,384]{1,0:T(8,128)(2,1)S(1)} %bitcast.27), channel_id=1, source_target_pairs={{0,8},{8,0},{16,24},{24,16},{32,40},{40,32},{48,56},{56,48},{64,72... | collective-permute-start | bytes 221192 | tf_op jit(solution)/shard_map/ppermute | solution.py:173
  75.7 11.2 %collective-permute-start.2 = (bf16[192,768]{1,0:T(8,128)(2,1)S(1)}, bf16[192,768]{1,0:T(8,128)(2,1)S(1)}, u32[]{:S(2)}, u32[]{:S(2)}) collective-permute-start(bf16[192,768]{1,0:T(8,128)(2,1)S(1)} %collective-permute-done.1.refs_0_), channel_id=1, source_target_pairs={{0,16},{8,248},{16,32},{24,8},{32,48},{40,24},{48,64},{56,40},{64,... | collective-permute-start | bytes 884744 | tf_op jit(solution)/shard_map/ppermute | solution.py:186
  80.8 9.3 %copy-start.11 = (bf16[192,1152]{1,0:T(8,128)(2,1)}, bf16[192,1152]{1,0:T(8,128)(2,1)S(1)}, u32[]{:S(2)}) copy-start(bf16[192,1152]{1,0:T(8,128)(2,1)S(1)} %collective-permute-done) | copy-start | bytes 1327108
  80.8 9.4 %collective-permute-start.9 = (bf16[192,768]{1,0:T(8,128)(2,1)S(1)}, bf16[192,768]{1,0:T(8,128)(2,1)S(1)}, u32[]{:S(2)}, u32[]{:S(2)}) collective-permute-start(bf16[192,768]{1,0:T(8,128)(2,1)S(1)} %slice.19), channel_id=1, source_target_pairs={{0,16},{8,248},{16,32},{24,8},{32,48},{40,24},{48,64},{56,40},{64,... | collective-permute-start | bytes 884744 | tf_op jit(solution)/shard_map/ppermute | solution.py:188
  82.8 10.7 %collective-permute-start.18 = (bf16[192,384]{1,0:T(8,128)(2,1)S(1)}, bf16[192,384]{1,0:T(8,128)(2,1)S(1)}, u32[]{:S(2)}, u32[]{:S(2)}) collective-permute-start(bf16[192,384]{1,0:T(8,128)(2,1)S(1)} %pad_maximum_fusion.self_ref), channel_id=1, source_target_pairs={{0,240},{8,24},{16,0},{24,40},{32,16},{40,56},{48,32},{56,72},{64,... | collective-permute-start | bytes 442376 | tf_op jit(solution)/shard_map/ppermute | solution.py:192
  86.9 16.8 %collective-permute-start.3 = (bf16[192,768]{1,0:T(8,128)(2,1)S(1)}, bf16[192,768]{1,0:T(8,128)(2,1)S(1)}, u32[]{:S(2)}, u32[]{:S(2)}) collective-permute-start(bf16[192,768]{1,0:T(8,128)(2,1)S(1)} %collective-permute-done.2.refs_0_), channel_id=1, source_target_pairs={{0,16},{8,248},{16,32},{24,8},{32,48},{40,24},{48,64},{56,40},{64,... | collective-permute-start | bytes 884744 | tf_op jit(solution)/shard_map/ppermute | solution.py:186
  90.2 18.9 %collective-permute-start.10 = (bf16[192,768]{1,0:T(8,128)(2,1)S(1)}, bf16[192,768]{1,0:T(8,128)(2,1)S(1)}, u32[]{:S(2)}, u32[]{:S(2)}) collective-permute-start(bf16[192,768]{1,0:T(8,128)(2,1)S(1)} %collective-permute-done.9.refs_1_), channel_id=1, source_target_pairs={{0,16},{8,248},{16,32},{24,8},{32,48},{40,24},{48,64},{56,40},{64,... | collective-permute-start | bytes 884744 | tf_op jit(solution)/shard_map/ppermute | solution.py:188
  93.6 8.2 %collective-permute-start.19 = (bf16[192,384]{1,0:T(8,128)(2,1)S(1)}, bf16[192,384]{1,0:T(8,128)(2,1)S(1)}, u32[]{:S(2)}, u32[]{:S(2)}) collective-permute-start(bf16[192,384]{1,0:T(8,128)(2,1)S(1)} %collective-permute-done.18), channel_id=1, source_target_pairs={{0,240},{8,24},{16,0},{24,40},{32,16},{40,56},{48,32},{56,72},{64,... | collective-permute-start | bytes 442376 | tf_op jit(solution)/shard_map/ppermute | solution.py:192
  101.8 10.0 %collective-permute-start.20 = (bf16[192,384]{1,0:T(8,128)(2,1)S(1)}, bf16[192,384]{1,0:T(8,128)(2,1)S(1)}, u32[]{:S(2)}, u32[]{:S(2)}) collective-permute-start(bf16[192,384]{1,0:T(8,128)(2,1)S(1)} %collective-permute-done.19), channel_id=1, source_target_pairs={{0,240},{8,24},{16,0},{24,40},{32,16},{40,56},{48,32},{56,72},{64,... | collective-permute-start | bytes 442376 | tf_op jit(solution)/shard_map/ppermute | solution.py:192
  103.7 18.8 %collective-permute-start.4 = (bf16[192,768]{1,0:T(8,128)(2,1)S(1)}, bf16[192,768]{1,0:T(8,128)(2,1)S(1)}, u32[]{:S(2)}, u32[]{:S(2)}) collective-permute-start(bf16[192,768]{1,0:T(8,128)(2,1)S(1)} %collective-permute-done.3.refs_0_), channel_id=1, source_target_pairs={{0,16},{8,248},{16,32},{24,8},{32,48},{40,24},{48,64},{56,40},{64,... | collective-permute-start | bytes 884744 | tf_op jit(solution)/shard_map/ppermute | solution.py:186
  109.1 18.1 %collective-permute-start.11 = (bf16[192,768]{1,0:T(8,128)(2,1)S(1)}, bf16[192,768]{1,0:T(8,128)(2,1)S(1)}, u32[]{:S(2)}, u32[]{:S(2)}) collective-permute-start(bf16[192,768]{1,0:T(8,128)(2,1)S(1)} %collective-permute-done.10.refs_1_), channel_id=1, source_target_pairs={{0,16},{8,248},{16,32},{24,8},{32,48},{40,24},{48,64},{56,40},{64,... | collective-permute-start | bytes 884744 | tf_op jit(solution)/shard_map/ppermute | solution.py:188
  111.7 8.8 %collective-permute-start.21 = (bf16[192,384]{1,0:T(8,128)(2,1)S(1)}, bf16[192,384]{1,0:T(8,128)(2,1)}, u32[]{:S(2)}, u32[]{:S(2)}) collective-permute-start(bf16[192,384]{1,0:T(8,128)(2,1)S(1)} %collective-permute-done.20), channel_id=1, source_target_pairs={{0,240},{8,24},{16,0},{24,40},{32,16},{40,56},{48,32},{56,72},{64,... | collective-permute-start | bytes 442376 | tf_op jit(solution)/shard_map/ppermute | solution.py:192
  120.6 8.6 %collective-permute-start.22 = (bf16[192,384]{1,0:T(8,128)(2,1)}, bf16[192,384]{1,0:T(8,128)(2,1)S(1)}, u32[]{:S(2)}, u32[]{:S(2)}) collective-permute-start(bf16[192,384]{1,0:T(8,128)(2,1)} %collective-permute-done.21), channel_id=1, source_target_pairs={{0,240},{8,24},{16,0},{24,40},{32,16},{40,56},{48,32},{56,72},{64,... | collective-permute-start | bytes 442376 | tf_op jit(solution)/shard_map/ppermute | solution.py:192
  122.5 29.7 %copy-start.6 = (bf16[192,768]{1,0:T(8,128)(2,1)}, bf16[192,768]{1,0:T(8,128)(2,1)S(1)}, u32[]{:S(2)}) copy-start(bf16[192,768]{1,0:T(8,128)(2,1)S(1)} %collective-permute-done.4.refs_0_) | copy-start | bytes 884740
  122.5 10.1 %collective-permute-start.5 = (bf16[192,768]{1,0:T(8,128)(2,1)S(1)}, bf16[192,768]{1,0:T(8,128)(2,1)S(1)}, u32[]{:S(2)}, u32[]{:S(2)}) collective-permute-start(bf16[192,768]{1,0:T(8,128)(2,1)S(1)} %collective-permute-done.4.refs_0_), channel_id=1, source_target_pairs={{0,16},{8,248},{16,32},{24,8},{32,48},{40,24},{48,64},{56,40},{64,... | collective-permute-start | bytes 884744 | tf_op jit(solution)/shard_map/ppermute | solution.py:186
  127.2 25.0 %copy-start.8 = (bf16[192,768]{1,0:T(8,128)(2,1)}, bf16[192,768]{1,0:T(8,128)(2,1)S(1)}, u32[]{:S(2)}) copy-start(bf16[192,768]{1,0:T(8,128)(2,1)S(1)} %collective-permute-done.11.refs_1_) | copy-start | bytes 884740
  127.2 8.8 %collective-permute-start.12 = (bf16[192,768]{1,0:T(8,128)(2,1)S(1)}, bf16[192,768]{1,0:T(8,128)(2,1)S(1)}, u32[]{:S(2)}, u32[]{:S(2)}) collective-permute-start(bf16[192,768]{1,0:T(8,128)(2,1)S(1)} %collective-permute-done.11.refs_1_), channel_id=1, source_target_pairs={{0,16},{8,248},{16,32},{24,8},{32,48},{40,24},{48,64},{56,40},{64,... | collective-permute-start | bytes 884744 | tf_op jit(solution)/shard_map/ppermute | solution.py:188
  129.2 10.9 %collective-permute-start.23 = (bf16[192,384]{1,0:T(8,128)(2,1)S(1)}, bf16[192,384]{1,0:T(8,128)(2,1)S(1)}, u32[]{:S(2)}, u32[]{:S(2)}) collective-permute-start(bf16[192,384]{1,0:T(8,128)(2,1)S(1)} %collective-permute-done.22), channel_id=1, source_target_pairs={{0,240},{8,24},{16,0},{24,40},{32,16},{40,56},{48,32},{56,72},{64,... | collective-permute-start | bytes 442376 | tf_op jit(solution)/shard_map/ppermute | solution.py:192
  132.6 9.7 %collective-permute-start.6 = (bf16[192,768]{1,0:T(8,128)(2,1)S(1)}, bf16[192,768]{1,0:T(8,128)(2,1)S(1)}, u32[]{:S(2)}, u32[]{:S(2)}) collective-permute-start(bf16[192,768]{1,0:T(8,128)(2,1)S(1)} %collective-permute-done.5.refs_0_), channel_id=1, source_target_pairs={{0,16},{8,248},{16,32},{24,8},{32,48},{40,24},{48,64},{56,40},{64,... | collective-permute-start | bytes 884744 | tf_op jit(solution)/shard_map/ppermute | solution.py:186
  136.0 10.7 %collective-permute-start.13 = (bf16[192,768]{1,0:T(8,128)(2,1)S(1)}, bf16[192,768]{1,0:T(8,128)(2,1)S(1)}, u32[]{:S(2)}, u32[]{:S(2)}) collective-permute-start(bf16[192,768]{1,0:T(8,128)(2,1)S(1)} %collective-permute-done.12.refs_1_), channel_id=1, source_target_pairs={{0,16},{8,248},{16,32},{24,8},{32,48},{40,24},{48,64},{56,40},{64,... | collective-permute-start | bytes 884744 | tf_op jit(solution)/shard_map/ppermute | solution.py:188
  140.1 8.7 %collective-permute-start.24 = (bf16[192,384]{1,0:T(8,128)(2,1)S(1)}, bf16[192,384]{1,0:T(8,128)(2,1)S(1)}, u32[]{:S(2)}, u32[]{:S(2)}) collective-permute-start(bf16[192,384]{1,0:T(8,128)(2,1)S(1)} %collective-permute-done.23), channel_id=1, source_target_pairs={{0,240},{8,24},{16,0},{24,40},{32,16},{40,56},{48,32},{56,72},{64,... | collective-permute-start | bytes 442376 | tf_op jit(solution)/shard_map/ppermute | solution.py:192
  142.4 19.8 %collective-permute-start.7 = (bf16[192,768]{1,0:T(8,128)(2,1)S(1)}, bf16[192,768]{1,0:T(8,128)(2,1)S(1)}, u32[]{:S(2)}, u32[]{:S(2)}) collective-permute-start(bf16[192,768]{1,0:T(8,128)(2,1)S(1)} %collective-permute-done.6.refs_0_), channel_id=1, source_target_pairs={{0,16},{8,248},{16,32},{24,8},{32,48},{40,24},{48,64},{56,40},{64,... | collective-permute-start | bytes 884744 | tf_op jit(solution)/shard_map/ppermute | solution.py:186
  146.8 20.7 %collective-permute-start.14 = (bf16[192,768]{1,0:T(8,128)(2,1)S(1)}, bf16[192,768]{1,0:T(8,128)(2,1)S(1)}, u32[]{:S(2)}, u32[]{:S(2)}) collective-permute-start(bf16[192,768]{1,0:T(8,128)(2,1)S(1)} %collective-permute-done.13.refs_1_), channel_id=1, source_target_pairs={{0,16},{8,248},{16,32},{24,8},{32,48},{40,24},{48,64},{56,40},{64,... | collective-permute-start | bytes 884744 | tf_op jit(solution)/shard_map/ppermute | solution.py:188
  148.8 7.4 %collective-permute-start.25 = (bf16[96,384]{1,0:T(8,128)(2,1)S(1)}, bf16[96,384]{1,0:T(8,128)(2,1)S(1)}, u32[]{:S(2)}, u32[]{:S(2)}) collective-permute-start(bf16[96,384]{1,0:T(8,128)(2,1)S(1)} %constant_dynamic-slice_fusion), channel_id=1, source_target_pairs={{0,240},{8,24},{16,0},{24,40},{32,16},{40,56},{48,32},{56,72},{64,... | collective-permute-start | bytes 221192 | tf_op jit(solution)/shard_map/ppermute | solution.py:192
  156.3 37.8 %collective-permute-start.26 = (bf16[1440,384]{1,0:T(8,128)(2,1)S(1)}, bf16[1440,384]{1,0:T(8,128)(2,1)S(1)}, u32[]{:S(2)}, u32[]{:S(2)}) collective-permute-start(bf16[1440,384]{1,0:T(8,128)(2,1)S(1)} %constant_dynamic-update-slice_fusion.mine_ref), channel_id=1, source_target_pairs={{0,8},{8,0},{16,24},{24,16},{32,40},{40,32},{48,56},{56,48},{64,72... | collective-permute-start | bytes 3317768 | tf_op jit(solution)/shard_map/ppermute | solution.py:196
  162.2 28.0 %collective-permute-start.8 = (bf16[192,768]{1,0:T(8,128)(2,1)S(1)}, bf16[192,768]{1,0:T(8,128)(2,1)S(1)}, u32[]{:S(2)}, u32[]{:S(2)}) collective-permute-start(bf16[192,768]{1,0:T(8,128)(2,1)S(1)} %collective-permute-done.7.refs_0_), channel_id=1, source_target_pairs={{0,16},{8,248},{16,32},{24,8},{32,48},{40,24},{48,64},{56,40},{64,... | collective-permute-start | bytes 884744 | tf_op jit(solution)/shard_map/ppermute | solution.py:186
  167.4 20.3 %collective-permute-start.15 = (bf16[192,768]{1,0:T(8,128)(2,1)S(1)}, bf16[192,768]{1,0:T(8,128)(2,1)S(1)}, u32[]{:S(2)}, u32[]{:S(2)}) collective-permute-start(bf16[192,768]{1,0:T(8,128)(2,1)S(1)} %collective-permute-done.14.refs_1_), channel_id=1, source_target_pairs={{0,16},{8,248},{16,32},{24,8},{32,48},{40,24},{48,64},{56,40},{64,... | collective-permute-start | bytes 884744 | tf_op jit(solution)/shard_map/ppermute | solution.py:188
  192.0 4.0 %collective-permute-start.16 = (f32[400,384]{1,0:T(8,128)S(1)}, f32[400,384]{1,0:T(8,128)S(1)}, u32[]{:S(2)}, u32[]{:S(2)}) collective-permute-start(f32[400,384]{1,0:T(8,128)S(1)} %shard_map.63.one_ref), channel_id=1, source_target_pairs={{0,8},{8,0},{16,24},{24,16},{32,40},{40,32},{48,56},{56,48},{64,72... | collective-permute-start | bytes 1843208 | tf_op jit(solution)/shard_map/ppermute | solution.py:197
  (9 other events, 13.8 us)

commit v2 on v1

--- a/solution.py
+++ b/solution.py
@@ -97,28 +97,25 @@
 
 
 def project_kernel(
-    depth, place_ref, one_ref, two_ref, self_ref, mine_ref, theirs_ref, out_ref, attended, weight
+    depth, place_ref, one_ref, two_ref, self_ref, mine_ref, theirs_ref, far_ref, out_ref, attended, weight
 ):
     z, core = place_ref[0], place_ref[1]
     rows, width = out_ref.shape
     features = attended.shape[1]
     pair = self_ref.shape[0]
-    cols = pair // 2
     last = depth // 2
 
-    def put(chip, offset, block):
-        at = pl.multiple_of(lax.rem(chip, depth) * pair + offset, 16)
-        weight[pl.ds(at, block.shape[0]), :] = block
-
-    put(z, 0, self_ref[...])
+    def put(chip, block):
+        at = pl.multiple_of(lax.rem(chip, depth) * pair, 16)
+        weight[pl.ds(at, pair), :] = block
+
+    put(z, self_ref[...])
+    put(z + last, far_ref[...])
     for step in range(1, last):
         block = slice((step - 1) * pair, step * pair)
         ahead, behind = z + step, z + depth - step
-        put(jnp.where(core == 0, ahead, behind), 0, mine_ref[block, :])
-        put(jnp.where(core == 0, behind, ahead), 0, theirs_ref[block, :])
-    block = slice((last - 1) * pair, (last - 1) * pair + cols)
-    put(z + last, core * cols, mine_ref[block, :])
-    put(z + last, (1 - core) * cols, theirs_ref[block, :])
+        put(jnp.where(core == 0, ahead, behind), mine_ref[block, :])
+        put(jnp.where(core == 0, behind, ahead), theirs_ref[block, :])
 
     attended[...] = merged(one_ref, two_ref, features)
     mine = attended[pl.ds(pl.multiple_of(core * rows, 16), rows), :]
@@ -136,7 +133,7 @@
     return pl.pallas_call(
         functools.partial(project_kernel, depth),
         out_shape=jax.ShapeDtypeStruct((row_count // 2, width), jnp.bfloat16),
-        in_specs=[pl.BlockSpec(memory_space=pltpu.SMEM)] + [vmem] * 5,
+        in_specs=[pl.BlockSpec(memory_space=pltpu.SMEM)] + [vmem] * 6,
         out_specs=vmem,
         scratch_shapes=[
             pltpu.VMEM((row_count, features), jnp.bfloat16),
@@ -144,6 +141,14 @@
         ],
         compiler_params=pltpu.CompilerParams(vmem_limit_bytes=VMEM_LIMIT),
     )(place, one, two, *weights)
+
+
+def weight_hops(depth):
+    held, hops, last = 1, [], depth // 2
+    while held <= last:
+        hops.append(min(held, 3, last + 1 - held))
+        held += hops[-1]
+    return hops
 
 
 def on_device(query, keys, values, out_weight, out_gain):
@@ -155,14 +160,15 @@
     rows = tokens * uly
     z, core = lax.axis_index("blk") // 2, lax.axis_index("blk") % 2
     swap = [(i, i ^ 1) for i in range(blk)]
-    ring, against = (
-        [
-            (2 * z + c, 2 * ((z + (way if c == 0 else -way)) % depth) + c)
+
+    def round_z(hop):
+        return [
+            (2 * z + c, 2 * ((z + (hop if c == 0 else -hop)) % depth) + c)
             for z in range(depth)
             for c in range(2)
         ]
-        for way in (1, -1)
-    )
+
+    ring = round_z(1)
 
     def by_core(own, other):
         return jnp.concatenate(
@@ -179,24 +185,26 @@
     q_all = by_core(own[:, :features], other[:, :features])
     q_all = q_all * jnp.bfloat16(1.0 / math.sqrt(HEAD))
 
-    a, b, w = own[:, features:], other[:, features:], w_self
-    w_blocks = []
+    pair = w_self.shape[0]
+    held, w_parts = 1, [w_self]
+    for hop in weight_hops(depth):
+        send = jnp.concatenate(w_parts, axis=0)[(held - hop) * pair :]
+        w_parts.append(lax.ppermute(send, "blk", round_z(-hop)))
+        held += hop
+    w_got = jnp.concatenate(w_parts[1:], axis=0)
+    w_mine, w_far = w_got[:-pair], w_got[-pair:]
+    w_theirs = lax.ppermute(w_mine, "blk", swap)
+
+    a, b = own[:, features:], other[:, features:]
     state = fold(q_all, (a,), None)
     for step in range(1, last + 1):
         a = lax.ppermute(a, "blk", ring)
         if step < last:
             b = lax.ppermute(b, "blk", ring)
-        else:
-            half = w.shape[0] // 2
-            w = lax.dynamic_slice_in_dim(w, core * half, half, axis=0)
-        w = lax.ppermute(w, "blk", against)
-        w_blocks.append(w)
         state = fold(q_all, (a, b) if step < last else (a,), state)
-    w_mine = jnp.concatenate(w_blocks, axis=0)
-    w_theirs = lax.ppermute(w_mine, "blk", swap)
     theirs = lax.ppermute(state, "blk", swap)
     place = jnp.stack([z, core]).astype(jnp.int32)
-    partial = project(depth, place, state, theirs, (w_self, w_mine, w_theirs))
+    partial = project(depth, place, state, theirs, (w_self, w_mine, w_theirs, w_far))
     blocks = lax.all_to_all(partial.reshape(uly, tokens, width), "uly", 0, 0, tiled=True)
     summed = jnp.sum(blocks.astype(jnp.float32), axis=0)
     return (out_gain * summed).astype(jnp.bfloat16)

time: 236 us -> 228 us (0.966)
  starting transfers between devices: 129 us -> 118 us
  waiting for transfers between devices: 19.5 us -> 25.6 us
  local copies, waits for them, and re-layouts: 6.66 us -> 3.5 us
    ppermute x8 -> x4, starting transfers between devices: 21.5 us -> 11.3 us  [on_device(): w_parts.append(lax.ppermute(send, 'blk', round_z(-hop)))]
    ppermute x8, waiting for transfers between devices: 1.68 us -> 10.4 us  [on_device(): a = lax.ppermute(a, 'blk', ring)]
    ppermute x8 -> x4, waiting for transfers between devices: 15.8 us -> 9.8 us  [on_device(): w_parts.append(lax.ppermute(send, 'blk', round_z(-hop)))]
    ppermute x7, starting transfers between devices: 16.5 us -> 21.9 us  [on_device(): b = lax.ppermute(b, 'blk', ring)]
    ppermute x7, waiting for transfers between devices: 0.12 us -> 4.42 us  [on_device(): b = lax.ppermute(b, 'blk', ring)]
    unnamed x35 -> x8, local copies, waits for them, and re-layouts: 4.65 us -> 0.57 us
    ppermute x8, starting transfers between devices: 42.2 us -> 38.9 us  [on_device(): a = lax.ppermute(a, 'blk', ring)]
    ppermute x1, starting transfers between devices: 5.89 us -> 2.92 us  [on_device(): w_theirs = lax.ppermute(w_mine, 'blk', swap)]
  transfers between devices with their start and end apart: 27 -> 23, of which waited for: 7 -> 7; matrix products, arithmetic and copies ran while one was open for 1% -> 1% of each run, Pallas kernels for 9% -> 9%
where the time goes in v2:
time: 228 us; the launch traced here: 227 us
  starting transfers between devices  118 us (52%)
  blocking collectives  53.4 us (23%)
  waiting for transfers between devices  25.6 us (11%)
  Pallas kernels  23 us (10%)
  local copies, waits for them, and re-layouts  3.5 us (2%)
  other arithmetic  3.16 us (1%)
    ppermute x1, starting transfers between devices, on_device(): other = lax.ppermute(own, 'blk', swap)  39.3 us
    ppermute x8, starting transfers between devices, on_device(): a = lax.ppermute(a, 'blk', ring)  38.9 us
    all_to_all x1, blocking collectives, on_device(): lax.all_to_all(partial.reshape(uly, tokens, width), 'uly', 0, 0, tiled=True)  34.4 us
    ppermute x7, starting transfers between devices, on_device(): b = lax.ppermute(b, 'blk', ring)  21.9 us
    pallas_call x9, Pallas kernels, fold(): pl.pallas_call(functools.partial(fold_kernel, state is None), out_shape=j...  21.2 us
    all_to_all x1, blocking collectives, on_device(): lax.all_to_all(packed, 'uly', 0, 0, tiled=True).reshape(rows, 3 * features)  18.9 us
    ppermute x4, starting transfers between devices, on_device(): w_parts.append(lax.ppermute(send, 'blk', round_z(-hop)))  11.3 us
    ppermute x8, waiting for transfers between devices, on_device(): a = lax.ppermute(a, 'blk', ring)  10.4 us
  transfers between devices with their start and end apart: 23, of which 7 were waited for; matrix products, arithmetic and copies ran while one was open for 1% of the time, Pallas kernels for 9%

profile of v2, /device:TPU:65, one launch (start us, length us, event | category | flops | bytes accessed | tf_op | source)
XLA Modules:
  0.0 227.3 jit_solution(16944735178541411285)
XLA Ops:
  2.0 18.9 %all_to_all.10 = bf16[8,24,1152]{2,1,0:T(8,128)(2,1)S(1)} all-to-all(bf16[8,24,1152]{2,1,0:T(8,128)(2,1)S(1)} %maximum_bitcast_fusion), channel_id=1, replica_groups=mesh['group'=2,'blk'=32,'uly'=8] {'uly'}, dimensions={0} | all-to-all | bytes 884736 | tf_op jit(solution)/shard_map/all_to_all | solution.py:183
  20.9 39.3 %collective-permute-start = (bf16[192,1152]{1,0:T(8,128)(2,1)S(1)}, bf16[192,1152]{1,0:T(8,128)(2,1)S(1)}, u32[]{:S(2)}, u32[]{:S(2)}) collective-permute-start(bf16[192,1152]{1,0:T(8,128)(2,1)S(1)} %bitcast.20), channel_id=1, source_target_pairs={{0,8},{8,0},{16,24},{24,16},{32,40},{40,32},{48,56},{56,48},{64,72... | collective-permute-start | bytes 1327112 | tf_op jit(solution)/shard_map/ppermute | solution.py:184
  60.2 11.8 %collective-permute-start.1 = (bf16[192,768]{1,0:T(8,128)(2,1)S(1)}, bf16[192,768]{1,0:T(8,128)(2,1)S(1)}, u32[]{:S(2)}, u32[]{:S(2)}) collective-permute-start(bf16[192,768]{1,0:T(8,128)(2,1)S(1)} %slice.30.refs_0_), channel_id=1, source_target_pairs={{0,16},{8,248},{16,32},{24,8},{32,48},{40,24},{48,64},{56,40},{64,... | collective-permute-start | bytes 884744 | tf_op jit(solution)/shard_map/ppermute | solution.py:201
  75.7 5.0 %collective-permute-start.2 = (bf16[192,768]{1,0:T(8,128)(2,1)S(1)}, bf16[192,768]{1,0:T(8,128)(2,1)S(1)}, u32[]{:S(2)}, u32[]{:S(2)}) collective-permute-start(bf16[192,768]{1,0:T(8,128)(2,1)S(1)} %collective-permute-done.1.refs_0_), channel_id=1, source_target_pairs={{0,16},{8,248},{16,32},{24,8},{32,48},{40,24},{48,64},{56,40},{64,... | collective-permute-start | bytes 884744 | tf_op jit(solution)/shard_map/ppermute | solution.py:201
  82.9 3.4 %collective-permute-start.18 = (bf16[192,384]{1,0:T(8,128)(2,1)S(1)}, bf16[192,384]{1,0:T(8,128)(2,1)S(1)}, u32[]{:S(2)}, u32[]{:S(2)}) collective-permute-start(bf16[192,384]{1,0:T(8,128)(2,1)S(1)} %pad_maximum_fusion.5.self_ref), channel_id=1, source_target_pairs={{0,240},{8,24},{16,0},{24,40},{32,16},{40,56},{48,32},{56,72},{64,... | collective-permute-start | bytes 442376 | tf_op jit(solution)/shard_map/ppermute | solution.py:192
  86.3 3.2 %collective-permute-start.3 = (bf16[192,768]{1,0:T(8,128)(2,1)S(1)}, bf16[192,768]{1,0:T(8,128)(2,1)S(1)}, u32[]{:S(2)}, u32[]{:S(2)}) collective-permute-start(bf16[192,768]{1,0:T(8,128)(2,1)S(1)} %collective-permute-done.2.refs_0_), channel_id=1, source_target_pairs={{0,16},{8,248},{16,32},{24,8},{32,48},{40,24},{48,64},{56,40},{64,... | collective-permute-start | bytes 884744 | tf_op jit(solution)/shard_map/ppermute | solution.py:201
  90.2 3.4 %collective-permute-start.10 = (bf16[192,768]{1,0:T(8,128)(2,1)S(1)}, bf16[192,768]{1,0:T(8,128)(2,1)S(1)}, u32[]{:S(2)}, u32[]{:S(2)}) collective-permute-start(bf16[192,768]{1,0:T(8,128)(2,1)S(1)} %collective-permute-done.9.refs_1_), channel_id=1, source_target_pairs={{0,16},{8,248},{16,32},{24,8},{32,48},{40,24},{48,64},{56,40},{64,... | collective-permute-start | bytes 884744 | tf_op jit(solution)/shard_map/ppermute | solution.py:203
  93.6 2.0 collective-permute-start.19
  95.6 4.3 %collective-permute-start.4 = (bf16[192,768]{1,0:T(8,128)(2,1)S(1)}, bf16[192,768]{1,0:T(8,128)(2,1)S(1)}, u32[]{:S(2)}, u32[]{:S(2)}) collective-permute-start(bf16[192,768]{1,0:T(8,128)(2,1)S(1)} %collective-permute-done.3.refs_0_), channel_id=1, source_target_pairs={{0,16},{8,248},{16,32},{24,8},{32,48},{40,24},{48,64},{56,40},{64,... | collective-permute-start | bytes 884744 | tf_op jit(solution)/shard_map/ppermute | solution.py:201
  100.0 3.4 %collective-permute-start.11 = (bf16[192,768]{1,0:T(8,128)(2,1)S(1)}, bf16[192,768]{1,0:T(8,128)(2,1)S(1)}, u32[]{:S(2)}, u32[]{:S(2)}) collective-permute-start(bf16[192,768]{1,0:T(8,128)(2,1)S(1)} %collective-permute-done.10.refs_1_), channel_id=1, source_target_pairs={{0,16},{8,248},{16,32},{24,8},{32,48},{40,24},{48,64},{56,40},{64,... | collective-permute-start | bytes 884744 | tf_op jit(solution)/shard_map/ppermute | solution.py:203
  103.4 4.7 %collective-permute-done.19 = bf16[384,384]{1,0:T(8,128)(2,1)S(1)} collective-permute-done((bf16[384,384]{1,0:T(8,128)(2,1)S(1)}, bf16[384,384]{1,0:T(8,128)(2,1)S(1)}, u32[]{:S(2)}, u32[]{:S(2)}) %collective-permute-start.19) | collective-permute-done | bytes 294944 | tf_op jit(solution)/shard_map/ppermute | solution.py:192
  110.1 2.8 %collective-permute-start.5 = (bf16[192,768]{1,0:T(8,128)(2,1)S(1)}, bf16[192,768]{1,0:T(8,128)(2,1)S(1)}, u32[]{:S(2)}, u32[]{:S(2)}) collective-permute-start(bf16[192,768]{1,0:T(8,128)(2,1)S(1)} %collective-permute-done.4.refs_0_), channel_id=1, source_target_pairs={{0,16},{8,248},{16,32},{24,8},{32,48},{40,24},{48,64},{56,40},{64,... | collective-permute-start | bytes 884744 | tf_op jit(solution)/shard_map/ppermute | solution.py:201
  112.9 5.1 %collective-permute-start.12 = (bf16[192,768]{1,0:T(8,128)(2,1)S(1)}, bf16[192,768]{1,0:T(8,128)(2,1)S(1)}, u32[]{:S(2)}, u32[]{:S(2)}) collective-permute-start(bf16[192,768]{1,0:T(8,128)(2,1)S(1)} %collective-permute-done.11.refs_1_), channel_id=1, source_target_pairs={{0,16},{8,248},{16,32},{24,8},{32,48},{40,24},{48,64},{56,40},{64,... | collective-permute-start | bytes 884744 | tf_op jit(solution)/shard_map/ppermute | solution.py:203
  118.0 8.7 %collective-permute-done.5.refs_0_ = bf16[192,768]{1,0:T(8,128)(2,1)S(1)} collective-permute-done((bf16[192,768]{1,0:T(8,128)(2,1)S(1)}, bf16[192,768]{1,0:T(8,128)(2,1)S(1)}, u32[]{:S(2)}, u32[]{:S(2)}) %collective-permute-start.5) | collective-permute-done | bytes 294944 | tf_op jit(solution)/shard_map/ppermute | solution.py:201
  126.7 3.4 %collective-permute-start.6 = (bf16[192,768]{1,0:T(8,128)(2,1)S(1)}, bf16[192,768]{1,0:T(8,128)(2,1)S(1)}, u32[]{:S(2)}, u32[]{:S(2)}) collective-permute-start(bf16[192,768]{1,0:T(8,128)(2,1)S(1)} %collective-permute-done.5.refs_0_), channel_id=1, source_target_pairs={{0,16},{8,248},{16,32},{24,8},{32,48},{40,24},{48,64},{56,40},{64,... | collective-permute-start | bytes 884744 | tf_op jit(solution)/shard_map/ppermute | solution.py:201
  130.2 3.7 %collective-permute-done.12.refs_1_ = bf16[192,768]{1,0:T(8,128)(2,1)S(1)} collective-permute-done((bf16[192,768]{1,0:T(8,128)(2,1)S(1)}, bf16[192,768]{1,0:T(8,128)(2,1)S(1)}, u32[]{:S(2)}, u32[]{:S(2)}) %collective-permute-start.12) | collective-permute-done | bytes 294944 | tf_op jit(solution)/shard_map/ppermute | solution.py:203
  133.8 2.4 %collective-permute-start.13 = (bf16[192,768]{1,0:T(8,128)(2,1)S(1)}, bf16[192,768]{1,0:T(8,128)(2,1)S(1)}, u32[]{:S(2)}, u32[]{:S(2)}) collective-permute-start(bf16[192,768]{1,0:T(8,128)(2,1)S(1)} %collective-permute-done.12.refs_1_), channel_id=1, source_target_pairs={{0,16},{8,248},{16,32},{24,8},{32,48},{40,24},{48,64},{56,40},{64,... | collective-permute-start | bytes 884744 | tf_op jit(solution)/shard_map/ppermute | solution.py:203
  136.2 4.0 %collective-permute-start.21 = (bf16[384,384]{1,0:T(8,128)(2,1)S(1)}, bf16[384,384]{1,0:T(8,128)(2,1)}, u32[]{:S(2)}, u32[]{:S(2)}) collective-permute-start(bf16[384,384]{1,0:T(8,128)(2,1)S(1)} %slice.32), channel_id=1, source_target_pairs={{0,224},{8,40},{16,240},{24,56},{32,0},{40,72},{48,16},{56,88},{64... | collective-permute-start | bytes 884744 | tf_op jit(solution)/shard_map/ppermute | solution.py:192
  140.3 3.3 %collective-permute-start.7 = (bf16[192,768]{1,0:T(8,128)(2,1)S(1)}, bf16[192,768]{1,0:T(8,128)(2,1)S(1)}, u32[]{:S(2)}, u32[]{:S(2)}) collective-permute-start(bf16[192,768]{1,0:T(8,128)(2,1)S(1)} %collective-permute-done.6.refs_0_), channel_id=1, source_target_pairs={{0,16},{8,248},{16,32},{24,8},{32,48},{40,24},{48,64},{56,40},{64,... | collective-permute-start | bytes 884744 | tf_op jit(solution)/shard_map/ppermute | solution.py:201
  143.6 2.4 %collective-permute-start.14 = (bf16[192,768]{1,0:T(8,128)(2,1)S(1)}, bf16[192,768]{1,0:T(8,128)(2,1)S(1)}, u32[]{:S(2)}, u32[]{:S(2)}) collective-permute-start(bf16[192,768]{1,0:T(8,128)(2,1)S(1)} %collective-permute-done.13.refs_1_), channel_id=1, source_target_pairs={{0,16},{8,248},{16,32},{24,8},{32,48},{40,24},{48,64},{56,40},{64,... | collective-permute-start | bytes 884744 | tf_op jit(solution)/shard_map/ppermute | solution.py:203
  146.0 5.1 %collective-permute-done.21 = bf16[384,384]{1,0:T(8,128)(2,1)} collective-permute-done((bf16[384,384]{1,0:T(8,128)(2,1)S(1)}, bf16[384,384]{1,0:T(8,128)(2,1)}, u32[]{:S(2)}, u32[]{:S(2)}) %collective-permute-start.21) | collective-permute-done | bytes 294944 | tf_op jit(solution)/shard_map/ppermute | solution.py:192
  152.1 2.9 %collective-permute-start.22 = (bf16[1344,384]{1,0:T(8,128)(2,1)S(1)}, bf16[1344,384]{1,0:T(8,128)(2,1)S(1)}, u32[]{:S(2)}, u32[]{:S(2)}) collective-permute-start(bf16[1344,384]{1,0:T(8,128)(2,1)S(1)} %pad_maximum_fusion.mine_ref), channel_id=1, source_target_pairs={{0,8},{8,0},{16,24},{24,16},{32,40},{40,32},{48,56},{56,48},{64,72... | collective-permute-start | bytes 3096584 | tf_op jit(solution)/shard_map/ppermute | solution.py:196
  155.0 4.9 %collective-permute-start.8 = (bf16[192,768]{1,0:T(8,128)(2,1)S(1)}, bf16[192,768]{1,0:T(8,128)(2,1)S(1)}, u32[]{:S(2)}, u32[]{:S(2)}) collective-permute-start(bf16[192,768]{1,0:T(8,128)(2,1)S(1)} %collective-permute-done.7.refs_0_), channel_id=1, source_target_pairs={{0,16},{8,248},{16,32},{24,8},{32,48},{40,24},{48,64},{56,40},{64,... | collective-permute-start | bytes 884744 | tf_op jit(solution)/shard_map/ppermute | solution.py:201
  160.0 3.4 %collective-permute-start.15 = (bf16[192,768]{1,0:T(8,128)(2,1)S(1)}, bf16[192,768]{1,0:T(8,128)(2,1)S(1)}, u32[]{:S(2)}, u32[]{:S(2)}) collective-permute-start(bf16[192,768]{1,0:T(8,128)(2,1)S(1)} %collective-permute-done.14.refs_1_), channel_id=1, source_target_pairs={{0,16},{8,248},{16,32},{24,8},{32,48},{40,24},{48,64},{56,40},{64,... | collective-permute-start | bytes 884744 | tf_op jit(solution)/shard_map/ppermute | solution.py:203
  166.2 2.5 %shard_map.56.refs_2_ = f32[400,384]{1,0:T(8,128)S(1)} custom-call(bf16[384,384]{1,0:T(8,128)(2,1)S(1)} %maximum_multiply_fusion.q_ref, bf16[192,768]{1,0:T(8,128)(2,1)S(1)} %collective-permute-done.1.refs_0_, bf16[192,768]{1,0:T(8,128)(2,1)S(1)} %collective-permute-done.9.refs_1_, f32[400,384]{1,0:T(8,128)S(1)} %shard_map.55.refs_2_), custom_call_target="tpu_custom_call" | custom-call | flops 226492416 | bytes 589824 | tf_op jit(solution)/shard_map/pallas_call | solution.py:70
  168.7 2.5 %shard_map.57.refs_2_ = f32[400,384]{1,0:T(8,128)S(1)} custom-call(bf16[384,384]{1,0:T(8,128)(2,1)S(1)} %maximum_multiply_fusion.q_ref, bf16[192,768]{1,0:T(8,128)(2,1)S(1)} %collective-permute-done.2.refs_0_, bf16[192,768]{1,0:T(8,128)(2,1)S(1)} %collective-permute-done.10.refs_1_, f32[400,384]{1,0:T(8,128)S(1)} %shard_map.56.refs_2_), custom_call_target="tpu_custom_call" | custom-call | flops 226492416 | bytes 589824 | tf_op jit(solution)/shard_map/pallas_call | solution.py:70
  171.2 2.5 %shard_map.58.refs_2_ = f32[400,384]{1,0:T(8,128)S(1)} custom-call(bf16[384,384]{1,0:T(8,128)(2,1)S(1)} %maximum_multiply_fusion.q_ref, bf16[192,768]{1,0:T(8,128)(2,1)S(1)} %collective-permute-done.3.refs_0_, bf16[192,768]{1,0:T(8,128)(2,1)S(1)} %collective-permute-done.11.refs_1_, f32[400,384]{1,0:T(8,128)S(1)} %shard_map.57.refs_2_), custom_call_target="tpu_custom_call" | custom-call | flops 226492416 | bytes 589824 | tf_op jit(solution)/shard_map/pallas_call | solution.py:70
  173.7 2.5 %shard_map.59.refs_2_ = f32[400,384]{1,0:T(8,128)S(1)} custom-call(bf16[384,384]{1,0:T(8,128)(2,1)S(1)} %maximum_multiply_fusion.q_ref, bf16[192,768]{1,0:T(8,128)(2,1)S(1)} %collective-permute-done.4.refs_0_, bf16[192,768]{1,0:T(8,128)(2,1)S(1)} %collective-permute-done.12.refs_1_, f32[400,384]{1,0:T(8,128)S(1)} %shard_map.58.refs_2_), custom_call_target="tpu_custom_call" | custom-call | flops 226492416 | bytes 589824 | tf_op jit(solution)/shard_map/pallas_call | solution.py:70
  176.2 2.5 %shard_map.60.refs_2_ = f32[400,384]{1,0:T(8,128)S(1)} custom-call(bf16[384,384]{1,0:T(8,128)(2,1)S(1)} %maximum_multiply_fusion.q_ref, bf16[192,768]{1,0:T(8,128)(2,1)S(1)} %collective-permute-done.5.refs_0_, bf16[192,768]{1,0:T(8,128)(2,1)S(1)} %collective-permute-done.13.refs_1_, f32[400,384]{1,0:T(8,128)S(1)} %shard_map.59.refs_2_), custom_call_target="tpu_custom_call" | custom-call | flops 226492416 | bytes 589824 | tf_op jit(solution)/shard_map/pallas_call | solution.py:70
  178.7 2.7 %shard_map.61.refs_2_ = f32[400,384]{1,0:T(8,128)S(1)} custom-call(bf16[384,384]{1,0:T(8,128)(2,1)S(1)} %maximum_multiply_fusion.q_ref, bf16[192,768]{1,0:T(8,128)(2,1)S(1)} %collective-permute-done.6.refs_0_, bf16[192,768]{1,0:T(8,128)(2,1)S(1)} %collective-permute-done.14.refs_1_, f32[400,384]{1,0:T(8,128)S(1)} %shard_map.60.refs_2_), custom_call_target="tpu_custom_call" | custom-call | flops 226492416 | bytes 589824 | tf_op jit(solution)/shard_map/pallas_call | solution.py:70
  181.4 2.5 %shard_map.62.refs_1_ = f32[400,384]{1,0:T(8,128)S(1)} custom-call(bf16[384,384]{1,0:T(8,128)(2,1)S(1)} %maximum_multiply_fusion.q_ref, bf16[192,768]{1,0:T(8,128)(2,1)S(1)} %collective-permute-done.7.refs_0_, bf16[192,768]{1,0:T(8,128)(2,1)S(1)} %collective-permute-done.15.refs_1_, f32[400,384]{1,0:T(8,128)S(1)} %shard_map.61.refs_2_), custom_call_target="tpu_custom_call" | custom-call | flops 226492416 | bytes 589824 | tf_op jit(solution)/shard_map/pallas_call | solution.py:70
  191.5 34.4 %all_to_all.11 = bf16[8,24,3072]{2,1,0:T(8,128)(2,1)S(1)} all-to-all(bf16[8,24,3072]{2,1,0:T(8,128)(2,1)S(1)} %bitcast.19), channel_id=1, replica_groups=mesh['group'=2,'blk'=32,'uly'=8] {'uly'}, dimensions={0} | all-to-all | bytes 2359296 | tf_op jit(solution)/shard_map/all_to_all | solution.py:208
  (51 shorter events, 23.2 us)
Async XLA Ops:
  1.9 70.1 %copy-start.2 = (bf16[384,96]{0,1:T(8,128)(2,1)S(1)}, bf16[384,96]{0,1:T(8,128)(2,1)}, u32[]{:S(2)}) copy-start(bf16[384,96]{0,1:T(8,128)(2,1)} %param.8) | copy-start | bytes 221188
  20.9 72.7 %copy-start = (bf16[8,24,1152]{2,1,0:T(8,128)(2,1)}, bf16[8,24,1152]{2,1,0:T(8,128)(2,1)S(1)}, u32[]{:S(2)}) copy-start(bf16[8,24,1152]{2,1,0:T(8,128)(2,1)S(1)} %all_to_all.10) | copy-start | bytes 1327108
  20.9 59.8 %collective-permute-start = (bf16[192,1152]{1,0:T(8,128)(2,1)S(1)}, bf16[192,1152]{1,0:T(8,128)(2,1)S(1)}, u32[]{:S(2)}, u32[]{:S(2)}) collective-permute-start(bf16[192,1152]{1,0:T(8,128)(2,1)S(1)} %bitcast.20), channel_id=1, source_target_pairs={{0,8},{8,0},{16,24},{24,16},{32,40},{40,32},{48,56},{56,48},{64,72... | collective-permute-start | bytes 1327112 | tf_op jit(solution)/shard_map/ppermute | solution.py:184
  60.2 15.5 %collective-permute-start.1 = (bf16[192,768]{1,0:T(8,128)(2,1)S(1)}, bf16[192,768]{1,0:T(8,128)(2,1)S(1)}, u32[]{:S(2)}, u32[]{:S(2)}) collective-permute-start(bf16[192,768]{1,0:T(8,128)(2,1)S(1)} %slice.30.refs_0_), channel_id=1, source_target_pairs={{0,16},{8,248},{16,32},{24,8},{32,48},{40,24},{48,64},{56,40},{64,... | collective-permute-start | bytes 884744 | tf_op jit(solution)/shard_map/ppermute | solution.py:201
  72.1 10.7 %collective-permute-start.17 = (bf16[96,384]{1,0:T(8,128)(2,1)S(1)}, bf16[96,384]{1,0:T(8,128)(2,1)S(1)}, u32[]{:S(2)}, u32[]{:S(2)}) collective-permute-start(bf16[96,384]{1,0:T(8,128)(2,1)S(1)} %bitcast.27), channel_id=1, source_target_pairs={{0,8},{8,0},{16,24},{24,16},{32,40},{40,32},{48,56},{56,48},{64,72... | collective-permute-start | bytes 221192 | tf_op jit(solution)/shard_map/ppermute | solution.py:179
  75.7 10.5 %collective-permute-start.2 = (bf16[192,768]{1,0:T(8,128)(2,1)S(1)}, bf16[192,768]{1,0:T(8,128)(2,1)S(1)}, u32[]{:S(2)}, u32[]{:S(2)}) collective-permute-start(bf16[192,768]{1,0:T(8,128)(2,1)S(1)} %collective-permute-done.1.refs_0_), channel_id=1, source_target_pairs={{0,16},{8,248},{16,32},{24,8},{32,48},{40,24},{48,64},{56,40},{64,... | collective-permute-start | bytes 884744 | tf_op jit(solution)/shard_map/ppermute | solution.py:201
  80.8 2.0 copy-start.1
  80.8 9.4 %collective-permute-start.9 = (bf16[192,768]{1,0:T(8,128)(2,1)S(1)}, bf16[192,768]{1,0:T(8,128)(2,1)S(1)}, u32[]{:S(2)}, u32[]{:S(2)}) collective-permute-start(bf16[192,768]{1,0:T(8,128)(2,1)S(1)} %slice.31), channel_id=1, source_target_pairs={{0,16},{8,248},{16,32},{24,8},{32,48},{40,24},{48,64},{56,40},{64,... | collective-permute-start | bytes 884744 | tf_op jit(solution)/shard_map/ppermute | solution.py:203
  82.9 10.7 %collective-permute-start.18 = (bf16[192,384]{1,0:T(8,128)(2,1)S(1)}, bf16[192,384]{1,0:T(8,128)(2,1)S(1)}, u32[]{:S(2)}, u32[]{:S(2)}) collective-permute-start(bf16[192,384]{1,0:T(8,128)(2,1)S(1)} %pad_maximum_fusion.5.self_ref), channel_id=1, source_target_pairs={{0,240},{8,24},{16,0},{24,40},{32,16},{40,56},{48,32},{56,72},{64,... | collective-permute-start | bytes 442376 | tf_op jit(solution)/shard_map/ppermute | solution.py:192
  86.3 9.3 %collective-permute-start.3 = (bf16[192,768]{1,0:T(8,128)(2,1)S(1)}, bf16[192,768]{1,0:T(8,128)(2,1)S(1)}, u32[]{:S(2)}, u32[]{:S(2)}) collective-permute-start(bf16[192,768]{1,0:T(8,128)(2,1)S(1)} %collective-permute-done.2.refs_0_), channel_id=1, source_target_pairs={{0,16},{8,248},{16,32},{24,8},{32,48},{40,24},{48,64},{56,40},{64,... | collective-permute-start | bytes 884744 | tf_op jit(solution)/shard_map/ppermute | solution.py:201
  90.2 9.8 %collective-permute-start.10 = (bf16[192,768]{1,0:T(8,128)(2,1)S(1)}, bf16[192,768]{1,0:T(8,128)(2,1)S(1)}, u32[]{:S(2)}, u32[]{:S(2)}) collective-permute-start(bf16[192,768]{1,0:T(8,128)(2,1)S(1)} %collective-permute-done.9.refs_1_), channel_id=1, source_target_pairs={{0,16},{8,248},{16,32},{24,8},{32,48},{40,24},{48,64},{56,40},{64,... | collective-permute-start | bytes 884744 | tf_op jit(solution)/shard_map/ppermute | solution.py:203
  93.6 14.4 %collective-permute-start.19 = (bf16[384,384]{1,0:T(8,128)(2,1)S(1)}, bf16[384,384]{1,0:T(8,128)(2,1)S(1)}, u32[]{:S(2)}, u32[]{:S(2)}) collective-permute-start(bf16[384,384]{1,0:T(8,128)(2,1)S(1)} %pad_maximum_fusion.4), channel_id=1, source_target_pairs={{0,224},{8,40},{16,240},{24,56},{32,0},{40,72},{48,16},{56,88},{64... | collective-permute-start | bytes 884744 | tf_op jit(solution)/shard_map/ppermute | solution.py:192
  95.6 14.5 %collective-permute-start.4 = (bf16[192,768]{1,0:T(8,128)(2,1)S(1)}, bf16[192,768]{1,0:T(8,128)(2,1)S(1)}, u32[]{:S(2)}, u32[]{:S(2)}) collective-permute-start(bf16[192,768]{1,0:T(8,128)(2,1)S(1)} %collective-permute-done.3.refs_0_), channel_id=1, source_target_pairs={{0,16},{8,248},{16,32},{24,8},{32,48},{40,24},{48,64},{56,40},{64,... | collective-permute-start | bytes 884744 | tf_op jit(solution)/shard_map/ppermute | solution.py:201
  100.0 12.9 %collective-permute-start.11 = (bf16[192,768]{1,0:T(8,128)(2,1)S(1)}, bf16[192,768]{1,0:T(8,128)(2,1)S(1)}, u32[]{:S(2)}, u32[]{:S(2)}) collective-permute-start(bf16[192,768]{1,0:T(8,128)(2,1)S(1)} %collective-permute-done.10.refs_1_), channel_id=1, source_target_pairs={{0,16},{8,248},{16,32},{24,8},{32,48},{40,24},{48,64},{56,40},{64,... | collective-permute-start | bytes 884744 | tf_op jit(solution)/shard_map/ppermute | solution.py:203
  108.1 28.1 %collective-permute-start.20 = (bf16[576,384]{1,0:T(8,128)(2,1)S(1)}, bf16[576,384]{1,0:T(8,128)(2,1)S(1)}, u32[]{:S(2)}, u32[]{:S(2)}) collective-permute-start(bf16[576,384]{1,0:T(8,128)(2,1)S(1)} %pad_maximum_fusion.3), channel_id=1, source_target_pairs={{0,208},{8,56},{16,224},{24,72},{32,240},{40,88},{48,0},{56,104},{... | collective-permute-start | bytes 1327112 | tf_op jit(solution)/shard_map/ppermute | solution.py:192
  110.1 16.6 %collective-permute-start.5 = (bf16[192,768]{1,0:T(8,128)(2,1)S(1)}, bf16[192,768]{1,0:T(8,128)(2,1)S(1)}, u32[]{:S(2)}, u32[]{:S(2)}) collective-permute-start(bf16[192,768]{1,0:T(8,128)(2,1)S(1)} %collective-permute-done.4.refs_0_), channel_id=1, source_target_pairs={{0,16},{8,248},{16,32},{24,8},{32,48},{40,24},{48,64},{56,40},{64,... | collective-permute-start | bytes 884744 | tf_op jit(solution)/shard_map/ppermute | solution.py:201
  112.9 20.9 %collective-permute-start.12 = (bf16[192,768]{1,0:T(8,128)(2,1)S(1)}, bf16[192,768]{1,0:T(8,128)(2,1)S(1)}, u32[]{:S(2)}, u32[]{:S(2)}) collective-permute-start(bf16[192,768]{1,0:T(8,128)(2,1)S(1)} %collective-permute-done.11.refs_1_), channel_id=1, source_target_pairs={{0,16},{8,248},{16,32},{24,8},{32,48},{40,24},{48,64},{56,40},{64,... | collective-permute-start | bytes 884744 | tf_op jit(solution)/shard_map/ppermute | solution.py:203
  126.7 13.5 %collective-permute-start.6 = (bf16[192,768]{1,0:T(8,128)(2,1)S(1)}, bf16[192,768]{1,0:T(8,128)(2,1)S(1)}, u32[]{:S(2)}, u32[]{:S(2)}) collective-permute-start(bf16[192,768]{1,0:T(8,128)(2,1)S(1)} %collective-permute-done.5.refs_0_), channel_id=1, source_target_pairs={{0,16},{8,248},{16,32},{24,8},{32,48},{40,24},{48,64},{56,40},{64,... | collective-permute-start | bytes 884744 | tf_op jit(solution)/shard_map/ppermute | solution.py:201
  133.8 9.8 %collective-permute-start.13 = (bf16[192,768]{1,0:T(8,128)(2,1)S(1)}, bf16[192,768]{1,0:T(8,128)(2,1)S(1)}, u32[]{:S(2)}, u32[]{:S(2)}) collective-permute-start(bf16[192,768]{1,0:T(8,128)(2,1)S(1)} %collective-permute-done.12.refs_1_), channel_id=1, source_target_pairs={{0,16},{8,248},{16,32},{24,8},{32,48},{40,24},{48,64},{56,40},{64,... | collective-permute-start | bytes 884744 | tf_op jit(solution)/shard_map/ppermute | solution.py:203
  136.2 14.8 %collective-permute-start.21 = (bf16[384,384]{1,0:T(8,128)(2,1)S(1)}, bf16[384,384]{1,0:T(8,128)(2,1)}, u32[]{:S(2)}, u32[]{:S(2)}) collective-permute-start(bf16[384,384]{1,0:T(8,128)(2,1)S(1)} %slice.32), channel_id=1, source_target_pairs={{0,224},{8,40},{16,240},{24,56},{32,0},{40,72},{48,16},{56,88},{64... | collective-permute-start | bytes 884744 | tf_op jit(solution)/shard_map/ppermute | solution.py:192
  140.3 14.7 %collective-permute-start.7 = (bf16[192,768]{1,0:T(8,128)(2,1)S(1)}, bf16[192,768]{1,0:T(8,128)(2,1)S(1)}, u32[]{:S(2)}, u32[]{:S(2)}) collective-permute-start(bf16[192,768]{1,0:T(8,128)(2,1)S(1)} %collective-permute-done.6.refs_0_), channel_id=1, source_target_pairs={{0,16},{8,248},{16,32},{24,8},{32,48},{40,24},{48,64},{56,40},{64,... | collective-permute-start | bytes 884744 | tf_op jit(solution)/shard_map/ppermute | solution.py:201
  143.6 16.4 %collective-permute-start.14 = (bf16[192,768]{1,0:T(8,128)(2,1)S(1)}, bf16[192,768]{1,0:T(8,128)(2,1)S(1)}, u32[]{:S(2)}, u32[]{:S(2)}) collective-permute-start(bf16[192,768]{1,0:T(8,128)(2,1)S(1)} %collective-permute-done.13.refs_1_), channel_id=1, source_target_pairs={{0,16},{8,248},{16,32},{24,8},{32,48},{40,24},{48,64},{56,40},{64,... | collective-permute-start | bytes 884744 | tf_op jit(solution)/shard_map/ppermute | solution.py:203
  152.1 36.6 %collective-permute-start.22 = (bf16[1344,384]{1,0:T(8,128)(2,1)S(1)}, bf16[1344,384]{1,0:T(8,128)(2,1)S(1)}, u32[]{:S(2)}, u32[]{:S(2)}) collective-permute-start(bf16[1344,384]{1,0:T(8,128)(2,1)S(1)} %pad_maximum_fusion.mine_ref), channel_id=1, source_target_pairs={{0,8},{8,0},{16,24},{24,16},{32,40},{40,32},{48,56},{56,48},{64,72... | collective-permute-start | bytes 3096584 | tf_op jit(solution)/shard_map/ppermute | solution.py:196
  155.0 28.9 %collective-permute-start.8 = (bf16[192,768]{1,0:T(8,128)(2,1)S(1)}, bf16[192,768]{1,0:T(8,128)(2,1)S(1)}, u32[]{:S(2)}, u32[]{:S(2)}) collective-permute-start(bf16[192,768]{1,0:T(8,128)(2,1)S(1)} %collective-permute-done.7.refs_0_), channel_id=1, source_target_pairs={{0,16},{8,248},{16,32},{24,8},{32,48},{40,24},{48,64},{56,40},{64,... | collective-permute-start | bytes 884744 | tf_op jit(solution)/shard_map/ppermute | solution.py:201
  160.0 21.4 %collective-permute-start.15 = (bf16[192,768]{1,0:T(8,128)(2,1)S(1)}, bf16[192,768]{1,0:T(8,128)(2,1)S(1)}, u32[]{:S(2)}, u32[]{:S(2)}) collective-permute-start(bf16[192,768]{1,0:T(8,128)(2,1)S(1)} %collective-permute-done.14.refs_1_), channel_id=1, source_target_pairs={{0,16},{8,248},{16,32},{24,8},{32,48},{40,24},{48,64},{56,40},{64,... | collective-permute-start | bytes 884744 | tf_op jit(solution)/shard_map/ppermute | solution.py:203
  185.7 4.0 %collective-permute-start.16 = (f32[400,384]{1,0:T(8,128)S(1)}, f32[400,384]{1,0:T(8,128)S(1)}, u32[]{:S(2)}, u32[]{:S(2)}) collective-permute-start(f32[400,384]{1,0:T(8,128)S(1)} %shard_map.63.one_ref), channel_id=1, source_target_pairs={{0,8},{8,0},{16,24},{24,16},{32,40},{40,32},{48,56},{56,48},{64,72... | collective-permute-start | bytes 1843208 | tf_op jit(solution)/shard_map/ppermute | solution.py:205
  225.9 0.7 copy-start.3

commit v3 on v2

--- a/solution.py
+++ b/solution.py
@@ -96,51 +96,65 @@
     return jnp.concatenate(parts, axis=0).astype(jnp.bfloat16).T
 
 
-def project_kernel(
-    depth, place_ref, one_ref, two_ref, self_ref, mine_ref, theirs_ref, far_ref, out_ref, attended, weight
+def lay_out(weight, blocks, core, mine_ref, theirs_ref):
+    pair = weight.shape[0] // (2 * len(blocks) + 1)
+    for here, step in enumerate(blocks):
+        block = slice(here * pair, (here + 1) * pair)
+        for ref, way in ((mine_ref, 1 - 2 * core), (theirs_ref, 2 * core - 1)):
+            at = pl.multiple_of((len(blocks) + way * step) * pair, 8)
+            weight[pl.ds(at, pair), :] = ref[block, :]
+
+
+def times_weight(mine, weight, out_ref):
+    chunks = 3
+    chunk = weight.shape[0] // chunks if weight.shape[0] % (chunks * 128) == 0 else weight.shape[0]
+    for at in range(0, weight.shape[0], chunk):
+        part = slice(at, at + chunk)
+        out_ref[:, part] = nt_dot(mine, weight[part, :]).astype(out_ref.dtype)
+
+
+def near_kernel(
+    core_ref, one_ref, two_ref, self_ref, mine_ref, theirs_ref, out_ref, own_ref, attended, weight
 ):
-    z, core = place_ref[0], place_ref[1]
-    rows, width = out_ref.shape
-    features = attended.shape[1]
+    core = core_ref[0]
+    rows, features = own_ref.shape
     pair = self_ref.shape[0]
-    last = depth // 2
-
-    def put(chip, block):
-        at = pl.multiple_of(lax.rem(chip, depth) * pair, 16)
-        weight[pl.ds(at, pair), :] = block
-
-    put(z, self_ref[...])
-    put(z + last, far_ref[...])
-    for step in range(1, last):
-        block = slice((step - 1) * pair, step * pair)
-        ahead, behind = z + step, z + depth - step
-        put(jnp.where(core == 0, ahead, behind), mine_ref[block, :])
-        put(jnp.where(core == 0, behind, ahead), theirs_ref[block, :])
-
+    near = mine_ref.shape[0] // pair
+    weight[near * pair : (near + 1) * pair, :] = self_ref[...]
+    lay_out(weight, range(1, near + 1), core, mine_ref, theirs_ref)
     attended[...] = merged(one_ref, two_ref, features)
-    mine = attended[pl.ds(pl.multiple_of(core * rows, 16), rows), :]
-    chunk = width // 4
-    for i in range(4):
-        part = slice(i * chunk, (i + 1) * chunk)
-        out_ref[:, part] = nt_dot(mine, weight[part, :]).astype(out_ref.dtype)
-
-
-def project(depth, place, one, two, weights):
-    row_count = one.shape[1]
-    features = weights[0].shape[1]
-    width = weights[0].shape[0] * depth
+    own_ref[...] = attended[pl.ds(pl.multiple_of(core * rows, 8), rows), :]
+    times_weight(own_ref[...], weight, out_ref)
+
+
+def far_kernel(core_ref, own_ref, mine_ref, theirs_ref, out_ref, weight):
+    core = core_ref[0]
+    pair = mine_ref.shape[0] - theirs_ref.shape[0]
+    far = theirs_ref.shape[0] // pair
+    weight[far * pair : (far + 1) * pair, :] = mine_ref[far * pair :, :]
+    lay_out(weight, [i - far for i in range(far)], core, mine_ref, theirs_ref)
+    times_weight(own_ref[...], weight, out_ref)
+
+
+def project(kernel, core, operands, width, attended_shape=None):
+    rows, features = attended_shape or operands[0].shape
     vmem = pl.BlockSpec(memory_space=pltpu.VMEM)
+    out = jax.ShapeDtypeStruct((rows, width), jnp.bfloat16)
+    weight = pltpu.VMEM((width, features), jnp.bfloat16)
+    first = attended_shape is not None
     return pl.pallas_call(
-        functools.partial(project_kernel, depth),
-        out_shape=jax.ShapeDtypeStruct((row_count // 2, width), jnp.bfloat16),
-        in_specs=[pl.BlockSpec(memory_space=pltpu.SMEM)] + [vmem] * 6,
-        out_specs=vmem,
-        scratch_shapes=[
-            pltpu.VMEM((row_count, features), jnp.bfloat16),
-            pltpu.VMEM((width, features), jnp.bfloat16),
-        ],
+        kernel,
+        out_shape=(out, jax.ShapeDtypeStruct((rows, features), jnp.bfloat16)) if first else out,
+        in_specs=[pl.BlockSpec(memory_space=pltpu.SMEM)] + [vmem] * len(operands),
+        out_specs=(vmem, vmem) if first else vmem,
+        scratch_shapes=(
+            [pltpu.VMEM((2 * rows, features), jnp.bfloat16), weight] if first else [weight]
+        ),
         compiler_params=pltpu.CompilerParams(vmem_limit_bytes=VMEM_LIMIT),
-    )(place, one, two, *weights)
+        cost_estimate=pl.CostEstimate(
+            flops=2 * rows * features * width, bytes_accessed=2 * width * features, transcendentals=0
+        ),
+    )(core[None], *operands)
 
 
 def weight_hops(depth):
@@ -149,6 +163,9 @@
         hops.append(min(held, 3, last + 1 - held))
         held += hops[-1]
     return hops
+
+
+EARLY = 2
 
 
 def on_device(query, keys, values, out_weight, out_gain):
@@ -158,7 +175,8 @@
     last = depth // 2
     features = width // uly
     rows = tokens * uly
-    z, core = lax.axis_index("blk") // 2, lax.axis_index("blk") % 2
+    at = lax.axis_index("blk").astype(jnp.int32)
+    z, core = lax.div(at, 2), lax.rem(at, 2)
     swap = [(i, i ^ 1) for i in range(blk)]
 
     def round_z(hop):
@@ -186,14 +204,18 @@
     q_all = q_all * jnp.bfloat16(1.0 / math.sqrt(HEAD))
 
     pair = w_self.shape[0]
+    hops = weight_hops(depth)
     held, w_parts = 1, [w_self]
-    for hop in weight_hops(depth):
+    for hop in hops:
         send = jnp.concatenate(w_parts, axis=0)[(held - hop) * pair :]
         w_parts.append(lax.ppermute(send, "blk", round_z(-hop)))
         held += hop
-    w_got = jnp.concatenate(w_parts[1:], axis=0)
-    w_mine, w_far = w_got[:-pair], w_got[-pair:]
-    w_theirs = lax.ppermute(w_mine, "blk", swap)
+    near = sum(hops[:EARLY])
+    w_near, w_far = (
+        jnp.concatenate(parts, axis=0) for parts in (w_parts[1 : EARLY + 1], w_parts[EARLY + 1 :])
+    )
+    near_theirs = lax.ppermute(w_near, "blk", swap)
+    far_theirs = lax.ppermute(w_far[:-pair], "blk", swap)
 
     a, b = own[:, features:], other[:, features:]
     state = fold(q_all, (a,), None)
@@ -203,10 +225,25 @@
             b = lax.ppermute(b, "blk", ring)
         state = fold(q_all, (a, b) if step < last else (a,), state)
     theirs = lax.ppermute(state, "blk", swap)
-    place = jnp.stack([z, core]).astype(jnp.int32)
-    partial = project(depth, place, state, theirs, (w_self, w_mine, w_theirs, w_far))
-    blocks = lax.all_to_all(partial.reshape(uly, tokens, width), "uly", 0, 0, tiled=True)
-    summed = jnp.sum(blocks.astype(jnp.float32), axis=0)
+
+    def exchanged(partial):
+        blocks = partial.reshape(uly, tokens, partial.shape[1])
+        blocks = lax.all_to_all(blocks, "uly", 0, 0, tiled=True)
+        return jnp.sum(blocks.astype(jnp.float32), axis=0)
+
+    near_width = (2 * near + 1) * pair
+    partial, attended = project(
+        near_kernel,
+        core,
+        (state, theirs, w_self, w_near, near_theirs),
+        near_width,
+        (rows, features),
+    )
+    near_sum = exchanged(partial)
+    partial = project(far_kernel, core, (attended, w_far, far_theirs), width - near_width)
+    far_sum = exchanged(partial)
+    turned = jnp.concatenate([near_sum, far_sum] * 2, axis=1)
+    summed = lax.dynamic_slice_in_dim(turned, lax.rem(near + depth - z, depth) * pair, width, axis=1)
     return (out_gain * summed).astype(jnp.bfloat16)
 
 

time: 228 us -> 245 us (1.075)
  blocking collectives: 53.4 us -> 18.9 us
  starting transfers between devices: 118 us -> 144 us
  waiting for transfers between devices: 25.6 us -> 49.4 us
    all_to_all x1 -> x0, blocking collectives: 34.4 us -> none  [on_device(): lax.all_to_all(partial.reshape(uly, tokens, width), 'uly', 0, 0, tiled=True)]
    all_to_all x0 -> x2, waiting for transfers between devices: none -> 30.1 us  [exchanged(): blocks = lax.all_to_all(blocks, 'uly', 0, 0, tiled=True)]
    ppermute x1, starting transfers between devices: 1.95 us -> 10.1 us  [on_device(): theirs = lax.ppermute(state, 'blk', swap)]
    all_to_all x0 -> x2, starting transfers between devices: none -> 7.49 us  [exchanged(): blocks = lax.all_to_all(blocks, 'uly', 0, 0, tiled=True)]
    ppermute x8, starting transfers between devices: 38.9 us -> 45.5 us  [on_device(): a = lax.ppermute(a, 'blk', ring)]
    ppermute x8, waiting for transfers between devices: 10.4 us -> 5.51 us  [on_device(): a = lax.ppermute(a, 'blk', ring)]
    ppermute x7, waiting for transfers between devices: 4.42 us -> 0.02 us  [on_device(): b = lax.ppermute(b, 'blk', ring)]
    ppermute x4, starting transfers between devices: 11.3 us -> 14 us  [on_device(): w_parts.append(lax.ppermute(send, 'blk', round_z(-hop)))]
  transfers between devices with their start and end apart: 23 -> 26, of which waited for: 7 -> 9; matrix products, arithmetic and copies ran while one was open for 1% -> 1% of each run, Pallas kernels for 9% -> 10%
where the time goes in v3:
time: 245 us; the launch traced here: 243 us
  starting transfers between devices  144 us (59%)
  waiting for transfers between devices  49.4 us (20%)
  Pallas kernels  24.3 us (10%)
  blocking collectives  18.9 us (8%)
  local copies, waits for them, and re-layouts  3.69 us (2%)
    ppermute x8, starting transfers between devices, on_device(): a = lax.ppermute(a, 'blk', ring)  45.5 us
    ppermute x1, starting transfers between devices, on_device(): other = lax.ppermute(own, 'blk', swap)  39.4 us
    all_to_all x2, waiting for transfers between devices, exchanged(): blocks = lax.all_to_all(blocks, 'uly', 0, 0, tiled=True)  30.1 us
    pallas_call x9, Pallas kernels, fold(): pl.pallas_call(functools.partial(fold_kernel, state is None), out_shape=j...  21.2 us
    ppermute x7, starting transfers between devices, on_device(): b = lax.ppermute(b, 'blk', ring)  19.6 us
    all_to_all x1, blocking collectives, on_device(): lax.all_to_all(packed, 'uly', 0, 0, tiled=True).reshape(rows, 3 * features)  18.9 us
    ppermute x4, starting transfers between devices, on_device(): w_parts.append(lax.ppermute(send, 'blk', round_z(-hop)))  14 us
    ppermute x4, waiting for transfers between devices, on_device(): w_parts.append(lax.ppermute(send, 'blk', round_z(-hop)))  11.8 us
  transfers between devices with their start and end apart: 26, of which 9 were waited for; matrix products, arithmetic and copies ran while one was open for 1% of the time, Pallas kernels for 10%

profile of v3, /device:TPU:65, one launch (start us, length us, event | category | flops | bytes accessed | tf_op | source)
XLA Modules:
  0.0 242.9 jit_solution(3277921588876847069)
XLA Ops:
  2.0 18.9 %all_to_all.15 = bf16[8,24,1152]{2,1,0:T(8,128)(2,1)S(1)} all-to-all(bf16[8,24,1152]{2,1,0:T(8,128)(2,1)S(1)} %maximum_bitcast_fusion), channel_id=1, replica_groups=mesh['group'=2,'blk'=32,'uly'=8] {'uly'}, dimensions={0} | all-to-all | bytes 884736 | tf_op jit(solution)/shard_map/all_to_all | solution.py:201
  20.9 39.4 %collective-permute-start = (bf16[192,1152]{1,0:T(8,128)(2,1)S(1)}, bf16[192,1152]{1,0:T(8,128)(2,1)S(1)}, u32[]{:S(2)}, u32[]{:S(2)}) collective-permute-start(bf16[192,1152]{1,0:T(8,128)(2,1)S(1)} %bitcast.19), channel_id=1, source_target_pairs={{0,8},{8,0},{16,24},{24,16},{32,40},{40,32},{48,56},{56,48},{64,72... | collective-permute-start | bytes 1327112 | tf_op jit(solution)/shard_map/ppermute | solution.py:202
  60.4 11.8 %collective-permute-start.1 = (bf16[192,768]{1,0:T(8,128)(2,1)S(1)}, bf16[192,768]{1,0:T(8,128)(2,1)S(1)}, u32[]{:S(2)}, u32[]{:S(2)}) collective-permute-start(bf16[192,768]{1,0:T(8,128)(2,1)S(1)} %slice.26.refs_0_), channel_id=1, source_target_pairs={{0,16},{8,248},{16,32},{24,8},{32,48},{40,24},{48,64},{56,40},{64,... | collective-permute-start | bytes 884744 | tf_op jit(solution)/shard_map/ppermute | solution.py:223
  72.2 3.6 %collective-permute-done.1.refs_0_ = bf16[192,768]{1,0:T(8,128)(2,1)S(1)} collective-permute-done((bf16[192,768]{1,0:T(8,128)(2,1)S(1)}, bf16[192,768]{1,0:T(8,128)(2,1)S(1)}, u32[]{:S(2)}, u32[]{:S(2)}) %collective-permute-start.1) | collective-permute-done | bytes 294944 | tf_op jit(solution)/shard_map/ppermute | solution.py:223
  75.8 5.0 %collective-permute-start.2 = (bf16[192,768]{1,0:T(8,128)(2,1)S(1)}, bf16[192,768]{1,0:T(8,128)(2,1)S(1)}, u32[]{:S(2)}, u32[]{:S(2)}) collective-permute-start(bf16[192,768]{1,0:T(8,128)(2,1)S(1)} %collective-permute-done.1.refs_0_), channel_id=1, source_target_pairs={{0,16},{8,248},{16,32},{24,8},{32,48},{40,24},{48,64},{56,40},{64,... | collective-permute-start | bytes 884744 | tf_op jit(solution)/shard_map/ppermute | solution.py:223
  84.5 5.0 %collective-permute-start.3 = (bf16[192,768]{1,0:T(8,128)(2,1)S(1)}, bf16[192,768]{1,0:T(8,128)(2,1)S(1)}, u32[]{:S(2)}, u32[]{:S(2)}) collective-permute-start(bf16[192,768]{1,0:T(8,128)(2,1)S(1)} %collective-permute-done.2.refs_0_), channel_id=1, source_target_pairs={{0,16},{8,248},{16,32},{24,8},{32,48},{40,24},{48,64},{56,40},{64,... | collective-permute-start | bytes 884744 | tf_op jit(solution)/shard_map/ppermute | solution.py:223
  89.6 3.1 %collective-permute-start.10 = (bf16[192,768]{1,0:T(8,128)(2,1)S(1)}, bf16[192,768]{1,0:T(8,128)(2,1)S(1)}, u32[]{:S(2)}, u32[]{:S(2)}) collective-permute-start(bf16[192,768]{1,0:T(8,128)(2,1)S(1)} %collective-permute-done.9.refs_1_), channel_id=1, source_target_pairs={{0,16},{8,248},{16,32},{24,8},{32,48},{40,24},{48,64},{56,40},{64,... | collective-permute-start | bytes 884744 | tf_op jit(solution)/shard_map/ppermute | solution.py:225
  93.2 5.0 %collective-permute-start.4 = (bf16[192,768]{1,0:T(8,128)(2,1)S(1)}, bf16[192,768]{1,0:T(8,128)(2,1)S(1)}, u32[]{:S(2)}, u32[]{:S(2)}) collective-permute-start(bf16[192,768]{1,0:T(8,128)(2,1)S(1)} %collective-permute-done.3.refs_0_), channel_id=1, source_target_pairs={{0,16},{8,248},{16,32},{24,8},{32,48},{40,24},{48,64},{56,40},{64,... | collective-permute-start | bytes 884744 | tf_op jit(solution)/shard_map/ppermute | solution.py:223
  98.3 3.1 %collective-permute-start.11 = (bf16[192,768]{1,0:T(8,128)(2,1)S(1)}, bf16[192,768]{1,0:T(8,128)(2,1)S(1)}, u32[]{:S(2)}, u32[]{:S(2)}) collective-permute-start(bf16[192,768]{1,0:T(8,128)(2,1)S(1)} %collective-permute-done.10.refs_1_), channel_id=1, source_target_pairs={{0,16},{8,248},{16,32},{24,8},{32,48},{40,24},{48,64},{56,40},{64,... | collective-permute-start | bytes 884744 | tf_op jit(solution)/shard_map/ppermute | solution.py:225
  101.9 5.0 %collective-permute-start.5 = (bf16[192,768]{1,0:T(8,128)(2,1)S(1)}, bf16[192,768]{1,0:T(8,128)(2,1)S(1)}, u32[]{:S(2)}, u32[]{:S(2)}) collective-permute-start(bf16[192,768]{1,0:T(8,128)(2,1)S(1)} %collective-permute-done.4.refs_0_), channel_id=1, source_target_pairs={{0,16},{8,248},{16,32},{24,8},{32,48},{40,24},{48,64},{56,40},{64,... | collective-permute-start | bytes 884744 | tf_op jit(solution)/shard_map/ppermute | solution.py:223
  107.0 3.1 %collective-permute-start.12 = (bf16[192,768]{1,0:T(8,128)(2,1)S(1)}, bf16[192,768]{1,0:T(8,128)(2,1)S(1)}, u32[]{:S(2)}, u32[]{:S(2)}) collective-permute-start(bf16[192,768]{1,0:T(8,128)(2,1)S(1)} %collective-permute-done.11.refs_1_), channel_id=1, source_target_pairs={{0,16},{8,248},{16,32},{24,8},{32,48},{40,24},{48,64},{56,40},{64,... | collective-permute-start | bytes 884744 | tf_op jit(solution)/shard_map/ppermute | solution.py:225
  110.2 3.6 %collective-permute-start.17 = (bf16[96,384]{1,0:T(8,128)(2,1)S(1)}, bf16[96,384]{1,0:T(8,128)(2,1)S(1)}, u32[]{:S(2)}, u32[]{:S(2)}) collective-permute-start(bf16[96,384]{1,0:T(8,128)(2,1)S(1)} %bitcast.26), channel_id=1, source_target_pairs={{0,8},{8,0},{16,24},{24,16},{32,40},{40,32},{48,56},{56,48},{64,72... | collective-permute-start | bytes 221192 | tf_op jit(solution)/shard_map/ppermute | solution.py:197
  113.8 4.9 %collective-permute-start.6 = (bf16[192,768]{1,0:T(8,128)(2,1)S(1)}, bf16[192,768]{1,0:T(8,128)(2,1)S(1)}, u32[]{:S(2)}, u32[]{:S(2)}) collective-permute-start(bf16[192,768]{1,0:T(8,128)(2,1)S(1)} %collective-permute-done.5.refs_0_), channel_id=1, source_target_pairs={{0,16},{8,248},{16,32},{24,8},{32,48},{40,24},{48,64},{56,40},{64,... | collective-permute-start | bytes 884744 | tf_op jit(solution)/shard_map/ppermute | solution.py:223
  121.3 2.9 %collective-permute-start.18 = (bf16[192,384]{1,0:T(8,128)(2,1)S(1)}, bf16[192,384]{1,0:T(8,128)(2,1)S(1)}, u32[]{:S(2)}, u32[]{:S(2)}) collective-permute-start(bf16[192,384]{1,0:T(8,128)(2,1)S(1)} %pad_maximum_fusion.1.self_ref), channel_id=1, source_target_pairs={{0,240},{8,24},{16,0},{24,40},{32,16},{40,56},{48,32},{56,72},{64,... | collective-permute-start | bytes 442376 | tf_op jit(solution)/shard_map/ppermute | solution.py:211
  124.1 3.7 %collective-permute-start.7 = (bf16[192,768]{1,0:T(8,128)(2,1)S(1)}, bf16[192,768]{1,0:T(8,128)(2,1)S(1)}, u32[]{:S(2)}, u32[]{:S(2)}) collective-permute-start(bf16[192,768]{1,0:T(8,128)(2,1)S(1)} %collective-permute-done.6.refs_0_), channel_id=1, source_target_pairs={{0,16},{8,248},{16,32},{24,8},{32,48},{40,24},{48,64},{56,40},{64,... | collective-permute-start | bytes 884744 | tf_op jit(solution)/shard_map/ppermute | solution.py:223
  127.8 2.7 %collective-permute-start.14 = (bf16[192,768]{1,0:T(8,128)(2,1)S(1)}, bf16[192,768]{1,0:T(8,128)(2,1)S(1)}, u32[]{:S(2)}, u32[]{:S(2)}) collective-permute-start(bf16[192,768]{1,0:T(8,128)(2,1)S(1)} %collective-permute-done.13.refs_1_), channel_id=1, source_target_pairs={{0,16},{8,248},{16,32},{24,8},{32,48},{40,24},{48,64},{56,40},{64,... | collective-permute-start | bytes 884744 | tf_op jit(solution)/shard_map/ppermute | solution.py:225
  132.7 4.9 %collective-permute-start.8 = (bf16[192,768]{1,0:T(8,128)(2,1)S(1)}, bf16[192,768]{1,0:T(8,128)(2,1)S(1)}, u32[]{:S(2)}, u32[]{:S(2)}) collective-permute-start(bf16[192,768]{1,0:T(8,128)(2,1)S(1)} %collective-permute-done.7.refs_0_), channel_id=1, source_target_pairs={{0,16},{8,248},{16,32},{24,8},{32,48},{40,24},{48,64},{56,40},{64,... | collective-permute-start | bytes 884744 | tf_op jit(solution)/shard_map/ppermute | solution.py:223
  137.6 3.1 %collective-permute-start.15 = (bf16[192,768]{1,0:T(8,128)(2,1)S(1)}, bf16[192,768]{1,0:T(8,128)(2,1)S(1)}, u32[]{:S(2)}, u32[]{:S(2)}) collective-permute-start(bf16[192,768]{1,0:T(8,128)(2,1)S(1)} %collective-permute-done.14.refs_1_), channel_id=1, source_target_pairs={{0,16},{8,248},{16,32},{24,8},{32,48},{40,24},{48,64},{56,40},{64,... | collective-permute-start | bytes 884744 | tf_op jit(solution)/shard_map/ppermute | solution.py:225
  143.4 2.5 %shard_map.56.refs_2_ = f32[400,384]{1,0:T(8,128)S(1)} custom-call(bf16[384,384]{1,0:T(8,128)(2,1)S(1)} %maximum_multiply_fusion.q_ref, bf16[192,768]{1,0:T(8,128)(2,1)S(1)} %collective-permute-done.1.refs_0_, bf16[192,768]{1,0:T(8,128)(2,1)S(1)} %collective-permute-done.9.refs_1_, f32[400,384]{1,0:T(8,128)S(1)} %shard_map.55.refs_2_), custom_call_target="tpu_custom_call" | custom-call | flops 226492416 | bytes 589824 | tf_op jit(solution)/shard_map/pallas_call | solution.py:70
  145.9 2.5 %shard_map.57.refs_2_ = f32[400,384]{1,0:T(8,128)S(1)} custom-call(bf16[384,384]{1,0:T(8,128)(2,1)S(1)} %maximum_multiply_fusion.q_ref, bf16[192,768]{1,0:T(8,128)(2,1)S(1)} %collective-permute-done.2.refs_0_, bf16[192,768]{1,0:T(8,128)(2,1)S(1)} %collective-permute-done.10.refs_1_, f32[400,384]{1,0:T(8,128)S(1)} %shard_map.56.refs_2_), custom_call_target="tpu_custom_call" | custom-call | flops 226492416 | bytes 589824 | tf_op jit(solution)/shard_map/pallas_call | solution.py:70
  148.4 2.5 %shard_map.58.refs_2_ = f32[400,384]{1,0:T(8,128)S(1)} custom-call(bf16[384,384]{1,0:T(8,128)(2,1)S(1)} %maximum_multiply_fusion.q_ref, bf16[192,768]{1,0:T(8,128)(2,1)S(1)} %collective-permute-done.3.refs_0_, bf16[192,768]{1,0:T(8,128)(2,1)S(1)} %collective-permute-done.11.refs_1_, f32[400,384]{1,0:T(8,128)S(1)} %shard_map.57.refs_2_), custom_call_target="tpu_custom_call" | custom-call | flops 226492416 | bytes 589824 | tf_op jit(solution)/shard_map/pallas_call | solution.py:70
  150.9 2.5 %shard_map.59.refs_2_ = f32[400,384]{1,0:T(8,128)S(1)} custom-call(bf16[384,384]{1,0:T(8,128)(2,1)S(1)} %maximum_multiply_fusion.q_ref, bf16[192,768]{1,0:T(8,128)(2,1)S(1)} %collective-permute-done.4.refs_0_, bf16[192,768]{1,0:T(8,128)(2,1)S(1)} %collective-permute-done.12.refs_1_, f32[400,384]{1,0:T(8,128)S(1)} %shard_map.58.refs_2_), custom_call_target="tpu_custom_call" | custom-call | flops 226492416 | bytes 589824 | tf_op jit(solution)/shard_map/pallas_call | solution.py:70
  153.4 2.5 %shard_map.60.refs_2_ = f32[400,384]{1,0:T(8,128)S(1)} custom-call(bf16[384,384]{1,0:T(8,128)(2,1)S(1)} %maximum_multiply_fusion.q_ref, bf16[192,768]{1,0:T(8,128)(2,1)S(1)} %collective-permute-done.5.refs_0_, bf16[192,768]{1,0:T(8,128)(2,1)S(1)} %collective-permute-done.13.refs_1_, f32[400,384]{1,0:T(8,128)S(1)} %shard_map.59.refs_2_), custom_call_target="tpu_custom_call" | custom-call | flops 226492416 | bytes 589824 | tf_op jit(solution)/shard_map/pallas_call | solution.py:70
  155.9 2.7 %shard_map.61.refs_2_ = f32[400,384]{1,0:T(8,128)S(1)} custom-call(bf16[384,384]{1,0:T(8,128)(2,1)S(1)} %maximum_multiply_fusion.q_ref, bf16[192,768]{1,0:T(8,128)(2,1)S(1)} %collective-permute-done.6.refs_0_, bf16[192,768]{1,0:T(8,128)(2,1)S(1)} %collective-permute-done.14.refs_1_, f32[400,384]{1,0:T(8,128)S(1)} %shard_map.60.refs_2_), custom_call_target="tpu_custom_call" | custom-call | flops 226492416 | bytes 589824 | tf_op jit(solution)/shard_map/pallas_call | solution.py:70
  158.6 2.5 %shard_map.62.refs_1_ = f32[400,384]{1,0:T(8,128)S(1)} custom-call(bf16[384,384]{1,0:T(8,128)(2,1)S(1)} %maximum_multiply_fusion.q_ref, bf16[192,768]{1,0:T(8,128)(2,1)S(1)} %collective-permute-done.7.refs_0_, bf16[192,768]{1,0:T(8,128)(2,1)S(1)} %collective-permute-done.15.refs_1_, f32[400,384]{1,0:T(8,128)S(1)} %shard_map.61.refs_2_), custom_call_target="tpu_custom_call" | custom-call | flops 226492416 | bytes 589824 | tf_op jit(solution)/shard_map/pallas_call | solution.py:70
  162.9 10.1 %collective-permute-start.16 = (f32[400,384]{1,0:T(8,128)S(1)}, f32[400,384]{1,0:T(8,128)S(1)}, u32[]{:S(2)}, u32[]{:S(2)}) collective-permute-start(f32[400,384]{1,0:T(8,128)S(1)} %shard_map.63.one_ref), channel_id=1, source_target_pairs={{0,8},{8,0},{16,24},{24,16},{32,40},{40,32},{48,56},{56,48},{64,72... | collective-permute-start | bytes 1843208 | tf_op jit(solution)/shard_map/ppermute | solution.py:227
  177.4 10.8 %collective-permute-done.21 = bf16[576,384]{1,0:T(8,128)(2,1)S(1)} collective-permute-done((bf16[576,384]{1,0:T(8,128)(2,1)S(1)}, bf16[576,384]{1,0:T(8,128)(2,1)S(1)}, u32[]{:S(2)}, u32[]{:S(2)}) %collective-permute-start.21) | collective-permute-done | bytes 442400 | tf_op jit(solution)/shard_map/ppermute | solution.py:211
  188.2 7.1 %collective-permute-start.22 = (bf16[384,384]{1,0:T(8,128)(2,1)S(1)}, bf16[384,384]{1,0:T(8,128)(2,1)S(1)}, u32[]{:S(2)}, u32[]{:S(2)}) collective-permute-start(bf16[384,384]{1,0:T(8,128)(2,1)S(1)} %slice.28), channel_id=1, source_target_pairs={{0,224},{8,40},{16,240},{24,56},{32,0},{40,72},{48,16},{56,88},{64... | collective-permute-start | bytes 884744 | tf_op jit(solution)/shard_map/ppermute | solution.py:211
  196.8 3.7 %all-to-all-start.1 = ((bf16[8,24,1344]{2,1,0:T(8,128)(2,1)}), bf16[8,24,1344]{2,1,0:T(8,128)(2,1)S(1)}, u32[]{:S(2)}, u32[]{:S(2)}) async-start(bf16[8,24,1344]{2,1,0:T(8,128)(2,1)} %bitcast.4), calls=%async_computation.1 | async-start | bytes 1081344 | tf_op jit(solution)/shard_map/all_to_all | solution.py:231
  207.3 10.8 %all-to-all-done.1 = bf16[8,24,1344]{2,1,0:T(8,128)(2,1)S(1)} async-done(((bf16[8,24,1344]{2,1,0:T(8,128)(2,1)}), bf16[8,24,1344]{2,1,0:T(8,128)(2,1)S(1)}, u32[]{:S(2)}, u32[]{:S(2)}) %all-to-all-start.1) | async-done | bytes 516128 | tf_op jit(solution)/shard_map/all_to_all | solution.py:231
  218.1 3.7 %all-to-all-start.2 = ((bf16[8,24,1728]{2,1,0:T(8,128)(2,1)}), bf16[8,24,1728]{2,1,0:T(8,128)(2,1)S(1)}, u32[]{:S(2)}, u32[]{:S(2)}) async-start(bf16[8,24,1728]{2,1,0:T(8,128)(2,1)} %bitcast.5), calls=%async_computation.2 | async-start | bytes 1376256 | tf_op jit(solution)/shard_map/all_to_all | solution.py:231
  221.9 19.4 %all-to-all-done.2 = bf16[8,24,1728]{2,1,0:T(8,128)(2,1)S(1)} async-done(((bf16[8,24,1728]{2,1,0:T(8,128)(2,1)}), bf16[8,24,1728]{2,1,0:T(8,128)(2,1)S(1)}, u32[]{:S(2)}, u32[]{:S(2)}) %all-to-all-start.2) | async-done | bytes 663584 | tf_op jit(solution)/shard_map/all_to_all | solution.py:231
  (58 shorter events, 30.1 us)
Async XLA Ops:
  20.9 89.2 %copy-start.1 = (bf16[384,96]{0,1:T(8,128)(2,1)S(1)}, bf16[384,96]{0,1:T(8,128)(2,1)}, u32[]{:S(2)}) copy-start(bf16[384,96]{0,1:T(8,128)(2,1)} %param.8) | copy-start | bytes 221188
  20.9 60.0 %collective-permute-start = (bf16[192,1152]{1,0:T(8,128)(2,1)S(1)}, bf16[192,1152]{1,0:T(8,128)(2,1)S(1)}, u32[]{:S(2)}, u32[]{:S(2)}) collective-permute-start(bf16[192,1152]{1,0:T(8,128)(2,1)S(1)} %bitcast.19), channel_id=1, source_target_pairs={{0,8},{8,0},{16,24},{24,16},{32,40},{40,32},{48,56},{56,48},{64,72... | collective-permute-start | bytes 1327112 | tf_op jit(solution)/shard_map/ppermute | solution.py:202
  60.4 15.5 %collective-permute-start.1 = (bf16[192,768]{1,0:T(8,128)(2,1)S(1)}, bf16[192,768]{1,0:T(8,128)(2,1)S(1)}, u32[]{:S(2)}, u32[]{:S(2)}) collective-permute-start(bf16[192,768]{1,0:T(8,128)(2,1)S(1)} %slice.26.refs_0_), channel_id=1, source_target_pairs={{0,16},{8,248},{16,32},{24,8},{32,48},{40,24},{48,64},{56,40},{64,... | collective-permute-start | bytes 884744 | tf_op jit(solution)/shard_map/ppermute | solution.py:223
  75.8 8.7 %collective-permute-start.2 = (bf16[192,768]{1,0:T(8,128)(2,1)S(1)}, bf16[192,768]{1,0:T(8,128)(2,1)S(1)}, u32[]{:S(2)}, u32[]{:S(2)}) collective-permute-start(bf16[192,768]{1,0:T(8,128)(2,1)S(1)} %collective-permute-done.1.refs_0_), channel_id=1, source_target_pairs={{0,16},{8,248},{16,32},{24,8},{32,48},{40,24},{48,64},{56,40},{64,... | collective-permute-start | bytes 884744 | tf_op jit(solution)/shard_map/ppermute | solution.py:223
  80.9 0.8 copy-start
  81.7 7.9 %collective-permute-start.9 = (bf16[192,768]{1,0:T(8,128)(2,1)S(1)}, bf16[192,768]{1,0:T(8,128)(2,1)S(1)}, u32[]{:S(2)}, u32[]{:S(2)}) collective-permute-start(bf16[192,768]{1,0:T(8,128)(2,1)S(1)} %slice.27), channel_id=1, source_target_pairs={{0,16},{8,248},{16,32},{24,8},{32,48},{40,24},{48,64},{56,40},{64,... | collective-permute-start | bytes 884744 | tf_op jit(solution)/shard_map/ppermute | solution.py:225
  84.5 8.7 %collective-permute-start.3 = (bf16[192,768]{1,0:T(8,128)(2,1)S(1)}, bf16[192,768]{1,0:T(8,128)(2,1)S(1)}, u32[]{:S(2)}, u32[]{:S(2)}) collective-permute-start(bf16[192,768]{1,0:T(8,128)(2,1)S(1)} %collective-permute-done.2.refs_0_), channel_id=1, source_target_pairs={{0,16},{8,248},{16,32},{24,8},{32,48},{40,24},{48,64},{56,40},{64,... | collective-permute-start | bytes 884744 | tf_op jit(solution)/shard_map/ppermute | solution.py:223
  89.6 8.7 %collective-permute-start.10 = (bf16[192,768]{1,0:T(8,128)(2,1)S(1)}, bf16[192,768]{1,0:T(8,128)(2,1)S(1)}, u32[]{:S(2)}, u32[]{:S(2)}) collective-permute-start(bf16[192,768]{1,0:T(8,128)(2,1)S(1)} %collective-permute-done.9.refs_1_), channel_id=1, source_target_pairs={{0,16},{8,248},{16,32},{24,8},{32,48},{40,24},{48,64},{56,40},{64,... | collective-permute-start | bytes 884744 | tf_op jit(solution)/shard_map/ppermute | solution.py:225
  93.2 8.7 %collective-permute-start.4 = (bf16[192,768]{1,0:T(8,128)(2,1)S(1)}, bf16[192,768]{1,0:T(8,128)(2,1)S(1)}, u32[]{:S(2)}, u32[]{:S(2)}) collective-permute-start(bf16[192,768]{1,0:T(8,128)(2,1)S(1)} %collective-permute-done.3.refs_0_), channel_id=1, source_target_pairs={{0,16},{8,248},{16,32},{24,8},{32,48},{40,24},{48,64},{56,40},{64,... | collective-permute-start | bytes 884744 | tf_op jit(solution)/shard_map/ppermute | solution.py:223
  98.3 8.7 %collective-permute-start.11 = (bf16[192,768]{1,0:T(8,128)(2,1)S(1)}, bf16[192,768]{1,0:T(8,128)(2,1)S(1)}, u32[]{:S(2)}, u32[]{:S(2)}) collective-permute-start(bf16[192,768]{1,0:T(8,128)(2,1)S(1)} %collective-permute-done.10.refs_1_), channel_id=1, source_target_pairs={{0,16},{8,248},{16,32},{24,8},{32,48},{40,24},{48,64},{56,40},{64,... | collective-permute-start | bytes 884744 | tf_op jit(solution)/shard_map/ppermute | solution.py:225
  101.9 11.9 %collective-permute-start.5 = (bf16[192,768]{1,0:T(8,128)(2,1)S(1)}, bf16[192,768]{1,0:T(8,128)(2,1)S(1)}, u32[]{:S(2)}, u32[]{:S(2)}) collective-permute-start(bf16[192,768]{1,0:T(8,128)(2,1)S(1)} %collective-permute-done.4.refs_0_), channel_id=1, source_target_pairs={{0,16},{8,248},{16,32},{24,8},{32,48},{40,24},{48,64},{56,40},{64,... | collective-permute-start | bytes 884744 | tf_op jit(solution)/shard_map/ppermute | solution.py:223
  107.0 11.7 %collective-permute-start.12 = (bf16[192,768]{1,0:T(8,128)(2,1)S(1)}, bf16[192,768]{1,0:T(8,128)(2,1)S(1)}, u32[]{:S(2)}, u32[]{:S(2)}) collective-permute-start(bf16[192,768]{1,0:T(8,128)(2,1)S(1)} %collective-permute-done.11.refs_1_), channel_id=1, source_target_pairs={{0,16},{8,248},{16,32},{24,8},{32,48},{40,24},{48,64},{56,40},{64,... | collective-permute-start | bytes 884744 | tf_op jit(solution)/shard_map/ppermute | solution.py:225
  110.2 11.0 %collective-permute-start.17 = (bf16[96,384]{1,0:T(8,128)(2,1)S(1)}, bf16[96,384]{1,0:T(8,128)(2,1)S(1)}, u32[]{:S(2)}, u32[]{:S(2)}) collective-permute-start(bf16[96,384]{1,0:T(8,128)(2,1)S(1)} %bitcast.26), channel_id=1, source_target_pairs={{0,8},{8,0},{16,24},{24,16},{32,40},{40,32},{48,56},{56,48},{64,72... | collective-permute-start | bytes 221192 | tf_op jit(solution)/shard_map/ppermute | solution.py:197
  113.8 10.3 %collective-permute-start.6 = (bf16[192,768]{1,0:T(8,128)(2,1)S(1)}, bf16[192,768]{1,0:T(8,128)(2,1)S(1)}, u32[]{:S(2)}, u32[]{:S(2)}) collective-permute-start(bf16[192,768]{1,0:T(8,128)(2,1)S(1)} %collective-permute-done.5.refs_0_), channel_id=1, source_target_pairs={{0,16},{8,248},{16,32},{24,8},{32,48},{40,24},{48,64},{56,40},{64,... | collective-permute-start | bytes 884744 | tf_op jit(solution)/shard_map/ppermute | solution.py:223
  118.7 9.1 %collective-permute-start.13 = (bf16[192,768]{1,0:T(8,128)(2,1)S(1)}, bf16[192,768]{1,0:T(8,128)(2,1)S(1)}, u32[]{:S(2)}, u32[]{:S(2)}) collective-permute-start(bf16[192,768]{1,0:T(8,128)(2,1)S(1)} %collective-permute-done.12.refs_1_), channel_id=1, source_target_pairs={{0,16},{8,248},{16,32},{24,8},{32,48},{40,24},{48,64},{56,40},{64,... | collective-permute-start | bytes 884744 | tf_op jit(solution)/shard_map/ppermute | solution.py:225
  121.3 9.3 %collective-permute-start.18 = (bf16[192,384]{1,0:T(8,128)(2,1)S(1)}, bf16[192,384]{1,0:T(8,128)(2,1)S(1)}, u32[]{:S(2)}, u32[]{:S(2)}) collective-permute-start(bf16[192,384]{1,0:T(8,128)(2,1)S(1)} %pad_maximum_fusion.1.self_ref), channel_id=1, source_target_pairs={{0,240},{8,24},{16,0},{24,40},{32,16},{40,56},{48,32},{56,72},{64,... | collective-permute-start | bytes 442376 | tf_op jit(solution)/shard_map/ppermute | solution.py:211
  124.1 8.6 %collective-permute-start.7 = (bf16[192,768]{1,0:T(8,128)(2,1)S(1)}, bf16[192,768]{1,0:T(8,128)(2,1)S(1)}, u32[]{:S(2)}, u32[]{:S(2)}) collective-permute-start(bf16[192,768]{1,0:T(8,128)(2,1)S(1)} %collective-permute-done.6.refs_0_), channel_id=1, source_target_pairs={{0,16},{8,248},{16,32},{24,8},{32,48},{40,24},{48,64},{56,40},{64,... | collective-permute-start | bytes 884744 | tf_op jit(solution)/shard_map/ppermute | solution.py:223
  127.8 9.8 %collective-permute-start.14 = (bf16[192,768]{1,0:T(8,128)(2,1)S(1)}, bf16[192,768]{1,0:T(8,128)(2,1)S(1)}, u32[]{:S(2)}, u32[]{:S(2)}) collective-permute-start(bf16[192,768]{1,0:T(8,128)(2,1)S(1)} %collective-permute-done.13.refs_1_), channel_id=1, source_target_pairs={{0,16},{8,248},{16,32},{24,8},{32,48},{40,24},{48,64},{56,40},{64,... | collective-permute-start | bytes 884744 | tf_op jit(solution)/shard_map/ppermute | solution.py:225
  130.6 42.4 %collective-permute-start.19 = (bf16[384,384]{1,0:T(8,128)(2,1)S(1)}, bf16[384,384]{1,0:T(8,128)(2,1)S(1)}, u32[]{:S(2)}, u32[]{:S(2)}) collective-permute-start(bf16[384,384]{1,0:T(8,128)(2,1)S(1)} %pad_maximum_fusion), channel_id=1, source_target_pairs={{0,224},{8,40},{16,240},{24,56},{32,0},{40,72},{48,16},{56,88},{64... | collective-permute-start | bytes 884744 | tf_op jit(solution)/shard_map/ppermute | solution.py:211
  132.7 28.4 %collective-permute-start.8 = (bf16[192,768]{1,0:T(8,128)(2,1)S(1)}, bf16[192,768]{1,0:T(8,128)(2,1)S(1)}, u32[]{:S(2)}, u32[]{:S(2)}) collective-permute-start(bf16[192,768]{1,0:T(8,128)(2,1)S(1)} %collective-permute-done.7.refs_0_), channel_id=1, source_target_pairs={{0,16},{8,248},{16,32},{24,8},{32,48},{40,24},{48,64},{56,40},{64,... | collective-permute-start | bytes 884744 | tf_op jit(solution)/shard_map/ppermute | solution.py:223
  137.6 21.0 %collective-permute-start.15 = (bf16[192,768]{1,0:T(8,128)(2,1)S(1)}, bf16[192,768]{1,0:T(8,128)(2,1)S(1)}, u32[]{:S(2)}, u32[]{:S(2)}) collective-permute-start(bf16[192,768]{1,0:T(8,128)(2,1)S(1)} %collective-permute-done.14.refs_1_), channel_id=1, source_target_pairs={{0,16},{8,248},{16,32},{24,8},{32,48},{40,24},{48,64},{56,40},{64,... | collective-permute-start | bytes 884744 | tf_op jit(solution)/shard_map/ppermute | solution.py:225
  162.9 32.4 %collective-permute-start.16 = (f32[400,384]{1,0:T(8,128)S(1)}, f32[400,384]{1,0:T(8,128)S(1)}, u32[]{:S(2)}, u32[]{:S(2)}) collective-permute-start(f32[400,384]{1,0:T(8,128)S(1)} %shard_map.63.one_ref), channel_id=1, source_target_pairs={{0,8},{8,0},{16,24},{24,16},{32,40},{40,32},{48,56},{56,48},{64,72... | collective-permute-start | bytes 1843208 | tf_op jit(solution)/shard_map/ppermute | solution.py:227
  173.1 15.0 %collective-permute-start.21 = (bf16[576,384]{1,0:T(8,128)(2,1)S(1)}, bf16[576,384]{1,0:T(8,128)(2,1)S(1)}, u32[]{:S(2)}, u32[]{:S(2)}) collective-permute-start(bf16[576,384]{1,0:T(8,128)(2,1)S(1)} %constant_dynamic-update-slice_fusion.mine_ref), channel_id=1, source_target_pairs={{0,208},{8,56},{16,224},{24,72},{32,240},{40,88},{48,0},{56,104},{... | collective-permute-start | bytes 1327112 | tf_op jit(solution)/shard_map/ppermute | solution.py:211
  175.1 20.2 %collective-permute-start.20 = (bf16[576,384]{1,0:T(8,128)(2,1)S(1)}, bf16[576,384]{1,0:T(8,128)(2,1)S(1)}, u32[]{:S(2)}, u32[]{:S(2)}) collective-permute-start(bf16[576,384]{1,0:T(8,128)(2,1)S(1)} %constant_dynamic-update-slice_fusion.mine_ref), channel_id=1, source_target_pairs={{0,8},{8,0},{16,24},{24,16},{32,40},{40,32},{48,56},{56,48},{64,72... | collective-permute-start | bytes 1327112 | tf_op jit(solution)/shard_map/ppermute | solution.py:217
  188.2 13.5 %collective-permute-start.22 = (bf16[384,384]{1,0:T(8,128)(2,1)S(1)}, bf16[384,384]{1,0:T(8,128)(2,1)S(1)}, u32[]{:S(2)}, u32[]{:S(2)}) collective-permute-start(bf16[384,384]{1,0:T(8,128)(2,1)S(1)} %slice.28), channel_id=1, source_target_pairs={{0,224},{8,40},{16,240},{24,56},{32,0},{40,72},{48,16},{56,88},{64... | collective-permute-start | bytes 884744 | tf_op jit(solution)/shard_map/ppermute | solution.py:211
  196.8 21.2 %all-to-all-start.1 = ((bf16[8,24,1344]{2,1,0:T(8,128)(2,1)}), bf16[8,24,1344]{2,1,0:T(8,128)(2,1)S(1)}, u32[]{:S(2)}, u32[]{:S(2)}) async-start(bf16[8,24,1344]{2,1,0:T(8,128)(2,1)} %bitcast.4), calls=%async_computation.1 | async-start | bytes 1081344 | tf_op jit(solution)/shard_map/all_to_all | solution.py:231
  201.8 3.9 %collective-permute-start.23 = (bf16[768,384]{1,0:T(8,128)(2,1)S(1)}, bf16[768,384]{1,0:T(8,128)(2,1)S(1)}, u32[]{:S(2)}, u32[]{:S(2)}) collective-permute-start(bf16[768,384]{1,0:T(8,128)(2,1)S(1)} %slice.29), channel_id=1, source_target_pairs={{0,8},{8,0},{16,24},{24,16},{32,40},{40,32},{48,56},{56,48},{64,72... | collective-permute-start | bytes 1769480 | tf_op jit(solution)/shard_map/ppermute | solution.py:218
  218.1 23.2 %all-to-all-start.2 = ((bf16[8,24,1728]{2,1,0:T(8,128)(2,1)}), bf16[8,24,1728]{2,1,0:T(8,128)(2,1)S(1)}, u32[]{:S(2)}, u32[]{:S(2)}) async-start(bf16[8,24,1728]{2,1,0:T(8,128)(2,1)} %bitcast.5), calls=%async_computation.2 | async-start | bytes 1376256 | tf_op jit(solution)/shard_map/all_to_all | solution.py:231
  241.4 0.7 copy-start.2

commit v4 on v2

--- a/solution.py
+++ b/solution.py
@@ -96,29 +96,30 @@
     return jnp.concatenate(parts, axis=0).astype(jnp.bfloat16).T
 
 
-def project_kernel(
-    depth, place_ref, one_ref, two_ref, self_ref, mine_ref, theirs_ref, far_ref, out_ref, attended, weight
-):
+def project_kernel(depth, place_ref, one_ref, two_ref, self_ref, *refs):
+    *got_refs, out_ref, attended, weight = refs
     z, core = place_ref[0], place_ref[1]
     rows, width = out_ref.shape
     features = attended.shape[1]
     pair = self_ref.shape[0]
-    last = depth // 2
 
     def put(chip, block):
-        at = pl.multiple_of(lax.rem(chip, depth) * pair, 16)
+        at = pl.multiple_of(lax.rem(chip, depth) * pair, 8)
         weight[pl.ds(at, pair), :] = block
 
     put(z, self_ref[...])
-    put(z + last, far_ref[...])
-    for step in range(1, last):
-        block = slice((step - 1) * pair, step * pair)
-        ahead, behind = z + step, z + depth - step
-        put(jnp.where(core == 0, ahead, behind), mine_ref[block, :])
-        put(jnp.where(core == 0, behind, ahead), theirs_ref[block, :])
+    step = 1
+    for crossed, turned in zip(got_refs[::2], got_refs[1::2] + [None]):
+        for here in range(0, crossed.shape[0], pair):
+            block = slice(here, here + pair)
+            ahead, behind = z + step, z + depth - step
+            put(jnp.where(core == 0, behind, ahead), crossed[block, :])
+            if turned is not None:
+                put(jnp.where(core == 0, ahead, behind), turned[block, :])
+            step += 1
 
     attended[...] = merged(one_ref, two_ref, features)
-    mine = attended[pl.ds(pl.multiple_of(core * rows, 16), rows), :]
+    mine = attended[pl.ds(pl.multiple_of(core * rows, 8), rows), :]
     chunk = width // 4
     for i in range(4):
         part = slice(i * chunk, (i + 1) * chunk)
@@ -133,7 +134,7 @@
     return pl.pallas_call(
         functools.partial(project_kernel, depth),
         out_shape=jax.ShapeDtypeStruct((row_count // 2, width), jnp.bfloat16),
-        in_specs=[pl.BlockSpec(memory_space=pltpu.SMEM)] + [vmem] * 6,
+        in_specs=[pl.BlockSpec(memory_space=pltpu.SMEM)] + [vmem] * (2 + len(weights)),
         out_specs=vmem,
         scratch_shapes=[
             pltpu.VMEM((row_count, features), jnp.bfloat16),
@@ -146,7 +147,7 @@
 def weight_hops(depth):
     held, hops, last = 1, [], depth // 2
     while held <= last:
-        hops.append(min(held, 3, last + 1 - held))
+        hops.append(2 if held == 2 and last > 2 else 1)
         held += hops[-1]
     return hops
 
@@ -158,7 +159,8 @@
     last = depth // 2
     features = width // uly
     rows = tokens * uly
-    z, core = lax.axis_index("blk") // 2, lax.axis_index("blk") % 2
+    at = lax.axis_index("blk").astype(jnp.int32)
+    z, core = lax.div(at, 2), lax.rem(at, 2)
     swap = [(i, i ^ 1) for i in range(blk)]
 
     def round_z(hop):
@@ -186,14 +188,18 @@
     q_all = q_all * jnp.bfloat16(1.0 / math.sqrt(HEAD))
 
     pair = w_self.shape[0]
-    held, w_parts = 1, [w_self]
-    for hop in weight_hops(depth):
-        send = jnp.concatenate(w_parts, axis=0)[(held - hop) * pair :]
-        w_parts.append(lax.ppermute(send, "blk", round_z(-hop)))
-        held += hop
-    w_got = jnp.concatenate(w_parts[1:], axis=0)
-    w_mine, w_far = w_got[:-pair], w_got[-pair:]
-    w_theirs = lax.ppermute(w_mine, "blk", swap)
+    hops = weight_hops(depth)
+    weights, held = [w_self], w_self
+    for i, hop in enumerate(hops):
+        crossing = [
+            (2 * z + c, 2 * ((z + (-hop if c == 0 else hop)) % depth) + 1 - c)
+            for z in range(depth)
+            for c in range(2)
+        ]
+        weights.append(lax.ppermute(held[-hop * pair :], "blk", crossing))
+        if i + 1 < len(hops):
+            weights.append(lax.ppermute(weights[-1], "blk", swap))
+            held = jnp.concatenate([held, weights[-1]], axis=0)[-2 * pair :]
 
     a, b = own[:, features:], other[:, features:]
     state = fold(q_all, (a,), None)
@@ -204,7 +210,7 @@
         state = fold(q_all, (a, b) if step < last else (a,), state)
     theirs = lax.ppermute(state, "blk", swap)
     place = jnp.stack([z, core]).astype(jnp.int32)
-    partial = project(depth, place, state, theirs, (w_self, w_mine, w_theirs, w_far))
+    partial = project(depth, place, state, theirs, weights)
     blocks = lax.all_to_all(partial.reshape(uly, tokens, width), "uly", 0, 0, tiled=True)
     summed = jnp.sum(blocks.astype(jnp.float32), axis=0)
     return (out_gain * summed).astype(jnp.bfloat16)

time: 228 us -> 245 us (1.075)
  starting transfers between devices: 118 us -> 139 us
  waiting for transfers between devices: 25.6 us -> 22.8 us
    ppermute x5 -> x13, starting transfers between devices: 14.2 us -> 29.3 us  [the longest x7 15.3 us: on_device(): weights.append(lax.ppermute(held[-hop * pair:], 'blk', crossing))]
    ppermute x5 -> x13, waiting for transfers between devices: 9.8 us -> 19.1 us  [the longest x7 14.4 us: on_device(): weights.append(lax.ppermute(held[-hop * pair:], 'blk', crossing))]
    ppermute x8, waiting for transfers between devices: 10.4 us -> 3.66 us  [on_device(): a = lax.ppermute(a, 'blk', ring)]
    ppermute x8, starting transfers between devices: 38.9 us -> 45 us  [on_device(): a = lax.ppermute(a, 'blk', ring)]
    ppermute x7, waiting for transfers between devices: 4.42 us -> 0.02 us  [on_device(): b = lax.ppermute(b, 'blk', ring)]
  transfers between devices with their start and end apart: 23 -> 31, of which waited for: 7 -> 8; matrix products, arithmetic and copies ran while one was open for 1% -> 0% of each run, Pallas kernels for 9% -> 9%
where the time goes in v4:
time: 245 us; the launch traced here: 243 us
  starting transfers between devices  139 us (57%)
  blocking collectives  51.9 us (21%)
  Pallas kernels  23.4 us (10%)
  waiting for transfers between devices  22.8 us (9%)
  local copies, waits for them, and re-layouts  3.31 us (1%)
    ppermute x8, starting transfers between devices, on_device(): a = lax.ppermute(a, 'blk', ring)  45 us
    ppermute x1, starting transfers between devices, on_device(): other = lax.ppermute(own, 'blk', swap)  39.3 us
    all_to_all x1, blocking collectives, on_device(): lax.all_to_all(partial.reshape(uly, tokens, width), 'uly', 0, 0, tiled=True)  32.8 us
    pallas_call x9, Pallas kernels, fold(): pl.pallas_call(functools.partial(fold_kernel, state is None), out_shape=j...  21.2 us
    ppermute x7, starting transfers between devices, on_device(): b = lax.ppermute(b, 'blk', ring)  20.8 us
    all_to_all x1, blocking collectives, on_device(): lax.all_to_all(packed, 'uly', 0, 0, tiled=True).reshape(rows, 3 * features)  19 us
    ppermute x7, starting transfers between devices, on_device(): weights.append(lax.ppermute(held[-hop * pair:], 'blk', crossing))  15.3 us
    ppermute x7, waiting for transfers between devices, on_device(): weights.append(lax.ppermute(held[-hop * pair:], 'blk', crossing))  14.4 us
  transfers between devices with their start and end apart: 31, of which 8 were waited for; matrix products, arithmetic and copies ran while one was open for 0% of the time, Pallas kernels for 9%

profile of v4, /device:TPU:65, one launch (start us, length us, event | category | flops | bytes accessed | tf_op | source)
XLA Modules:
  0.0 243.0 jit_solution(14014513273797186647)
XLA Ops:
  2.0 19.0 %all_to_all.10 = bf16[8,24,1152]{2,1,0:T(8,128)(2,1)S(1)} all-to-all(bf16[8,24,1152]{2,1,0:T(8,128)(2,1)S(1)} %maximum_bitcast_fusion), channel_id=1, replica_groups=mesh['group'=2,'blk'=32,'uly'=8] {'uly'}, dimensions={0} | all-to-all | bytes 884736 | tf_op jit(solution)/shard_map/all_to_all | solution.py:185
  21.1 39.3 %collective-permute-start = (bf16[192,1152]{1,0:T(8,128)(2,1)S(1)}, bf16[192,1152]{1,0:T(8,128)(2,1)S(1)}, u32[]{:S(2)}, u32[]{:S(2)}) collective-permute-start(bf16[192,1152]{1,0:T(8,128)(2,1)S(1)} %bitcast.20), channel_id=1, source_target_pairs={{0,8},{8,0},{16,24},{24,16},{32,40},{40,32},{48,56},{56,48},{64,72... | collective-permute-start | bytes 1327112 | tf_op jit(solution)/shard_map/ppermute | solution.py:186
  60.4 11.8 %collective-permute-start.1 = (bf16[192,768]{1,0:T(8,128)(2,1)S(1)}, bf16[192,768]{1,0:T(8,128)(2,1)S(1)}, u32[]{:S(2)}, u32[]{:S(2)}) collective-permute-start(bf16[192,768]{1,0:T(8,128)(2,1)S(1)} %slice.34.refs_0_), channel_id=1, source_target_pairs={{0,16},{8,248},{16,32},{24,8},{32,48},{40,24},{48,64},{56,40},{64,... | collective-permute-start | bytes 884744 | tf_op jit(solution)/shard_map/ppermute | solution.py:207
  72.2 3.6 %collective-permute-done.1.refs_0_ = bf16[192,768]{1,0:T(8,128)(2,1)S(1)} collective-permute-done((bf16[192,768]{1,0:T(8,128)(2,1)S(1)}, bf16[192,768]{1,0:T(8,128)(2,1)S(1)}, u32[]{:S(2)}, u32[]{:S(2)}) %collective-permute-start.1) | collective-permute-done | bytes 294944 | tf_op jit(solution)/shard_map/ppermute | solution.py:207
  75.8 5.0 %collective-permute-start.2 = (bf16[192,768]{1,0:T(8,128)(2,1)S(1)}, bf16[192,768]{1,0:T(8,128)(2,1)S(1)}, u32[]{:S(2)}, u32[]{:S(2)}) collective-permute-start(bf16[192,768]{1,0:T(8,128)(2,1)S(1)} %collective-permute-done.1.refs_0_), channel_id=1, source_target_pairs={{0,16},{8,248},{16,32},{24,8},{32,48},{40,24},{48,64},{56,40},{64,... | collective-permute-start | bytes 884744 | tf_op jit(solution)/shard_map/ppermute | solution.py:207
  85.6 3.9 %collective-permute-start.3 = (bf16[192,768]{1,0:T(8,128)(2,1)S(1)}, bf16[192,768]{1,0:T(8,128)(2,1)S(1)}, u32[]{:S(2)}, u32[]{:S(2)}) collective-permute-start(bf16[192,768]{1,0:T(8,128)(2,1)S(1)} %collective-permute-done.2.refs_0_), channel_id=1, source_target_pairs={{0,16},{8,248},{16,32},{24,8},{32,48},{40,24},{48,64},{56,40},{64,... | collective-permute-start | bytes 884744 | tf_op jit(solution)/shard_map/ppermute | solution.py:207
  89.6 3.1 %collective-permute-start.10 = (bf16[192,768]{1,0:T(8,128)(2,1)S(1)}, bf16[192,768]{1,0:T(8,128)(2,1)S(1)}, u32[]{:S(2)}, u32[]{:S(2)}) collective-permute-start(bf16[192,768]{1,0:T(8,128)(2,1)S(1)} %collective-permute-done.9.refs_1_), channel_id=1, source_target_pairs={{0,16},{8,248},{16,32},{24,8},{32,48},{40,24},{48,64},{56,40},{64,... | collective-permute-start | bytes 884744 | tf_op jit(solution)/shard_map/ppermute | solution.py:209
  94.8 3.9 %collective-permute-start.4 = (bf16[192,768]{1,0:T(8,128)(2,1)S(1)}, bf16[192,768]{1,0:T(8,128)(2,1)S(1)}, u32[]{:S(2)}, u32[]{:S(2)}) collective-permute-start(bf16[192,768]{1,0:T(8,128)(2,1)S(1)} %collective-permute-done.3.refs_0_), channel_id=1, source_target_pairs={{0,16},{8,248},{16,32},{24,8},{32,48},{40,24},{48,64},{56,40},{64,... | collective-permute-start | bytes 884744 | tf_op jit(solution)/shard_map/ppermute | solution.py:207
  98.7 3.7 %collective-permute-start.11 = (bf16[192,768]{1,0:T(8,128)(2,1)S(1)}, bf16[192,768]{1,0:T(8,128)(2,1)S(1)}, u32[]{:S(2)}, u32[]{:S(2)}) collective-permute-start(bf16[192,768]{1,0:T(8,128)(2,1)S(1)} %collective-permute-done.10.refs_1_), channel_id=1, source_target_pairs={{0,16},{8,248},{16,32},{24,8},{32,48},{40,24},{48,64},{56,40},{64,... | collective-permute-start | bytes 884744 | tf_op jit(solution)/shard_map/ppermute | solution.py:209
  102.4 3.1 %collective-permute-start.19 = (bf16[192,384]{1,0:T(8,128)(2,1)S(1)}, bf16[192,384]{1,0:T(8,128)(2,1)S(1)}, u32[]{:S(2)}, u32[]{:S(2)}) collective-permute-start(bf16[192,384]{1,0:T(8,128)(2,1)S(1)} %collective-permute-done.18.refs_0_), channel_id=1, source_target_pairs={{0,8},{8,0},{16,24},{24,16},{32,40},{40,32},{48,56},{56,48},{64,72... | collective-permute-start | bytes 442376 | tf_op jit(solution)/shard_map/ppermute | solution.py:201
  108.5 4.9 %collective-permute-start.5 = (bf16[192,768]{1,0:T(8,128)(2,1)S(1)}, bf16[192,768]{1,0:T(8,128)(2,1)S(1)}, u32[]{:S(2)}, u32[]{:S(2)}) collective-permute-start(bf16[192,768]{1,0:T(8,128)(2,1)S(1)} %collective-permute-done.4.refs_0_), channel_id=1, source_target_pairs={{0,16},{8,248},{16,32},{24,8},{32,48},{40,24},{48,64},{56,40},{64,... | collective-permute-start | bytes 884744 | tf_op jit(solution)/shard_map/ppermute | solution.py:207
  113.4 3.1 %collective-permute-start.12 = (bf16[192,768]{1,0:T(8,128)(2,1)S(1)}, bf16[192,768]{1,0:T(8,128)(2,1)S(1)}, u32[]{:S(2)}, u32[]{:S(2)}) collective-permute-start(bf16[192,768]{1,0:T(8,128)(2,1)S(1)} %collective-permute-done.11.refs_1_), channel_id=1, source_target_pairs={{0,16},{8,248},{16,32},{24,8},{32,48},{40,24},{48,64},{56,40},{64,... | collective-permute-start | bytes 884744 | tf_op jit(solution)/shard_map/ppermute | solution.py:209
  116.5 4.7 %collective-permute-done.20.refs_2_ = bf16[384,384]{1,0:T(8,128)(2,1)S(1)} collective-permute-done((bf16[384,384]{1,0:T(8,128)(2,1)S(1)}, bf16[384,384]{1,0:T(8,128)(2,1)S(1)}, u32[]{:S(2)}, u32[]{:S(2)}) %collective-permute-start.20) | collective-permute-done | bytes 294944 | tf_op jit(solution)/shard_map/ppermute | solution.py:199
  123.2 6.1 %collective-permute-start.6 = (bf16[192,768]{1,0:T(8,128)(2,1)S(1)}, bf16[192,768]{1,0:T(8,128)(2,1)S(1)}, u32[]{:S(2)}, u32[]{:S(2)}) collective-permute-start(bf16[192,768]{1,0:T(8,128)(2,1)S(1)} %collective-permute-done.5.refs_0_), channel_id=1, source_target_pairs={{0,16},{8,248},{16,32},{24,8},{32,48},{40,24},{48,64},{56,40},{64,... | collective-permute-start | bytes 884744 | tf_op jit(solution)/shard_map/ppermute | solution.py:207
  133.3 4.7 %collective-permute-start.7 = (bf16[192,768]{1,0:T(8,128)(2,1)S(1)}, bf16[192,768]{1,0:T(8,128)(2,1)S(1)}, u32[]{:S(2)}, u32[]{:S(2)}) collective-permute-start(bf16[192,768]{1,0:T(8,128)(2,1)S(1)} %collective-permute-done.6.refs_0_), channel_id=1, source_target_pairs={{0,16},{8,248},{16,32},{24,8},{32,48},{40,24},{48,64},{56,40},{64,... | collective-permute-start | bytes 884744 | tf_op jit(solution)/shard_map/ppermute | solution.py:207
  138.0 4.7 %collective-permute-start.14 = (bf16[192,768]{1,0:T(8,128)(2,1)S(1)}, bf16[192,768]{1,0:T(8,128)(2,1)S(1)}, u32[]{:S(2)}, u32[]{:S(2)}) collective-permute-start(bf16[192,768]{1,0:T(8,128)(2,1)S(1)} %collective-permute-done.13.refs_1_), channel_id=1, source_target_pairs={{0,16},{8,248},{16,32},{24,8},{32,48},{40,24},{48,64},{56,40},{64,... | collective-permute-start | bytes 884744 | tf_op jit(solution)/shard_map/ppermute | solution.py:209
  148.0 4.6 %collective-permute-start.8 = (bf16[192,768]{1,0:T(8,128)(2,1)S(1)}, bf16[192,768]{1,0:T(8,128)(2,1)S(1)}, u32[]{:S(2)}, u32[]{:S(2)}) collective-permute-start(bf16[192,768]{1,0:T(8,128)(2,1)S(1)} %collective-permute-done.7.refs_0_), channel_id=1, source_target_pairs={{0,16},{8,248},{16,32},{24,8},{32,48},{40,24},{48,64},{56,40},{64,... | collective-permute-start | bytes 884744 | tf_op jit(solution)/shard_map/ppermute | solution.py:207
  152.7 2.2 collective-permute-start.15
  159.6 2.5 %shard_map.56.refs_2_ = f32[400,384]{1,0:T(8,128)S(1)} custom-call(bf16[384,384]{1,0:T(8,128)(2,1)S(1)} %maximum_multiply_fusion.q_ref, bf16[192,768]{1,0:T(8,128)(2,1)S(1)} %collective-permute-done.1.refs_0_, bf16[192,768]{1,0:T(8,128)(2,1)S(1)} %collective-permute-done.9.refs_1_, f32[400,384]{1,0:T(8,128)S(1)} %shard_map.55.refs_2_), custom_call_target="tpu_custom_call" | custom-call | flops 226492416 | bytes 589824 | tf_op jit(solution)/shard_map/pallas_call | solution.py:70
  162.1 3.7 %collective-permute-start.26 = (bf16[192,384]{1,0:T(8,128)(2,1)S(1)}, bf16[192,384]{1,0:T(8,128)(2,1)S(1)}, u32[]{:S(2)}, u32[]{:S(2)}) collective-permute-start(bf16[192,384]{1,0:T(8,128)(2,1)S(1)} %collective-permute-done.25.refs_7_), channel_id=1, source_target_pairs={{0,248},{8,16},{16,8},{24,32},{32,24},{40,48},{48,40},{56,64},{64,... | collective-permute-start | bytes 442376 | tf_op jit(solution)/shard_map/ppermute | solution.py:199
  165.8 2.5 %shard_map.57.refs_2_ = f32[400,384]{1,0:T(8,128)S(1)} custom-call(bf16[384,384]{1,0:T(8,128)(2,1)S(1)} %maximum_multiply_fusion.q_ref, bf16[192,768]{1,0:T(8,128)(2,1)S(1)} %collective-permute-done.2.refs_0_, bf16[192,768]{1,0:T(8,128)(2,1)S(1)} %collective-permute-done.10.refs_1_, f32[400,384]{1,0:T(8,128)S(1)} %shard_map.56.refs_2_), custom_call_target="tpu_custom_call" | custom-call | flops 226492416 | bytes 589824 | tf_op jit(solution)/shard_map/pallas_call | solution.py:70
  168.3 2.5 %shard_map.58.refs_2_ = f32[400,384]{1,0:T(8,128)S(1)} custom-call(bf16[384,384]{1,0:T(8,128)(2,1)S(1)} %maximum_multiply_fusion.q_ref, bf16[192,768]{1,0:T(8,128)(2,1)S(1)} %collective-permute-done.3.refs_0_, bf16[192,768]{1,0:T(8,128)(2,1)S(1)} %collective-permute-done.11.refs_1_, f32[400,384]{1,0:T(8,128)S(1)} %shard_map.57.refs_2_), custom_call_target="tpu_custom_call" | custom-call | flops 226492416 | bytes 589824 | tf_op jit(solution)/shard_map/pallas_call | solution.py:70
  170.8 2.5 %shard_map.59.refs_2_ = f32[400,384]{1,0:T(8,128)S(1)} custom-call(bf16[384,384]{1,0:T(8,128)(2,1)S(1)} %maximum_multiply_fusion.q_ref, bf16[192,768]{1,0:T(8,128)(2,1)S(1)} %collective-permute-done.4.refs_0_, bf16[192,768]{1,0:T(8,128)(2,1)S(1)} %collective-permute-done.12.refs_1_, f32[400,384]{1,0:T(8,128)S(1)} %shard_map.58.refs_2_), custom_call_target="tpu_custom_call" | custom-call | flops 226492416 | bytes 589824 | tf_op jit(solution)/shard_map/pallas_call | solution.py:70
  173.3 2.5 %shard_map.60.refs_2_ = f32[400,384]{1,0:T(8,128)S(1)} custom-call(bf16[384,384]{1,0:T(8,128)(2,1)S(1)} %maximum_multiply_fusion.q_ref, bf16[192,768]{1,0:T(8,128)(2,1)S(1)} %collective-permute-done.5.refs_0_, bf16[192,768]{1,0:T(8,128)(2,1)S(1)} %collective-permute-done.13.refs_1_, f32[400,384]{1,0:T(8,128)S(1)} %shard_map.59.refs_2_), custom_call_target="tpu_custom_call" | custom-call | flops 226492416 | bytes 589824 | tf_op jit(solution)/shard_map/pallas_call | solution.py:70
  175.8 2.5 %shard_map.61.refs_2_ = f32[400,384]{1,0:T(8,128)S(1)} custom-call(bf16[384,384]{1,0:T(8,128)(2,1)S(1)} %maximum_multiply_fusion.q_ref, bf16[192,768]{1,0:T(8,128)(2,1)S(1)} %collective-permute-done.6.refs_0_, bf16[192,768]{1,0:T(8,128)(2,1)S(1)} %collective-permute-done.14.refs_1_, f32[400,384]{1,0:T(8,128)S(1)} %shard_map.60.refs_2_), custom_call_target="tpu_custom_call" | custom-call | flops 226492416 | bytes 589824 | tf_op jit(solution)/shard_map/pallas_call | solution.py:70
  178.3 2.5 %shard_map.62.refs_1_ = f32[400,384]{1,0:T(8,128)S(1)} custom-call(bf16[384,384]{1,0:T(8,128)(2,1)S(1)} %maximum_multiply_fusion.q_ref, bf16[192,768]{1,0:T(8,128)(2,1)S(1)} %collective-permute-done.7.refs_0_, bf16[192,768]{1,0:T(8,128)(2,1)S(1)} %collective-permute-done.15.refs_1_, f32[400,384]{1,0:T(8,128)S(1)} %shard_map.61.refs_2_), custom_call_target="tpu_custom_call" | custom-call | flops 226492416 | bytes 589824 | tf_op jit(solution)/shard_map/pallas_call | solution.py:70
  182.8 2.9 %collective-permute-start.16 = (f32[400,384]{1,0:T(8,128)S(1)}, f32[400,384]{1,0:T(8,128)S(1)}, u32[]{:S(2)}, u32[]{:S(2)}) collective-permute-start(f32[400,384]{1,0:T(8,128)S(1)} %shard_map.63.one_ref), channel_id=1, source_target_pairs={{0,8},{8,0},{16,24},{24,16},{32,40},{40,32},{48,56},{56,48},{64,72... | collective-permute-start | bytes 1843208 | tf_op jit(solution)/shard_map/ppermute | solution.py:211
  190.9 4.8 %collective-permute-done.28.refs_10_ = bf16[192,384]{1,0:T(8,128)(2,1)S(1)} collective-permute-done((bf16[192,384]{1,0:T(8,128)(2,1)S(1)}, bf16[192,384]{1,0:T(8,128)(2,1)S(1)}, u32[]{:S(2)}, u32[]{:S(2)}) %collective-permute-start.28) | collective-permute-done | bytes 147488 | tf_op jit(solution)/shard_map/ppermute | solution.py:199
  195.8 3.0 %collective-permute-start.29 = (bf16[192,384]{1,0:T(8,128)(2,1)S(1)}, bf16[192,384]{1,0:T(8,128)(2,1)S(1)}, u32[]{:S(2)}, u32[]{:S(2)}) collective-permute-start(bf16[192,384]{1,0:T(8,128)(2,1)S(1)} %collective-permute-done.28.refs_10_), channel_id=1, source_target_pairs={{0,8},{8,0},{16,24},{24,16},{32,40},{40,32},{48,56},{56,48},{64,72... | collective-permute-start | bytes 442376 | tf_op jit(solution)/shard_map/ppermute | solution.py:201
  201.8 4.9 %collective-permute-done.30.refs_12_ = bf16[192,384]{1,0:T(8,128)(2,1)} collective-permute-done((bf16[192,384]{1,0:T(8,128)(2,1)S(1)}, bf16[192,384]{1,0:T(8,128)(2,1)}, u32[]{:S(2)}, u32[]{:S(2)}) %collective-permute-start.30) | collective-permute-done | bytes 147488 | tf_op jit(solution)/shard_map/ppermute | solution.py:199
  206.6 2.2 shard_map.64
  208.8 32.8 %all_to_all.11 = bf16[8,24,3072]{2,1,0:T(8,128)(2,1)S(1)} all-to-all(bf16[8,24,3072]{2,1,0:T(8,128)(2,1)S(1)} %bitcast.19), channel_id=1, replica_groups=mesh['group'=2,'blk'=32,'uly'=8] {'uly'}, dimensions={0} | all-to-all | bytes 2359296 | tf_op jit(solution)/shard_map/all_to_all | solution.py:214
  (62 shorter events, 39.1 us)
Async XLA Ops:
  2.0 81.7 %copy-start.1 = (bf16[384,96]{0,1:T(8,128)(2,1)S(1)}, bf16[384,96]{0,1:T(8,128)(2,1)}, u32[]{:S(2)}) copy-start(bf16[384,96]{0,1:T(8,128)(2,1)} %param.8) | copy-start | bytes 221188
  21.1 59.8 %collective-permute-start = (bf16[192,1152]{1,0:T(8,128)(2,1)S(1)}, bf16[192,1152]{1,0:T(8,128)(2,1)S(1)}, u32[]{:S(2)}, u32[]{:S(2)}) collective-permute-start(bf16[192,1152]{1,0:T(8,128)(2,1)S(1)} %bitcast.20), channel_id=1, source_target_pairs={{0,8},{8,0},{16,24},{24,16},{32,40},{40,32},{48,56},{56,48},{64,72... | collective-permute-start | bytes 1327112 | tf_op jit(solution)/shard_map/ppermute | solution.py:186
  60.4 15.5 %collective-permute-start.1 = (bf16[192,768]{1,0:T(8,128)(2,1)S(1)}, bf16[192,768]{1,0:T(8,128)(2,1)S(1)}, u32[]{:S(2)}, u32[]{:S(2)}) collective-permute-start(bf16[192,768]{1,0:T(8,128)(2,1)S(1)} %slice.34.refs_0_), channel_id=1, source_target_pairs={{0,16},{8,248},{16,32},{24,8},{32,48},{40,24},{48,64},{56,40},{64,... | collective-permute-start | bytes 884744 | tf_op jit(solution)/shard_map/ppermute | solution.py:207
  75.8 9.8 %collective-permute-start.2 = (bf16[192,768]{1,0:T(8,128)(2,1)S(1)}, bf16[192,768]{1,0:T(8,128)(2,1)S(1)}, u32[]{:S(2)}, u32[]{:S(2)}) collective-permute-start(bf16[192,768]{1,0:T(8,128)(2,1)S(1)} %collective-permute-done.1.refs_0_), channel_id=1, source_target_pairs={{0,16},{8,248},{16,32},{24,8},{32,48},{40,24},{48,64},{56,40},{64,... | collective-permute-start | bytes 884744 | tf_op jit(solution)/shard_map/ppermute | solution.py:207
  81.7 7.9 %collective-permute-start.9 = (bf16[192,768]{1,0:T(8,128)(2,1)S(1)}, bf16[192,768]{1,0:T(8,128)(2,1)S(1)}, u32[]{:S(2)}, u32[]{:S(2)}) collective-permute-start(bf16[192,768]{1,0:T(8,128)(2,1)S(1)} %slice.35), channel_id=1, source_target_pairs={{0,16},{8,248},{16,32},{24,8},{32,48},{40,24},{48,64},{56,40},{64,... | collective-permute-start | bytes 884744 | tf_op jit(solution)/shard_map/ppermute | solution.py:209
  83.7 9.1 %collective-permute-start.17 = (bf16[96,384]{1,0:T(8,128)(2,1)S(1)}, bf16[96,384]{1,0:T(8,128)(2,1)S(1)}, u32[]{:S(2)}, u32[]{:S(2)}) collective-permute-start(bf16[96,384]{1,0:T(8,128)(2,1)S(1)} %bitcast.27), channel_id=1, source_target_pairs={{0,8},{8,0},{16,24},{24,16},{32,40},{40,32},{48,56},{56,48},{64,72... | collective-permute-start | bytes 221192 | tf_op jit(solution)/shard_map/ppermute | solution.py:181
  85.6 9.1 %collective-permute-start.3 = (bf16[192,768]{1,0:T(8,128)(2,1)S(1)}, bf16[192,768]{1,0:T(8,128)(2,1)S(1)}, u32[]{:S(2)}, u32[]{:S(2)}) collective-permute-start(bf16[192,768]{1,0:T(8,128)(2,1)S(1)} %collective-permute-done.2.refs_0_), channel_id=1, source_target_pairs={{0,16},{8,248},{16,32},{24,8},{32,48},{40,24},{48,64},{56,40},{64,... | collective-permute-start | bytes 884744 | tf_op jit(solution)/shard_map/ppermute | solution.py:207
  89.6 9.1 %collective-permute-start.10 = (bf16[192,768]{1,0:T(8,128)(2,1)S(1)}, bf16[192,768]{1,0:T(8,128)(2,1)S(1)}, u32[]{:S(2)}, u32[]{:S(2)}) collective-permute-start(bf16[192,768]{1,0:T(8,128)(2,1)S(1)} %collective-permute-done.9.refs_1_), channel_id=1, source_target_pairs={{0,16},{8,248},{16,32},{24,8},{32,48},{40,24},{48,64},{56,40},{64,... | collective-permute-start | bytes 884744 | tf_op jit(solution)/shard_map/ppermute | solution.py:209
  92.8 9.5 %collective-permute-start.18 = (bf16[192,384]{1,0:T(8,128)(2,1)S(1)}, bf16[192,384]{1,0:T(8,128)(2,1)S(1)}, u32[]{:S(2)}, u32[]{:S(2)}) collective-permute-start(bf16[192,384]{1,0:T(8,128)(2,1)S(1)} %pad_maximum_fusion.1.self_ref), channel_id=1, source_target_pairs={{0,248},{8,16},{16,8},{24,32},{32,24},{40,48},{48,40},{56,64},{64,... | collective-permute-start | bytes 442376 | tf_op jit(solution)/shard_map/ppermute | solution.py:199
  94.8 13.7 %collective-permute-start.4 = (bf16[192,768]{1,0:T(8,128)(2,1)S(1)}, bf16[192,768]{1,0:T(8,128)(2,1)S(1)}, u32[]{:S(2)}, u32[]{:S(2)}) collective-permute-start(bf16[192,768]{1,0:T(8,128)(2,1)S(1)} %collective-permute-done.3.refs_0_), channel_id=1, source_target_pairs={{0,16},{8,248},{16,32},{24,8},{32,48},{40,24},{48,64},{56,40},{64,... | collective-permute-start | bytes 884744 | tf_op jit(solution)/shard_map/ppermute | solution.py:207
  98.7 14.7 %collective-permute-start.11 = (bf16[192,768]{1,0:T(8,128)(2,1)S(1)}, bf16[192,768]{1,0:T(8,128)(2,1)S(1)}, u32[]{:S(2)}, u32[]{:S(2)}) collective-permute-start(bf16[192,768]{1,0:T(8,128)(2,1)S(1)} %collective-permute-done.10.refs_1_), channel_id=1, source_target_pairs={{0,16},{8,248},{16,32},{24,8},{32,48},{40,24},{48,64},{56,40},{64,... | collective-permute-start | bytes 884744 | tf_op jit(solution)/shard_map/ppermute | solution.py:209
  102.4 4.1 %collective-permute-start.19 = (bf16[192,384]{1,0:T(8,128)(2,1)S(1)}, bf16[192,384]{1,0:T(8,128)(2,1)S(1)}, u32[]{:S(2)}, u32[]{:S(2)}) collective-permute-start(bf16[192,384]{1,0:T(8,128)(2,1)S(1)} %collective-permute-done.18.refs_0_), channel_id=1, source_target_pairs={{0,8},{8,0},{16,24},{24,16},{32,40},{40,32},{48,56},{56,48},{64,72... | collective-permute-start | bytes 442376 | tf_op jit(solution)/shard_map/ppermute | solution.py:201
  106.5 14.7 %collective-permute-start.20 = (bf16[384,384]{1,0:T(8,128)(2,1)S(1)}, bf16[384,384]{1,0:T(8,128)(2,1)S(1)}, u32[]{:S(2)}, u32[]{:S(2)}) collective-permute-start(bf16[384,384]{1,0:T(8,128)(2,1)S(1)} %pad_maximum_fusion), channel_id=1, source_target_pairs={{0,232},{8,32},{16,248},{24,48},{32,8},{40,64},{48,24},{56,80},{64... | collective-permute-start | bytes 884744 | tf_op jit(solution)/shard_map/ppermute | solution.py:199
  108.5 14.7 %collective-permute-start.5 = (bf16[192,768]{1,0:T(8,128)(2,1)S(1)}, bf16[192,768]{1,0:T(8,128)(2,1)S(1)}, u32[]{:S(2)}, u32[]{:S(2)}) collective-permute-start(bf16[192,768]{1,0:T(8,128)(2,1)S(1)} %collective-permute-done.4.refs_0_), channel_id=1, source_target_pairs={{0,16},{8,248},{16,32},{24,8},{32,48},{40,24},{48,64},{56,40},{64,... | collective-permute-start | bytes 884744 | tf_op jit(solution)/shard_map/ppermute | solution.py:207
  113.4 15.9 %collective-permute-start.12 = (bf16[192,768]{1,0:T(8,128)(2,1)S(1)}, bf16[192,768]{1,0:T(8,128)(2,1)S(1)}, u32[]{:S(2)}, u32[]{:S(2)}) collective-permute-start(bf16[192,768]{1,0:T(8,128)(2,1)S(1)} %collective-permute-done.11.refs_1_), channel_id=1, source_target_pairs={{0,16},{8,248},{16,32},{24,8},{32,48},{40,24},{48,64},{56,40},{64,... | collective-permute-start | bytes 884744 | tf_op jit(solution)/shard_map/ppermute | solution.py:209
  121.2 10.0 %collective-permute-start.21 = (bf16[384,384]{1,0:T(8,128)(2,1)S(1)}, bf16[384,384]{1,0:T(8,128)(2,1)S(1)}, u32[]{:S(2)}, u32[]{:S(2)}) collective-permute-start(bf16[384,384]{1,0:T(8,128)(2,1)S(1)} %collective-permute-done.20.refs_2_), channel_id=1, source_target_pairs={{0,8},{8,0},{16,24},{24,16},{32,40},{40,32},{48,56},{56,48},{64,72... | collective-permute-start | bytes 884744 | tf_op jit(solution)/shard_map/ppermute | solution.py:201
  123.2 10.1 %collective-permute-start.6 = (bf16[192,768]{1,0:T(8,128)(2,1)S(1)}, bf16[192,768]{1,0:T(8,128)(2,1)S(1)}, u32[]{:S(2)}, u32[]{:S(2)}) collective-permute-start(bf16[192,768]{1,0:T(8,128)(2,1)S(1)} %collective-permute-done.5.refs_0_), channel_id=1, source_target_pairs={{0,16},{8,248},{16,32},{24,8},{32,48},{40,24},{48,64},{56,40},{64,... | collective-permute-start | bytes 884744 | tf_op jit(solution)/shard_map/ppermute | solution.py:207
  129.3 8.7 %collective-permute-start.13 = (bf16[192,768]{1,0:T(8,128)(2,1)S(1)}, bf16[192,768]{1,0:T(8,128)(2,1)S(1)}, u32[]{:S(2)}, u32[]{:S(2)}) collective-permute-start(bf16[192,768]{1,0:T(8,128)(2,1)S(1)} %collective-permute-done.12.refs_1_), channel_id=1, source_target_pairs={{0,16},{8,248},{16,32},{24,8},{32,48},{40,24},{48,64},{56,40},{64,... | collective-permute-start | bytes 884744 | tf_op jit(solution)/shard_map/ppermute | solution.py:209
  131.3 11.4 %collective-permute-start.22 = (bf16[192,384]{1,0:T(8,128)(2,1)S(1)}, bf16[192,384]{1,0:T(8,128)(2,1)S(1)}, u32[]{:S(2)}, u32[]{:S(2)}) collective-permute-start(bf16[192,384]{1,0:T(8,128)(2,1)S(1)} %slice.36), channel_id=1, source_target_pairs={{0,248},{8,16},{16,8},{24,32},{32,24},{40,48},{48,40},{56,64},{64,... | collective-permute-start | bytes 442376 | tf_op jit(solution)/shard_map/ppermute | solution.py:199
  133.3 14.7 %collective-permute-start.7 = (bf16[192,768]{1,0:T(8,128)(2,1)S(1)}, bf16[192,768]{1,0:T(8,128)(2,1)S(1)}, u32[]{:S(2)}, u32[]{:S(2)}) collective-permute-start(bf16[192,768]{1,0:T(8,128)(2,1)S(1)} %collective-permute-done.6.refs_0_), channel_id=1, source_target_pairs={{0,16},{8,248},{16,32},{24,8},{32,48},{40,24},{48,64},{56,40},{64,... | collective-permute-start | bytes 884744 | tf_op jit(solution)/shard_map/ppermute | solution.py:207
  138.0 14.6 %collective-permute-start.14 = (bf16[192,768]{1,0:T(8,128)(2,1)S(1)}, bf16[192,768]{1,0:T(8,128)(2,1)S(1)}, u32[]{:S(2)}, u32[]{:S(2)}) collective-permute-start(bf16[192,768]{1,0:T(8,128)(2,1)S(1)} %collective-permute-done.13.refs_1_), channel_id=1, source_target_pairs={{0,16},{8,248},{16,32},{24,8},{32,48},{40,24},{48,64},{56,40},{64,... | collective-permute-start | bytes 884744 | tf_op jit(solution)/shard_map/ppermute | solution.py:209
  142.8 3.3 %collective-permute-start.23 = (bf16[192,384]{1,0:T(8,128)(2,1)S(1)}, bf16[192,384]{1,0:T(8,128)(2,1)S(1)}, u32[]{:S(2)}, u32[]{:S(2)}) collective-permute-start(bf16[192,384]{1,0:T(8,128)(2,1)S(1)} %collective-permute-done.22.refs_4_), channel_id=1, source_target_pairs={{0,8},{8,0},{16,24},{24,16},{32,40},{40,32},{48,56},{56,48},{64,72... | collective-permute-start | bytes 442376 | tf_op jit(solution)/shard_map/ppermute | solution.py:201
  146.0 9.8 %collective-permute-start.24 = (bf16[192,384]{1,0:T(8,128)(2,1)S(1)}, bf16[192,384]{1,0:T(8,128)(2,1)S(1)}, u32[]{:S(2)}, u32[]{:S(2)}) collective-permute-start(bf16[192,384]{1,0:T(8,128)(2,1)S(1)} %collective-permute-done.23.refs_5_), channel_id=1, source_target_pairs={{0,248},{8,16},{16,8},{24,32},{32,24},{40,48},{48,40},{56,64},{64,... | collective-permute-start | bytes 442376 | tf_op jit(solution)/shard_map/ppermute | solution.py:199
  148.0 32.8 %collective-permute-start.8 = (bf16[192,768]{1,0:T(8,128)(2,1)S(1)}, bf16[192,768]{1,0:T(8,128)(2,1)S(1)}, u32[]{:S(2)}, u32[]{:S(2)}) collective-permute-start(bf16[192,768]{1,0:T(8,128)(2,1)S(1)} %collective-permute-done.7.refs_0_), channel_id=1, source_target_pairs={{0,16},{8,248},{16,32},{24,8},{32,48},{40,24},{48,64},{56,40},{64,... | collective-permute-start | bytes 884744 | tf_op jit(solution)/shard_map/ppermute | solution.py:207
  152.7 25.7 %collective-permute-start.15 = (bf16[192,768]{1,0:T(8,128)(2,1)S(1)}, bf16[192,768]{1,0:T(8,128)(2,1)S(1)}, u32[]{:S(2)}, u32[]{:S(2)}) collective-permute-start(bf16[192,768]{1,0:T(8,128)(2,1)S(1)} %collective-permute-done.14.refs_1_), channel_id=1, source_target_pairs={{0,16},{8,248},{16,32},{24,8},{32,48},{40,24},{48,64},{56,40},{64,... | collective-permute-start | bytes 884744 | tf_op jit(solution)/shard_map/ppermute | solution.py:209
  155.9 6.3 %collective-permute-start.25 = (bf16[192,384]{1,0:T(8,128)(2,1)S(1)}, bf16[192,384]{1,0:T(8,128)(2,1)S(1)}, u32[]{:S(2)}, u32[]{:S(2)}) collective-permute-start(bf16[192,384]{1,0:T(8,128)(2,1)S(1)} %collective-permute-done.24.refs_6_), channel_id=1, source_target_pairs={{0,8},{8,0},{16,24},{24,16},{32,40},{40,32},{48,56},{56,48},{64,72... | collective-permute-start | bytes 442376 | tf_op jit(solution)/shard_map/ppermute | solution.py:201
  162.1 23.5 %collective-permute-start.26 = (bf16[192,384]{1,0:T(8,128)(2,1)S(1)}, bf16[192,384]{1,0:T(8,128)(2,1)S(1)}, u32[]{:S(2)}, u32[]{:S(2)}) collective-permute-start(bf16[192,384]{1,0:T(8,128)(2,1)S(1)} %collective-permute-done.25.refs_7_), channel_id=1, source_target_pairs={{0,248},{8,16},{16,8},{24,32},{32,24},{40,48},{48,40},{56,64},{64,... | collective-permute-start | bytes 442376 | tf_op jit(solution)/shard_map/ppermute | solution.py:199
  182.8 23.8 %collective-permute-start.16 = (f32[400,384]{1,0:T(8,128)S(1)}, f32[400,384]{1,0:T(8,128)S(1)}, u32[]{:S(2)}, u32[]{:S(2)}) collective-permute-start(f32[400,384]{1,0:T(8,128)S(1)} %shard_map.63.one_ref), channel_id=1, source_target_pairs={{0,8},{8,0},{16,24},{24,16},{32,40},{40,32},{48,56},{56,48},{64,72... | collective-permute-start | bytes 1843208 | tf_op jit(solution)/shard_map/ppermute | solution.py:211
  185.7 3.3 %collective-permute-start.27 = (bf16[192,384]{1,0:T(8,128)(2,1)S(1)}, bf16[192,384]{1,0:T(8,128)(2,1)S(1)}, u32[]{:S(2)}, u32[]{:S(2)}) collective-permute-start(bf16[192,384]{1,0:T(8,128)(2,1)S(1)} %collective-permute-done.26.refs_8_), channel_id=1, source_target_pairs={{0,8},{8,0},{16,24},{24,16},{32,40},{40,32},{48,56},{56,48},{64,72... | collective-permute-start | bytes 442376 | tf_op jit(solution)/shard_map/ppermute | solution.py:201
  189.0 6.8 %collective-permute-start.28 = (bf16[192,384]{1,0:T(8,128)(2,1)S(1)}, bf16[192,384]{1,0:T(8,128)(2,1)S(1)}, u32[]{:S(2)}, u32[]{:S(2)}) collective-permute-start(bf16[192,384]{1,0:T(8,128)(2,1)S(1)} %collective-permute-done.27.refs_9_), channel_id=1, source_target_pairs={{0,248},{8,16},{16,8},{24,32},{32,24},{40,48},{48,40},{56,64},{64,... | collective-permute-start | bytes 442376 | tf_op jit(solution)/shard_map/ppermute | solution.py:199
  195.8 4.0 %collective-permute-start.29 = (bf16[192,384]{1,0:T(8,128)(2,1)S(1)}, bf16[192,384]{1,0:T(8,128)(2,1)S(1)}, u32[]{:S(2)}, u32[]{:S(2)}) collective-permute-start(bf16[192,384]{1,0:T(8,128)(2,1)S(1)} %collective-permute-done.28.refs_10_), channel_id=1, source_target_pairs={{0,8},{8,0},{16,24},{24,16},{32,40},{40,32},{48,56},{56,48},{64,72... | collective-permute-start | bytes 442376 | tf_op jit(solution)/shard_map/ppermute | solution.py:201
  199.7 6.9 %collective-permute-start.30 = (bf16[192,384]{1,0:T(8,128)(2,1)S(1)}, bf16[192,384]{1,0:T(8,128)(2,1)}, u32[]{:S(2)}, u32[]{:S(2)}) collective-permute-start(bf16[192,384]{1,0:T(8,128)(2,1)S(1)} %collective-permute-done.29.refs_11_), channel_id=1, source_target_pairs={{0,248},{8,16},{16,8},{24,32},{32,24},{40,48},{48,40},{56,64},{64,... | collective-permute-start | bytes 442376 | tf_op jit(solution)/shard_map/ppermute | solution.py:199
  (2 other events, 1.5 us)

commit v5 on v0

--- a/solution.py
+++ b/solution.py
@@ -81,8 +81,7 @@
     )(*operands)
 
 
-def merge_kernel(one_ref, two_ref, out_ref):
-    features = out_ref.shape[1]
+def merged(one_ref, two_ref, features):
     heads = features // HEAD
     max_rows, den_rows = (slice(features + i, features + i + heads) for i in (0, STATS))
     one_max, two_max = one_ref[max_rows, :], two_ref[max_rows, :]
@@ -94,70 +93,72 @@
     for head in range(heads):
         rows, row = slice(head * HEAD, (head + 1) * HEAD), slice(head, head + 1)
         parts.append(one_ref[rows, :] * one[row, :] + two_ref[rows, :] * two[row, :])
-    out_ref[...] = jnp.concatenate(parts, axis=0).astype(out_ref.dtype).T
+    return jnp.concatenate(parts, axis=0).astype(jnp.bfloat16).T
 
 
-def merge(one, two, features):
+def project_kernel(core_ref, one_ref, two_ref, weight_ref, out_ref, attended):
+    rows, width = out_ref.shape
+    attended[...] = merged(one_ref, two_ref, attended.shape[1])
+    mine = attended[pl.ds(pl.multiple_of(core_ref[0] * rows, 16), rows), :]
+    chunk = width // 4
+    for i in range(4):
+        part = slice(i * chunk, (i + 1) * chunk)
+        out_ref[:, part] = nt_dot(mine, weight_ref[part, :]).astype(out_ref.dtype)
+
+
+def project(core, one, two, weight):
+    row_count = one.shape[1]
+    width, features = weight.shape
     vmem = pl.BlockSpec(memory_space=pltpu.VMEM)
     return pl.pallas_call(
-        merge_kernel,
-        out_shape=jax.ShapeDtypeStruct((one.shape[1], features), jnp.bfloat16),
-        in_specs=[vmem] * 2,
+        project_kernel,
+        out_shape=jax.ShapeDtypeStruct((row_count // 2, width), jnp.bfloat16),
+        in_specs=[pl.BlockSpec(memory_space=pltpu.SMEM)] + [vmem] * 3,
         out_specs=vmem,
+        scratch_shapes=[pltpu.VMEM((row_count, features), jnp.bfloat16)],
         compiler_params=pltpu.CompilerParams(vmem_limit_bytes=VMEM_LIMIT),
-    )(one, two)
+    )(core[None], one, two, weight)
 
 
 def on_device(query, keys, values, out_weight, out_gain):
     tokens, width = query.shape
     blk, uly = lax.axis_size("blk"), lax.axis_size("uly")
-    depth, quad = blk // 2, uly // 2
+    depth = blk // 2
+    last = depth // 2
     features = width // uly
     rows = tokens * uly
-    core = lax.axis_index("blk") % 2
-    side = lax.axis_index("uly") // quad
+    core = lax.rem(lax.axis_index("blk").astype(jnp.int32), 2)
     swap = [(i, i ^ 1) for i in range(blk)]
     ring = [
         (2 * z + c, 2 * ((z + (1 if c == 0 else -1)) % depth) + c)
         for z in range(depth)
         for c in range(2)
     ]
-    across = [(i, (i + quad) % uly) for i in range(uly)]
-    quads = [[h * quad + i for i in range(quad)] for h in range(2)]
 
-    far_weight = lax.ppermute(out_weight, "uly", across)
-    both = jnp.concatenate([out_weight, far_weight], axis=0)
-    weight = lax.all_gather(both, "blk", axis=1, tiled=True)
+    def by_core(own, other):
+        return jnp.concatenate(
+            [jnp.where(core == 0, own, other), jnp.where(core == 0, other, own)], axis=0
+        )
+
+    weight = lax.all_gather(out_weight, "blk", axis=1, tiled=True).T
 
     cut = [a.reshape(tokens, uly, features) for a in (query, keys, values)]
     packed = jnp.concatenate(cut, axis=2).transpose(1, 0, 2)
     own = lax.all_to_all(packed, "uly", 0, 0, tiled=True).reshape(rows, 3 * features)
     other = lax.ppermute(own, "blk", swap)
-    q_own, q_other = own[:, :features], other[:, :features]
-    q_all = jnp.concatenate(
-        [jnp.where(core == 0, q_own, q_other), jnp.where(core == 0, q_other, q_own)], axis=0
-    ) * jnp.bfloat16(1.0 / math.sqrt(HEAD))
+    q_all = by_core(own[:, :features], other[:, :features])
+    q_all = q_all * jnp.bfloat16(1.0 / math.sqrt(HEAD))
 
     a, b = own[:, features:], other[:, features:]
     state = fold(q_all, (a,), None)
-    last = depth // 2
     for step in range(1, last + 1):
         a = lax.ppermute(a, "blk", ring)
         if step < last:
             b = lax.ppermute(b, "blk", ring)
         state = fold(q_all, (a, b) if step < last else (a,), state)
     theirs = lax.ppermute(state, "blk", swap)
-    attended = merge(state, theirs, features)
-
-    half = quad * tokens
-    near = lax.dynamic_slice_in_dim(attended, core * rows + side * half, half, axis=0)
-    far = lax.dynamic_slice_in_dim(attended, core * rows + (1 - side) * half, half, axis=0)
-    far = lax.ppermute(far, "uly", across)
-    joined = jnp.concatenate([near, far], axis=1)
-    partial = jnp.dot(joined, weight, preferred_element_type=jnp.float32).astype(jnp.bfloat16)
-    blocks = lax.all_to_all(
-        partial.reshape(quad, tokens, width), "uly", 0, 0, tiled=True, axis_index_groups=quads
-    )
+    partial = project(core, state, theirs, weight)
+    blocks = lax.all_to_all(partial.reshape(uly, tokens, width), "uly", 0, 0, tiled=True)
     summed = jnp.sum(blocks.astype(jnp.float32), axis=0)
     return (out_gain * summed).astype(jnp.bfloat16)
 

time: 238 us -> 227 us (0.954)
  blocking collectives: 39.5 us -> 53.4 us
  starting transfers between devices: 132 us -> 119 us
  waiting for transfers between devices: 19.5 us -> 9.67 us
  matrix products: 3.89 us -> 0 us
    all_to_all x1, blocking collectives: 20.4 us -> 34.4 us  [on_device(): lax.all_to_all(partial.reshape(uly, tokens, width), 'uly', 0, 0, tiled=True)]
    ppermute x2 -> x0, starting transfers between devices: 13.5 us -> none  [the longest x1 8.49 us: on_device(): far_weight = lax.ppermute(out_weight, 'uly', across)]
    ppermute x2 -> x0, waiting for transfers between devices: 6.19 us -> none  [the longest x1 4.15 us: on_device(): far = lax.ppermute(far, 'uly', across)]
    dot_general x1 -> x0, matrix products: 3.89 us -> none  [on_device(): jnp.dot(joined, weight, preferred_element_type=jnp.float32)]
    ppermute x8, waiting for transfers between devices: 10.6 us -> 7.25 us  [on_device(): a = lax.ppermute(a, 'blk', ring)]
  transfers between devices with their start and end apart: 20 -> 18, of which waited for: 7 -> 4; matrix products, arithmetic and copies ran while one was open for 1% -> 1% of each run, Pallas kernels for 10% -> 10%
where the time goes in v5:
time: 227 us; the launch traced here: 226 us
  starting transfers between devices  119 us (52%)
  blocking collectives  53.4 us (24%)
  Pallas kernels  24.1 us (11%)
  between operations  13.8 us (6%)
  waiting for transfers between devices  9.67 us (4%)
  local copies, waits for them, and re-layouts  4.21 us (2%)
    ppermute x8, starting transfers between devices, on_device(): a = lax.ppermute(a, 'blk', ring)  46.3 us
    ppermute x1, starting transfers between devices, on_device(): other = lax.ppermute(own, 'blk', swap)  39.3 us
    all_to_all x1, blocking collectives, on_device(): lax.all_to_all(partial.reshape(uly, tokens, width), 'uly', 0, 0, tiled=True)  34.4 us
    ppermute x7, starting transfers between devices, on_device(): b = lax.ppermute(b, 'blk', ring)  27.9 us
    pallas_call x9, Pallas kernels, fold(): pl.pallas_call(functools.partial(fold_kernel, state is None), out_shape=j...  23 us
    all_to_all x1, blocking collectives, on_device(): lax.all_to_all(packed, 'uly', 0, 0, tiled=True).reshape(rows, 3 * features)  18.9 us
    ppermute x8, waiting for transfers between devices, on_device(): a = lax.ppermute(a, 'blk', ring)  7.25 us
    ppermute x1, starting transfers between devices, on_device(): theirs = lax.ppermute(state, 'blk', swap)  5.7 us
  transfers between devices with their start and end apart: 18, of which 4 were waited for; matrix products, arithmetic and copies ran while one was open for 1% of the time, Pallas kernels for 10%

profile of v5, /device:TPU:65, one launch (start us, length us, event | category | flops | bytes accessed | tf_op | source)
XLA Modules:
  0.0 226.2 jit_solution(9960256078681888521)
XLA Ops:
  9.3 18.9 %all_to_all.10 = bf16[8,24,1152]{2,1,0:T(8,128)(2,1)S(1)} all-to-all(bf16[8,24,1152]{2,1,0:T(8,128)(2,1)S(1)} %maximum_bitcast_fusion), channel_id=1, replica_groups=mesh['group'=2,'blk'=32,'uly'=8] {'uly'}, dimensions={0} | all-to-all | bytes 884736 | tf_op jit(solution)/shard_map/all_to_all | solution.py:147
  28.2 39.3 %collective-permute-start = (bf16[192,1152]{1,0:T(8,128)(2,1)S(1)}, bf16[192,1152]{1,0:T(8,128)(2,1)S(1)}, u32[]{:S(2)}, u32[]{:S(2)}) collective-permute-start(bf16[192,1152]{1,0:T(8,128)(2,1)S(1)} %bitcast.18), channel_id=1, source_target_pairs={{0,8},{8,0},{16,24},{24,16},{32,40},{40,32},{48,56},{56,48},{64,72... | collective-permute-start | bytes 1327112 | tf_op jit(solution)/shard_map/ppermute | solution.py:148
  67.5 11.8 %collective-permute-start.1 = (bf16[192,768]{1,0:T(8,128)(2,1)S(1)}, bf16[192,768]{1,0:T(8,128)(2,1)S(1)}, u32[]{:S(2)}, u32[]{:S(2)}) collective-permute-start(bf16[192,768]{1,0:T(8,128)(2,1)S(1)} %slice.18.refs_0_), channel_id=1, source_target_pairs={{0,16},{8,248},{16,32},{24,8},{32,48},{40,24},{48,64},{56,40},{64,... | collective-permute-start | bytes 884744 | tf_op jit(solution)/shard_map/ppermute | solution.py:155
  79.4 4.5 %collective-permute-done.1.refs_0_ = bf16[192,768]{1,0:T(8,128)(2,1)S(1)} collective-permute-done((bf16[192,768]{1,0:T(8,128)(2,1)S(1)}, bf16[192,768]{1,0:T(8,128)(2,1)S(1)}, u32[]{:S(2)}, u32[]{:S(2)}) %collective-permute-start.1) | collective-permute-done | bytes 294944 | tf_op jit(solution)/shard_map/ppermute | solution.py:155
  83.9 5.6 %collective-permute-start.2 = (bf16[192,768]{1,0:T(8,128)(2,1)S(1)}, bf16[192,768]{1,0:T(8,128)(2,1)S(1)}, u32[]{:S(2)}, u32[]{:S(2)}) collective-permute-start(bf16[192,768]{1,0:T(8,128)(2,1)S(1)} %collective-permute-done.1.refs_0_), channel_id=1, source_target_pairs={{0,16},{8,248},{16,32},{24,8},{32,48},{40,24},{48,64},{56,40},{64,... | collective-permute-start | bytes 884744 | tf_op jit(solution)/shard_map/ppermute | solution.py:155
  89.6 2.0 collective-permute-start.9
  91.5 2.5 %collective-permute-done.2.refs_0_ = bf16[192,768]{1,0:T(8,128)(2,1)S(1)} collective-permute-done((bf16[192,768]{1,0:T(8,128)(2,1)S(1)}, bf16[192,768]{1,0:T(8,128)(2,1)S(1)}, u32[]{:S(2)}, u32[]{:S(2)}) %collective-permute-start.2) | collective-permute-done | bytes 294944 | tf_op jit(solution)/shard_map/ppermute | solution.py:155
  94.0 5.1 %collective-permute-start.3 = (bf16[192,768]{1,0:T(8,128)(2,1)S(1)}, bf16[192,768]{1,0:T(8,128)(2,1)S(1)}, u32[]{:S(2)}, u32[]{:S(2)}) collective-permute-start(bf16[192,768]{1,0:T(8,128)(2,1)S(1)} %collective-permute-done.2.refs_0_), channel_id=1, source_target_pairs={{0,16},{8,248},{16,32},{24,8},{32,48},{40,24},{48,64},{56,40},{64,... | collective-permute-start | bytes 884744 | tf_op jit(solution)/shard_map/ppermute | solution.py:155
  99.1 4.5 %collective-permute-start.10 = (bf16[192,768]{1,0:T(8,128)(2,1)S(1)}, bf16[192,768]{1,0:T(8,128)(2,1)S(1)}, u32[]{:S(2)}, u32[]{:S(2)}) collective-permute-start(bf16[192,768]{1,0:T(8,128)(2,1)S(1)} %collective-permute-done.9.refs_1_), channel_id=1, source_target_pairs={{0,16},{8,248},{16,32},{24,8},{32,48},{40,24},{48,64},{56,40},{64,... | collective-permute-start | bytes 884744 | tf_op jit(solution)/shard_map/ppermute | solution.py:157
  103.9 5.0 %collective-permute-start.4 = (bf16[192,768]{1,0:T(8,128)(2,1)S(1)}, bf16[192,768]{1,0:T(8,128)(2,1)S(1)}, u32[]{:S(2)}, u32[]{:S(2)}) collective-permute-start(bf16[192,768]{1,0:T(8,128)(2,1)S(1)} %collective-permute-done.3.refs_0_), channel_id=1, source_target_pairs={{0,16},{8,248},{16,32},{24,8},{32,48},{40,24},{48,64},{56,40},{64,... | collective-permute-start | bytes 884744 | tf_op jit(solution)/shard_map/ppermute | solution.py:155
  108.9 4.4 %collective-permute-start.11 = (bf16[192,768]{1,0:T(8,128)(2,1)S(1)}, bf16[192,768]{1,0:T(8,128)(2,1)S(1)}, u32[]{:S(2)}, u32[]{:S(2)}) collective-permute-start(bf16[192,768]{1,0:T(8,128)(2,1)S(1)} %collective-permute-done.10.refs_1_), channel_id=1, source_target_pairs={{0,16},{8,248},{16,32},{24,8},{32,48},{40,24},{48,64},{56,40},{64,... | collective-permute-start | bytes 884744 | tf_op jit(solution)/shard_map/ppermute | solution.py:157
  113.4 5.0 %collective-permute-start.5 = (bf16[192,768]{1,0:T(8,128)(2,1)S(1)}, bf16[192,768]{1,0:T(8,128)(2,1)S(1)}, u32[]{:S(2)}, u32[]{:S(2)}) collective-permute-start(bf16[192,768]{1,0:T(8,128)(2,1)S(1)} %collective-permute-done.4.refs_0_), channel_id=1, source_target_pairs={{0,16},{8,248},{16,32},{24,8},{32,48},{40,24},{48,64},{56,40},{64,... | collective-permute-start | bytes 884744 | tf_op jit(solution)/shard_map/ppermute | solution.py:155
  118.4 4.1 %collective-permute-start.12 = (bf16[192,768]{1,0:T(8,128)(2,1)S(1)}, bf16[192,768]{1,0:T(8,128)(2,1)S(1)}, u32[]{:S(2)}, u32[]{:S(2)}) collective-permute-start(bf16[192,768]{1,0:T(8,128)(2,1)S(1)} %collective-permute-done.11.refs_1_), channel_id=1, source_target_pairs={{0,16},{8,248},{16,32},{24,8},{32,48},{40,24},{48,64},{56,40},{64,... | collective-permute-start | bytes 884744 | tf_op jit(solution)/shard_map/ppermute | solution.py:157
  122.5 4.6 %collective-permute-start.6 = (bf16[192,768]{1,0:T(8,128)(2,1)S(1)}, bf16[192,768]{1,0:T(8,128)(2,1)S(1)}, u32[]{:S(2)}, u32[]{:S(2)}) collective-permute-start(bf16[192,768]{1,0:T(8,128)(2,1)S(1)} %collective-permute-done.5.refs_0_), channel_id=1, source_target_pairs={{0,16},{8,248},{16,32},{24,8},{32,48},{40,24},{48,64},{56,40},{64,... | collective-permute-start | bytes 884744 | tf_op jit(solution)/shard_map/ppermute | solution.py:155
  127.1 4.1 %collective-permute-start.13 = (bf16[192,768]{1,0:T(8,128)(2,1)S(1)}, bf16[192,768]{1,0:T(8,128)(2,1)}, u32[]{:S(2)}, u32[]{:S(2)}) collective-permute-start(bf16[192,768]{1,0:T(8,128)(2,1)S(1)} %collective-permute-done.12.refs_1_), channel_id=1, source_target_pairs={{0,16},{8,248},{16,32},{24,8},{32,48},{40,24},{48,64},{56,40},{64,... | collective-permute-start | bytes 884744 | tf_op jit(solution)/shard_map/ppermute | solution.py:157
  131.2 4.6 %collective-permute-start.7 = (bf16[192,768]{1,0:T(8,128)(2,1)S(1)}, bf16[192,768]{1,0:T(8,128)(2,1)S(1)}, u32[]{:S(2)}, u32[]{:S(2)}) collective-permute-start(bf16[192,768]{1,0:T(8,128)(2,1)S(1)} %collective-permute-done.6.refs_0_), channel_id=1, source_target_pairs={{0,16},{8,248},{16,32},{24,8},{32,48},{40,24},{48,64},{56,40},{64,... | collective-permute-start | bytes 884744 | tf_op jit(solution)/shard_map/ppermute | solution.py:155
  135.9 4.2 %collective-permute-start.14 = (bf16[192,768]{1,0:T(8,128)(2,1)}, bf16[192,768]{1,0:T(8,128)(2,1)}, u32[]{:S(2)}, u32[]{:S(2)}) collective-permute-start(bf16[192,768]{1,0:T(8,128)(2,1)} %collective-permute-done.13.refs_1_), channel_id=1, source_target_pairs={{0,16},{8,248},{16,32},{24,8},{32,48},{40,24},{48,64},{56,40},{64,... | collective-permute-start | bytes 884744 | tf_op jit(solution)/shard_map/ppermute | solution.py:157
  140.0 4.5 %collective-permute-start.8 = (bf16[192,768]{1,0:T(8,128)(2,1)S(1)}, bf16[192,768]{1,0:T(8,128)(2,1)S(1)}, u32[]{:S(2)}, u32[]{:S(2)}) collective-permute-start(bf16[192,768]{1,0:T(8,128)(2,1)S(1)} %collective-permute-done.7.refs_0_), channel_id=1, source_target_pairs={{0,16},{8,248},{16,32},{24,8},{32,48},{40,24},{48,64},{56,40},{64,... | collective-permute-start | bytes 884744 | tf_op jit(solution)/shard_map/ppermute | solution.py:155
  144.5 4.7 %collective-permute-start.15 = (bf16[192,768]{1,0:T(8,128)(2,1)}, bf16[192,768]{1,0:T(8,128)(2,1)S(1)}, u32[]{:S(2)}, u32[]{:S(2)}) collective-permute-start(bf16[192,768]{1,0:T(8,128)(2,1)} %collective-permute-done.14.refs_1_), channel_id=1, source_target_pairs={{0,16},{8,248},{16,32},{24,8},{32,48},{40,24},{48,64},{56,40},{64,... | collective-permute-start | bytes 884744 | tf_op jit(solution)/shard_map/ppermute | solution.py:157
  150.3 1.7 shard_map.55.refs_2_
  152.0 2.5 %shard_map.56.refs_2_ = f32[400,384]{1,0:T(8,128)S(1)} custom-call(bf16[384,384]{1,0:T(8,128)(2,1)S(1)} %maximum_multiply_fusion.q_ref, bf16[192,768]{1,0:T(8,128)(2,1)S(1)} %collective-permute-done.1.refs_0_, bf16[192,768]{1,0:T(8,128)(2,1)S(1)} %collective-permute-done.9.refs_1_, f32[400,384]{1,0:T(8,128)S(1)} %shard_map.55.refs_2_), custom_call_target="tpu_custom_call" | custom-call | flops 226492416 | bytes 589824 | tf_op jit(solution)/shard_map/pallas_call | solution.py:70
  154.5 2.5 %shard_map.57.refs_2_ = f32[400,384]{1,0:T(8,128)S(1)} custom-call(bf16[384,384]{1,0:T(8,128)(2,1)S(1)} %maximum_multiply_fusion.q_ref, bf16[192,768]{1,0:T(8,128)(2,1)S(1)} %collective-permute-done.2.refs_0_, bf16[192,768]{1,0:T(8,128)(2,1)S(1)} %collective-permute-done.10.refs_1_, f32[400,384]{1,0:T(8,128)S(1)} %shard_map.56.refs_2_), custom_call_target="tpu_custom_call" | custom-call | flops 226492416 | bytes 589824 | tf_op jit(solution)/shard_map/pallas_call | solution.py:70
  157.0 2.5 %shard_map.58.refs_2_ = f32[400,384]{1,0:T(8,128)S(1)} custom-call(bf16[384,384]{1,0:T(8,128)(2,1)S(1)} %maximum_multiply_fusion.q_ref, bf16[192,768]{1,0:T(8,128)(2,1)S(1)} %collective-permute-done.3.refs_0_, bf16[192,768]{1,0:T(8,128)(2,1)S(1)} %collective-permute-done.11.refs_1_, f32[400,384]{1,0:T(8,128)S(1)} %shard_map.57.refs_2_), custom_call_target="tpu_custom_call" | custom-call | flops 226492416 | bytes 589824 | tf_op jit(solution)/shard_map/pallas_call | solution.py:70
  159.5 2.5 %shard_map.59.refs_2_ = f32[400,384]{1,0:T(8,128)S(1)} custom-call(bf16[384,384]{1,0:T(8,128)(2,1)S(1)} %maximum_multiply_fusion.q_ref, bf16[192,768]{1,0:T(8,128)(2,1)S(1)} %collective-permute-done.4.refs_0_, bf16[192,768]{1,0:T(8,128)(2,1)S(1)} %collective-permute-done.12.refs_1_, f32[400,384]{1,0:T(8,128)S(1)} %shard_map.58.refs_2_), custom_call_target="tpu_custom_call" | custom-call | flops 226492416 | bytes 589824 | tf_op jit(solution)/shard_map/pallas_call | solution.py:70
  162.0 3.4 %shard_map.60.refs_2_ = f32[400,384]{1,0:T(8,128)S(1)} custom-call(bf16[384,384]{1,0:T(8,128)(2,1)S(1)} %maximum_multiply_fusion.q_ref, bf16[192,768]{1,0:T(8,128)(2,1)S(1)} %collective-permute-done.5.refs_0_, bf16[192,768]{1,0:T(8,128)(2,1)} %collective-permute-done.13.refs_1_, f32[400,384]{1,0:T(8,128)S(1)} %shard_map.59.refs_2_), custom_call_target="tpu_custom_call" | custom-call | flops 226492416 | bytes 589824 | tf_op jit(solution)/shard_map/pallas_call | solution.py:70
  165.4 3.7 %shard_map.61.refs_2_ = f32[400,384]{1,0:T(8,128)S(1)} custom-call(bf16[384,384]{1,0:T(8,128)(2,1)S(1)} %maximum_multiply_fusion.q_ref, bf16[192,768]{1,0:T(8,128)(2,1)S(1)} %collective-permute-done.6.refs_0_, bf16[192,768]{1,0:T(8,128)(2,1)} %collective-permute-done.14.refs_1_, f32[400,384]{1,0:T(8,128)S(1)} %shard_map.60.refs_2_), custom_call_target="tpu_custom_call" | custom-call | flops 226492416 | bytes 589824 | tf_op jit(solution)/shard_map/pallas_call | solution.py:70
  169.1 2.5 %shard_map.62.refs_1_ = f32[400,384]{1,0:T(8,128)S(1)} custom-call(bf16[384,384]{1,0:T(8,128)(2,1)S(1)} %maximum_multiply_fusion.q_ref, bf16[192,768]{1,0:T(8,128)(2,1)S(1)} %collective-permute-done.7.refs_0_, bf16[192,768]{1,0:T(8,128)(2,1)S(1)} %collective-permute-done.15.refs_1_, f32[400,384]{1,0:T(8,128)S(1)} %shard_map.61.refs_2_), custom_call_target="tpu_custom_call" | custom-call | flops 226492416 | bytes 589824 | tf_op jit(solution)/shard_map/pallas_call | solution.py:70
  171.6 1.8 shard_map.63.one_ref
  173.4 5.7 %collective-permute-start.16 = (f32[400,384]{1,0:T(8,128)S(1)}, f32[400,384]{1,0:T(8,128)S(1)}, u32[]{:S(2)}, u32[]{:S(2)}) collective-permute-start(f32[400,384]{1,0:T(8,128)S(1)} %shard_map.63.one_ref), channel_id=1, source_target_pairs={{0,8},{8,0},{16,24},{24,16},{32,40},{40,32},{48,56},{56,48},{64,72... | collective-permute-start | bytes 1843208 | tf_op jit(solution)/shard_map/ppermute | solution.py:159
  179.1 1.6 collective-permute-done.16.two_ref
  180.7 1.7 copy-done
  183.5 34.4 %all_to_all.11 = bf16[8,24,3072]{2,1,0:T(8,128)(2,1)S(1)} all-to-all(bf16[8,24,3072]{2,1,0:T(8,128)(2,1)S(1)} %bitcast.16), channel_id=1, replica_groups=mesh['group'=2,'blk'=32,'uly'=8] {'uly'}, dimensions={0} | all-to-all | bytes 2359296 | tf_op jit(solution)/shard_map/all_to_all | solution.py:161
  (34 shorter events, 6.5 us)
Async XLA Ops:
  6.5 174.2 %all-gather.2.cloned.1.call-start = ((), (), s32[]{:S(2)}) async-start(), calls=%async_computation.2 | async-start | bytes 2433024 | tf_op jit(solution)/shard_map/all_gather | solution.py:143
  28.2 107.6 %copy-start.1 = (bf16[8,24,1152]{2,1,0:T(8,128)(2,1)}, bf16[8,24,1152]{2,1,0:T(8,128)(2,1)S(1)}, u32[]{:S(2)}) copy-start(bf16[8,24,1152]{2,1,0:T(8,128)(2,1)S(1)} %all_to_all.10) | copy-start | bytes 1327108
  28.2 61.3 %collective-permute-start = (bf16[192,1152]{1,0:T(8,128)(2,1)S(1)}, bf16[192,1152]{1,0:T(8,128)(2,1)S(1)}, u32[]{:S(2)}, u32[]{:S(2)}) collective-permute-start(bf16[192,1152]{1,0:T(8,128)(2,1)S(1)} %bitcast.18), channel_id=1, source_target_pairs={{0,8},{8,0},{16,24},{24,16},{32,40},{40,32},{48,56},{56,48},{64,72... | collective-permute-start | bytes 1327112 | tf_op jit(solution)/shard_map/ppermute | solution.py:148
  67.5 16.4 %collective-permute-start.1 = (bf16[192,768]{1,0:T(8,128)(2,1)S(1)}, bf16[192,768]{1,0:T(8,128)(2,1)S(1)}, u32[]{:S(2)}, u32[]{:S(2)}) collective-permute-start(bf16[192,768]{1,0:T(8,128)(2,1)S(1)} %slice.18.refs_0_), channel_id=1, source_target_pairs={{0,16},{8,248},{16,32},{24,8},{32,48},{40,24},{48,64},{56,40},{64,... | collective-permute-start | bytes 884744 | tf_op jit(solution)/shard_map/ppermute | solution.py:155
  83.9 10.1 %collective-permute-start.2 = (bf16[192,768]{1,0:T(8,128)(2,1)S(1)}, bf16[192,768]{1,0:T(8,128)(2,1)S(1)}, u32[]{:S(2)}, u32[]{:S(2)}) collective-permute-start(bf16[192,768]{1,0:T(8,128)(2,1)S(1)} %collective-permute-done.1.refs_0_), channel_id=1, source_target_pairs={{0,16},{8,248},{16,32},{24,8},{32,48},{40,24},{48,64},{56,40},{64,... | collective-permute-start | bytes 884744 | tf_op jit(solution)/shard_map/ppermute | solution.py:155
  89.5 50.5 %copy-start.2 = (bf16[192,1152]{1,0:T(8,128)(2,1)}, bf16[192,1152]{1,0:T(8,128)(2,1)S(1)}, u32[]{:S(2)}) copy-start(bf16[192,1152]{1,0:T(8,128)(2,1)S(1)} %collective-permute-done) | copy-start | bytes 1327108
  89.6 9.6 %collective-permute-start.9 = (bf16[192,768]{1,0:T(8,128)(2,1)S(1)}, bf16[192,768]{1,0:T(8,128)(2,1)S(1)}, u32[]{:S(2)}, u32[]{:S(2)}) collective-permute-start(bf16[192,768]{1,0:T(8,128)(2,1)S(1)} %slice.19), channel_id=1, source_target_pairs={{0,16},{8,248},{16,32},{24,8},{32,48},{40,24},{48,64},{56,40},{64,... | collective-permute-start | bytes 884744 | tf_op jit(solution)/shard_map/ppermute | solution.py:157
  94.0 9.8 %collective-permute-start.3 = (bf16[192,768]{1,0:T(8,128)(2,1)S(1)}, bf16[192,768]{1,0:T(8,128)(2,1)S(1)}, u32[]{:S(2)}, u32[]{:S(2)}) collective-permute-start(bf16[192,768]{1,0:T(8,128)(2,1)S(1)} %collective-permute-done.2.refs_0_), channel_id=1, source_target_pairs={{0,16},{8,248},{16,32},{24,8},{32,48},{40,24},{48,64},{56,40},{64,... | collective-permute-start | bytes 884744 | tf_op jit(solution)/shard_map/ppermute | solution.py:155
  99.1 9.8 %collective-permute-start.10 = (bf16[192,768]{1,0:T(8,128)(2,1)S(1)}, bf16[192,768]{1,0:T(8,128)(2,1)S(1)}, u32[]{:S(2)}, u32[]{:S(2)}) collective-permute-start(bf16[192,768]{1,0:T(8,128)(2,1)S(1)} %collective-permute-done.9.refs_1_), channel_id=1, source_target_pairs={{0,16},{8,248},{16,32},{24,8},{32,48},{40,24},{48,64},{56,40},{64,... | collective-permute-start | bytes 884744 | tf_op jit(solution)/shard_map/ppermute | solution.py:157
  103.9 9.5 %collective-permute-start.4 = (bf16[192,768]{1,0:T(8,128)(2,1)S(1)}, bf16[192,768]{1,0:T(8,128)(2,1)S(1)}, u32[]{:S(2)}, u32[]{:S(2)}) collective-permute-start(bf16[192,768]{1,0:T(8,128)(2,1)S(1)} %collective-permute-done.3.refs_0_), channel_id=1, source_target_pairs={{0,16},{8,248},{16,32},{24,8},{32,48},{40,24},{48,64},{56,40},{64,... | collective-permute-start | bytes 884744 | tf_op jit(solution)/shard_map/ppermute | solution.py:155
  108.9 9.5 %collective-permute-start.11 = (bf16[192,768]{1,0:T(8,128)(2,1)S(1)}, bf16[192,768]{1,0:T(8,128)(2,1)S(1)}, u32[]{:S(2)}, u32[]{:S(2)}) collective-permute-start(bf16[192,768]{1,0:T(8,128)(2,1)S(1)} %collective-permute-done.10.refs_1_), channel_id=1, source_target_pairs={{0,16},{8,248},{16,32},{24,8},{32,48},{40,24},{48,64},{56,40},{64,... | collective-permute-start | bytes 884744 | tf_op jit(solution)/shard_map/ppermute | solution.py:157
  113.4 9.1 %collective-permute-start.5 = (bf16[192,768]{1,0:T(8,128)(2,1)S(1)}, bf16[192,768]{1,0:T(8,128)(2,1)S(1)}, u32[]{:S(2)}, u32[]{:S(2)}) collective-permute-start(bf16[192,768]{1,0:T(8,128)(2,1)S(1)} %collective-permute-done.4.refs_0_), channel_id=1, source_target_pairs={{0,16},{8,248},{16,32},{24,8},{32,48},{40,24},{48,64},{56,40},{64,... | collective-permute-start | bytes 884744 | tf_op jit(solution)/shard_map/ppermute | solution.py:155
  118.4 8.7 %collective-permute-start.12 = (bf16[192,768]{1,0:T(8,128)(2,1)S(1)}, bf16[192,768]{1,0:T(8,128)(2,1)S(1)}, u32[]{:S(2)}, u32[]{:S(2)}) collective-permute-start(bf16[192,768]{1,0:T(8,128)(2,1)S(1)} %collective-permute-done.11.refs_1_), channel_id=1, source_target_pairs={{0,16},{8,248},{16,32},{24,8},{32,48},{40,24},{48,64},{56,40},{64,... | collective-permute-start | bytes 884744 | tf_op jit(solution)/shard_map/ppermute | solution.py:157
  122.5 8.7 %collective-permute-start.6 = (bf16[192,768]{1,0:T(8,128)(2,1)S(1)}, bf16[192,768]{1,0:T(8,128)(2,1)S(1)}, u32[]{:S(2)}, u32[]{:S(2)}) collective-permute-start(bf16[192,768]{1,0:T(8,128)(2,1)S(1)} %collective-permute-done.5.refs_0_), channel_id=1, source_target_pairs={{0,16},{8,248},{16,32},{24,8},{32,48},{40,24},{48,64},{56,40},{64,... | collective-permute-start | bytes 884744 | tf_op jit(solution)/shard_map/ppermute | solution.py:155
  127.1 8.7 %collective-permute-start.13 = (bf16[192,768]{1,0:T(8,128)(2,1)S(1)}, bf16[192,768]{1,0:T(8,128)(2,1)}, u32[]{:S(2)}, u32[]{:S(2)}) collective-permute-start(bf16[192,768]{1,0:T(8,128)(2,1)S(1)} %collective-permute-done.12.refs_1_), channel_id=1, source_target_pairs={{0,16},{8,248},{16,32},{24,8},{32,48},{40,24},{48,64},{56,40},{64,... | collective-permute-start | bytes 884744 | tf_op jit(solution)/shard_map/ppermute | solution.py:157
  131.2 8.8 %collective-permute-start.7 = (bf16[192,768]{1,0:T(8,128)(2,1)S(1)}, bf16[192,768]{1,0:T(8,128)(2,1)S(1)}, u32[]{:S(2)}, u32[]{:S(2)}) collective-permute-start(bf16[192,768]{1,0:T(8,128)(2,1)S(1)} %collective-permute-done.6.refs_0_), channel_id=1, source_target_pairs={{0,16},{8,248},{16,32},{24,8},{32,48},{40,24},{48,64},{56,40},{64,... | collective-permute-start | bytes 884744 | tf_op jit(solution)/shard_map/ppermute | solution.py:155
  135.9 8.7 %collective-permute-start.14 = (bf16[192,768]{1,0:T(8,128)(2,1)}, bf16[192,768]{1,0:T(8,128)(2,1)}, u32[]{:S(2)}, u32[]{:S(2)}) collective-permute-start(bf16[192,768]{1,0:T(8,128)(2,1)} %collective-permute-done.13.refs_1_), channel_id=1, source_target_pairs={{0,16},{8,248},{16,32},{24,8},{32,48},{40,24},{48,64},{56,40},{64,... | collective-permute-start | bytes 884744 | tf_op jit(solution)/shard_map/ppermute | solution.py:157
  140.0 31.6 %collective-permute-start.8 = (bf16[192,768]{1,0:T(8,128)(2,1)S(1)}, bf16[192,768]{1,0:T(8,128)(2,1)S(1)}, u32[]{:S(2)}, u32[]{:S(2)}) collective-permute-start(bf16[192,768]{1,0:T(8,128)(2,1)S(1)} %collective-permute-done.7.refs_0_), channel_id=1, source_target_pairs={{0,16},{8,248},{16,32},{24,8},{32,48},{40,24},{48,64},{56,40},{64,... | collective-permute-start | bytes 884744 | tf_op jit(solution)/shard_map/ppermute | solution.py:155
  144.5 24.6 %collective-permute-start.15 = (bf16[192,768]{1,0:T(8,128)(2,1)}, bf16[192,768]{1,0:T(8,128)(2,1)S(1)}, u32[]{:S(2)}, u32[]{:S(2)}) collective-permute-start(bf16[192,768]{1,0:T(8,128)(2,1)} %collective-permute-done.14.refs_1_), channel_id=1, source_target_pairs={{0,16},{8,248},{16,32},{24,8},{32,48},{40,24},{48,64},{56,40},{64,... | collective-permute-start | bytes 884744 | tf_op jit(solution)/shard_map/ppermute | solution.py:157
  173.4 7.4 %collective-permute-start.16 = (f32[400,384]{1,0:T(8,128)S(1)}, f32[400,384]{1,0:T(8,128)S(1)}, u32[]{:S(2)}, u32[]{:S(2)}) collective-permute-start(f32[400,384]{1,0:T(8,128)S(1)} %shard_map.63.one_ref), channel_id=1, source_target_pairs={{0,8},{8,0},{16,24},{24,16},{32,40},{40,32},{48,56},{56,48},{64,72... | collective-permute-start | bytes 1843208 | tf_op jit(solution)/shard_map/ppermute | solution.py:159
  180.7 1.7 copy-start
  217.9 0.7 copy-start.3
Sparse Core Ops, SparseCore 0:
  9.5 109.9 all-gather.1

commit v6 on v5

--- a/solution.py
+++ b/solution.py
@@ -13,6 +13,7 @@
 PAIR = 2 * HEAD
 STATS = 8
 VMEM_LIMIT = 16 * 1024 * 1024
+ALL_VMEM = 67043328
 LOG2E = math.log2(math.e)
 
 
@@ -120,6 +121,38 @@
     )(core[None], one, two, weight)
 
 
+def pack_kernel(*refs):
+    count = (len(refs) - 2) // 2
+    in_refs, out_ref, held_refs, sems = refs[:count], refs[count], refs[count + 1 : -1], refs[-1]
+    features = out_ref.shape[2] // count
+    copies = [
+        pltpu.make_async_copy(ref, held, sems.at[i])
+        for i, (ref, held) in enumerate(zip(in_refs, held_refs))
+    ]
+    for copy in copies:
+        copy.start()
+    for i, (copy, held) in enumerate(zip(copies, held_refs)):
+        copy.wait()
+        for to in range(out_ref.shape[0]):
+            out_ref[to, :, i * features : (i + 1) * features] = held[
+                :, to * features : (to + 1) * features
+            ]
+
+
+def pack(arrays, parts):
+    tokens, width = arrays[0].shape
+    count = len(arrays)
+    return pl.pallas_call(
+        pack_kernel,
+        out_shape=jax.ShapeDtypeStruct((parts, tokens, count * (width // parts)), arrays[0].dtype),
+        in_specs=[pl.BlockSpec(memory_space=pltpu.HBM)] * count,
+        out_specs=pl.BlockSpec(memory_space=pltpu.VMEM),
+        scratch_shapes=[pltpu.VMEM(a.shape, a.dtype) for a in arrays]
+        + [pltpu.SemaphoreType.DMA((count,))],
+        compiler_params=pltpu.CompilerParams(vmem_limit_bytes=ALL_VMEM),
+    )(*arrays)
+
+
 def on_device(query, keys, values, out_weight, out_gain):
     tokens, width = query.shape
     blk, uly = lax.axis_size("blk"), lax.axis_size("uly")
@@ -142,8 +175,7 @@
 
     weight = lax.all_gather(out_weight, "blk", axis=1, tiled=True).T
 
-    cut = [a.reshape(tokens, uly, features) for a in (query, keys, values)]
-    packed = jnp.concatenate(cut, axis=2).transpose(1, 0, 2)
+    packed = pack((query, keys, values), uly)
     own = lax.all_to_all(packed, "uly", 0, 0, tiled=True).reshape(rows, 3 * features)
     other = lax.ppermute(own, "blk", swap)
     q_all = by_core(own[:, :features], other[:, :features])

time: 227 us -> 227 us (level)
  starting transfers between devices: 119 us -> 116 us
  waiting for transfers between devices: 9.67 us -> 12.6 us
    ppermute x7, starting transfers between devices: 27.9 us -> 22.6 us  [on_device(): b = lax.ppermute(b, 'blk', ring)]
    ppermute x8, waiting for transfers between devices: 7.25 us -> 10.2 us  [on_device(): a = lax.ppermute(a, 'blk', ring)]
  transfers between devices with their start and end apart: 18 -> 18, of which waited for: 4 -> 8; matrix products, arithmetic and copies ran while one was open for 1% -> 0% of each run, Pallas kernels for 10% -> 11%
where the time goes in v6:
time: 227 us; the launch traced here: 226 us
  starting transfers between devices  116 us (51%)
  blocking collectives  53.6 us (24%)
  Pallas kernels  26 us (11%)
  between operations  13.7 us (6%)
  waiting for transfers between devices  12.6 us (6%)
  local copies, waits for them, and re-layouts  2.27 us (1%)
    ppermute x8, starting transfers between devices, on_device(): a = lax.ppermute(a, 'blk', ring)  48 us
    ppermute x1, starting transfers between devices, on_device(): other = lax.ppermute(own, 'blk', swap)  40 us
    all_to_all x1, blocking collectives, on_device(): lax.all_to_all(partial.reshape(uly, tokens, width), 'uly', 0, 0, tiled=True)  34.4 us
    pallas_call x9, Pallas kernels, fold(): pl.pallas_call(functools.partial(fold_kernel, state is None), out_shape=j...  23 us
    ppermute x7, starting transfers between devices, on_device(): b = lax.ppermute(b, 'blk', ring)  22.6 us
    all_to_all x1, blocking collectives, on_device(): lax.all_to_all(packed, 'uly', 0, 0, tiled=True).reshape(rows, 3 * features)  19.1 us
    ppermute x8, waiting for transfers between devices, on_device(): a = lax.ppermute(a, 'blk', ring)  10.2 us
    ppermute x1, starting transfers between devices, on_device(): theirs = lax.ppermute(state, 'blk', swap)  5.69 us
  transfers between devices with their start and end apart: 18, of which 8 were waited for; matrix products, arithmetic and copies ran while one was open for 0% of the time, Pallas kernels for 11%

profile of v6, /device:TPU:65, one launch (start us, length us, event | category | flops | bytes accessed | tf_op | source)
XLA Modules:
  0.0 226.4 jit_solution(15536495943528791176)
XLA Ops:
  7.3 1.9 shard_map.55
  9.2 19.1 %all_to_all.10 = bf16[8,24,1152]{2,1,0:T(8,128)(2,1)S(1)} all-to-all(bf16[8,24,1152]{2,1,0:T(8,128)(2,1)} %shard_map.55), channel_id=1, replica_groups=mesh['group'=2,'blk'=32,'uly'=8] {'uly'}, dimensions={0} | all-to-all | bytes 884736 | tf_op jit(solution)/shard_map/all_to_all | solution.py:179
  28.3 40.0 %collective-permute-start = (bf16[192,1152]{1,0:T(8,128)(2,1)S(1)}, bf16[192,1152]{1,0:T(8,128)(2,1)S(1)}, u32[]{:S(2)}, u32[]{:S(2)}) collective-permute-start(bf16[192,1152]{1,0:T(8,128)(2,1)S(1)} %bitcast.6), channel_id=1, source_target_pairs={{0,8},{8,0},{16,24},{24,16},{32,40},{40,32},{48,56},{56,48},{64,72... | collective-permute-start | bytes 1327112 | tf_op jit(solution)/shard_map/ppermute | solution.py:180
  68.4 11.1 %collective-permute-start.1 = (bf16[192,768]{1,0:T(8,128)(2,1)S(1)}, bf16[192,768]{1,0:T(8,128)(2,1)S(1)}, u32[]{:S(2)}, u32[]{:S(2)}) collective-permute-start(bf16[192,768]{1,0:T(8,128)(2,1)S(1)} %slice.18.refs_0_), channel_id=1, source_target_pairs={{0,16},{8,248},{16,32},{24,8},{32,48},{40,24},{48,64},{56,40},{64,... | collective-permute-start | bytes 884744 | tf_op jit(solution)/shard_map/ppermute | solution.py:187
  79.5 4.8 %collective-permute-done.1.refs_0_ = bf16[192,768]{1,0:T(8,128)(2,1)S(1)} collective-permute-done((bf16[192,768]{1,0:T(8,128)(2,1)S(1)}, bf16[192,768]{1,0:T(8,128)(2,1)S(1)}, u32[]{:S(2)}, u32[]{:S(2)}) %collective-permute-start.1) | collective-permute-done | bytes 294944 | tf_op jit(solution)/shard_map/ppermute | solution.py:187
  84.2 5.4 %collective-permute-start.2 = (bf16[192,768]{1,0:T(8,128)(2,1)S(1)}, bf16[192,768]{1,0:T(8,128)(2,1)S(1)}, u32[]{:S(2)}, u32[]{:S(2)}) collective-permute-start(bf16[192,768]{1,0:T(8,128)(2,1)S(1)} %collective-permute-done.1.refs_0_), channel_id=1, source_target_pairs={{0,16},{8,248},{16,32},{24,8},{32,48},{40,24},{48,64},{56,40},{64,... | collective-permute-start | bytes 884744 | tf_op jit(solution)/shard_map/ppermute | solution.py:187
  89.7 2.0 collective-permute-start.9
  91.7 2.4 %collective-permute-done.2.refs_0_ = bf16[192,768]{1,0:T(8,128)(2,1)S(1)} collective-permute-done((bf16[192,768]{1,0:T(8,128)(2,1)S(1)}, bf16[192,768]{1,0:T(8,128)(2,1)S(1)}, u32[]{:S(2)}, u32[]{:S(2)}) %collective-permute-start.2) | collective-permute-done | bytes 294944 | tf_op jit(solution)/shard_map/ppermute | solution.py:187
  94.1 5.5 %collective-permute-start.3 = (bf16[192,768]{1,0:T(8,128)(2,1)S(1)}, bf16[192,768]{1,0:T(8,128)(2,1)S(1)}, u32[]{:S(2)}, u32[]{:S(2)}) collective-permute-start(bf16[192,768]{1,0:T(8,128)(2,1)S(1)} %collective-permute-done.2.refs_0_), channel_id=1, source_target_pairs={{0,16},{8,248},{16,32},{24,8},{32,48},{40,24},{48,64},{56,40},{64,... | collective-permute-start | bytes 884744 | tf_op jit(solution)/shard_map/ppermute | solution.py:187
  99.6 4.0 %collective-permute-start.10 = (bf16[192,768]{1,0:T(8,128)(2,1)S(1)}, bf16[192,768]{1,0:T(8,128)(2,1)S(1)}, u32[]{:S(2)}, u32[]{:S(2)}) collective-permute-start(bf16[192,768]{1,0:T(8,128)(2,1)S(1)} %collective-permute-done.9.refs_1_), channel_id=1, source_target_pairs={{0,16},{8,248},{16,32},{24,8},{32,48},{40,24},{48,64},{56,40},{64,... | collective-permute-start | bytes 884744 | tf_op jit(solution)/shard_map/ppermute | solution.py:189
  104.7 5.3 %collective-permute-start.4 = (bf16[192,768]{1,0:T(8,128)(2,1)S(1)}, bf16[192,768]{1,0:T(8,128)(2,1)S(1)}, u32[]{:S(2)}, u32[]{:S(2)}) collective-permute-start(bf16[192,768]{1,0:T(8,128)(2,1)S(1)} %collective-permute-done.3.refs_0_), channel_id=1, source_target_pairs={{0,16},{8,248},{16,32},{24,8},{32,48},{40,24},{48,64},{56,40},{64,... | collective-permute-start | bytes 884744 | tf_op jit(solution)/shard_map/ppermute | solution.py:187
  110.0 3.5 %collective-permute-start.11 = (bf16[192,768]{1,0:T(8,128)(2,1)S(1)}, bf16[192,768]{1,0:T(8,128)(2,1)S(1)}, u32[]{:S(2)}, u32[]{:S(2)}) collective-permute-start(bf16[192,768]{1,0:T(8,128)(2,1)S(1)} %collective-permute-done.10.refs_1_), channel_id=1, source_target_pairs={{0,16},{8,248},{16,32},{24,8},{32,48},{40,24},{48,64},{56,40},{64,... | collective-permute-start | bytes 884744 | tf_op jit(solution)/shard_map/ppermute | solution.py:189
  114.0 5.5 %collective-permute-start.5 = (bf16[192,768]{1,0:T(8,128)(2,1)S(1)}, bf16[192,768]{1,0:T(8,128)(2,1)S(1)}, u32[]{:S(2)}, u32[]{:S(2)}) collective-permute-start(bf16[192,768]{1,0:T(8,128)(2,1)S(1)} %collective-permute-done.4.refs_0_), channel_id=1, source_target_pairs={{0,16},{8,248},{16,32},{24,8},{32,48},{40,24},{48,64},{56,40},{64,... | collective-permute-start | bytes 884744 | tf_op jit(solution)/shard_map/ppermute | solution.py:187
  119.5 3.0 %collective-permute-start.12 = (bf16[192,768]{1,0:T(8,128)(2,1)S(1)}, bf16[192,768]{1,0:T(8,128)(2,1)S(1)}, u32[]{:S(2)}, u32[]{:S(2)}) collective-permute-start(bf16[192,768]{1,0:T(8,128)(2,1)S(1)} %collective-permute-done.11.refs_1_), channel_id=1, source_target_pairs={{0,16},{8,248},{16,32},{24,8},{32,48},{40,24},{48,64},{56,40},{64,... | collective-permute-start | bytes 884744 | tf_op jit(solution)/shard_map/ppermute | solution.py:189
  123.2 5.0 %collective-permute-start.6 = (bf16[192,768]{1,0:T(8,128)(2,1)S(1)}, bf16[192,768]{1,0:T(8,128)(2,1)S(1)}, u32[]{:S(2)}, u32[]{:S(2)}) collective-permute-start(bf16[192,768]{1,0:T(8,128)(2,1)S(1)} %collective-permute-done.5.refs_0_), channel_id=1, source_target_pairs={{0,16},{8,248},{16,32},{24,8},{32,48},{40,24},{48,64},{56,40},{64,... | collective-permute-start | bytes 884744 | tf_op jit(solution)/shard_map/ppermute | solution.py:187
  128.2 3.1 %collective-permute-start.13 = (bf16[192,768]{1,0:T(8,128)(2,1)S(1)}, bf16[192,768]{1,0:T(8,128)(2,1)}, u32[]{:S(2)}, u32[]{:S(2)}) collective-permute-start(bf16[192,768]{1,0:T(8,128)(2,1)S(1)} %collective-permute-done.12.refs_1_), channel_id=1, source_target_pairs={{0,16},{8,248},{16,32},{24,8},{32,48},{40,24},{48,64},{56,40},{64,... | collective-permute-start | bytes 884744 | tf_op jit(solution)/shard_map/ppermute | solution.py:189
  131.9 5.0 %collective-permute-start.7 = (bf16[192,768]{1,0:T(8,128)(2,1)S(1)}, bf16[192,768]{1,0:T(8,128)(2,1)S(1)}, u32[]{:S(2)}, u32[]{:S(2)}) collective-permute-start(bf16[192,768]{1,0:T(8,128)(2,1)S(1)} %collective-permute-done.6.refs_0_), channel_id=1, source_target_pairs={{0,16},{8,248},{16,32},{24,8},{32,48},{40,24},{48,64},{56,40},{64,... | collective-permute-start | bytes 884744 | tf_op jit(solution)/shard_map/ppermute | solution.py:187
  136.9 3.2 %collective-permute-start.14 = (bf16[192,768]{1,0:T(8,128)(2,1)}, bf16[192,768]{1,0:T(8,128)(2,1)}, u32[]{:S(2)}, u32[]{:S(2)}) collective-permute-start(bf16[192,768]{1,0:T(8,128)(2,1)} %collective-permute-done.13.refs_1_), channel_id=1, source_target_pairs={{0,16},{8,248},{16,32},{24,8},{32,48},{40,24},{48,64},{56,40},{64,... | collective-permute-start | bytes 884744 | tf_op jit(solution)/shard_map/ppermute | solution.py:189
  140.6 5.0 %collective-permute-start.8 = (bf16[192,768]{1,0:T(8,128)(2,1)S(1)}, bf16[192,768]{1,0:T(8,128)(2,1)S(1)}, u32[]{:S(2)}, u32[]{:S(2)}) collective-permute-start(bf16[192,768]{1,0:T(8,128)(2,1)S(1)} %collective-permute-done.7.refs_0_), channel_id=1, source_target_pairs={{0,16},{8,248},{16,32},{24,8},{32,48},{40,24},{48,64},{56,40},{64,... | collective-permute-start | bytes 884744 | tf_op jit(solution)/shard_map/ppermute | solution.py:187
  145.6 3.7 %collective-permute-start.15 = (bf16[192,768]{1,0:T(8,128)(2,1)}, bf16[192,768]{1,0:T(8,128)(2,1)S(1)}, u32[]{:S(2)}, u32[]{:S(2)}) collective-permute-start(bf16[192,768]{1,0:T(8,128)(2,1)} %collective-permute-done.14.refs_1_), channel_id=1, source_target_pairs={{0,16},{8,248},{16,32},{24,8},{32,48},{40,24},{48,64},{56,40},{64,... | collective-permute-start | bytes 884744 | tf_op jit(solution)/shard_map/ppermute | solution.py:189
  150.5 1.7 shard_map.56.refs_2_
  152.2 2.5 %shard_map.57.refs_2_ = f32[400,384]{1,0:T(8,128)S(1)} custom-call(bf16[384,384]{1,0:T(8,128)(2,1)S(1)} %maximum_multiply_fusion.q_ref, bf16[192,768]{1,0:T(8,128)(2,1)S(1)} %collective-permute-done.1.refs_0_, bf16[192,768]{1,0:T(8,128)(2,1)S(1)} %collective-permute-done.9.refs_1_, f32[400,384]{1,0:T(8,128)S(1)} %shard_map.56.refs_2_), custom_call_target="tpu_custom_call" | custom-call | flops 226492416 | bytes 589824 | tf_op jit(solution)/shard_map/pallas_call | solution.py:71
  154.7 2.5 %shard_map.58.refs_2_ = f32[400,384]{1,0:T(8,128)S(1)} custom-call(bf16[384,384]{1,0:T(8,128)(2,1)S(1)} %maximum_multiply_fusion.q_ref, bf16[192,768]{1,0:T(8,128)(2,1)S(1)} %collective-permute-done.2.refs_0_, bf16[192,768]{1,0:T(8,128)(2,1)S(1)} %collective-permute-done.10.refs_1_, f32[400,384]{1,0:T(8,128)S(1)} %shard_map.57.refs_2_), custom_call_target="tpu_custom_call" | custom-call | flops 226492416 | bytes 589824 | tf_op jit(solution)/shard_map/pallas_call | solution.py:71
  157.2 2.5 %shard_map.59.refs_2_ = f32[400,384]{1,0:T(8,128)S(1)} custom-call(bf16[384,384]{1,0:T(8,128)(2,1)S(1)} %maximum_multiply_fusion.q_ref, bf16[192,768]{1,0:T(8,128)(2,1)S(1)} %collective-permute-done.3.refs_0_, bf16[192,768]{1,0:T(8,128)(2,1)S(1)} %collective-permute-done.11.refs_1_, f32[400,384]{1,0:T(8,128)S(1)} %shard_map.58.refs_2_), custom_call_target="tpu_custom_call" | custom-call | flops 226492416 | bytes 589824 | tf_op jit(solution)/shard_map/pallas_call | solution.py:71
  159.7 2.5 %shard_map.60.refs_2_ = f32[400,384]{1,0:T(8,128)S(1)} custom-call(bf16[384,384]{1,0:T(8,128)(2,1)S(1)} %maximum_multiply_fusion.q_ref, bf16[192,768]{1,0:T(8,128)(2,1)S(1)} %collective-permute-done.4.refs_0_, bf16[192,768]{1,0:T(8,128)(2,1)S(1)} %collective-permute-done.12.refs_1_, f32[400,384]{1,0:T(8,128)S(1)} %shard_map.59.refs_2_), custom_call_target="tpu_custom_call" | custom-call | flops 226492416 | bytes 589824 | tf_op jit(solution)/shard_map/pallas_call | solution.py:71
  162.2 3.4 %shard_map.61.refs_2_ = f32[400,384]{1,0:T(8,128)S(1)} custom-call(bf16[384,384]{1,0:T(8,128)(2,1)S(1)} %maximum_multiply_fusion.q_ref, bf16[192,768]{1,0:T(8,128)(2,1)S(1)} %collective-permute-done.5.refs_0_, bf16[192,768]{1,0:T(8,128)(2,1)} %collective-permute-done.13.refs_1_, f32[400,384]{1,0:T(8,128)S(1)} %shard_map.60.refs_2_), custom_call_target="tpu_custom_call" | custom-call | flops 226492416 | bytes 589824 | tf_op jit(solution)/shard_map/pallas_call | solution.py:71
  165.6 3.7 %shard_map.62.refs_2_ = f32[400,384]{1,0:T(8,128)S(1)} custom-call(bf16[384,384]{1,0:T(8,128)(2,1)S(1)} %maximum_multiply_fusion.q_ref, bf16[192,768]{1,0:T(8,128)(2,1)S(1)} %collective-permute-done.6.refs_0_, bf16[192,768]{1,0:T(8,128)(2,1)} %collective-permute-done.14.refs_1_, f32[400,384]{1,0:T(8,128)S(1)} %shard_map.61.refs_2_), custom_call_target="tpu_custom_call" | custom-call | flops 226492416 | bytes 589824 | tf_op jit(solution)/shard_map/pallas_call | solution.py:71
  169.3 2.5 %shard_map.63.refs_1_ = f32[400,384]{1,0:T(8,128)S(1)} custom-call(bf16[384,384]{1,0:T(8,128)(2,1)S(1)} %maximum_multiply_fusion.q_ref, bf16[192,768]{1,0:T(8,128)(2,1)S(1)} %collective-permute-done.7.refs_0_, bf16[192,768]{1,0:T(8,128)(2,1)S(1)} %collective-permute-done.15.refs_1_, f32[400,384]{1,0:T(8,128)S(1)} %shard_map.62.refs_2_), custom_call_target="tpu_custom_call" | custom-call | flops 226492416 | bytes 589824 | tf_op jit(solution)/shard_map/pallas_call | solution.py:71
  171.8 1.8 shard_map.64.one_ref
  173.5 5.7 %collective-permute-start.16 = (f32[400,384]{1,0:T(8,128)S(1)}, f32[400,384]{1,0:T(8,128)S(1)}, u32[]{:S(2)}, u32[]{:S(2)}) collective-permute-start(f32[400,384]{1,0:T(8,128)S(1)} %shard_map.64.one_ref), channel_id=1, source_target_pairs={{0,8},{8,0},{16,24},{24,16},{32,40},{40,32},{48,56},{56,48},{64,72... | collective-permute-start | bytes 1843208 | tf_op jit(solution)/shard_map/ppermute | solution.py:191
  180.9 1.7 copy-done
  183.7 34.4 %all_to_all.11 = bf16[8,24,3072]{2,1,0:T(8,128)(2,1)S(1)} all-to-all(bf16[8,24,3072]{2,1,0:T(8,128)(2,1)S(1)} %bitcast.4), channel_id=1, replica_groups=mesh['group'=2,'blk'=32,'uly'=8] {'uly'}, dimensions={0} | all-to-all | bytes 2359296 | tf_op jit(solution)/shard_map/all_to_all | solution.py:193
  (32 shorter events, 9.0 us)
Async XLA Ops:
  6.5 174.3 %all-gather.2.cloned.1.call-start = ((), (), s32[]{:S(2)}) async-start(), calls=%async_computation.2 | async-start | bytes 2433024 | tf_op jit(solution)/shard_map/all_gather | solution.py:176
  28.3 108.6 %copy-start.1 = (bf16[8,24,1152]{2,1,0:T(8,128)(2,1)}, bf16[8,24,1152]{2,1,0:T(8,128)(2,1)S(1)}, u32[]{:S(2)}) copy-start(bf16[8,24,1152]{2,1,0:T(8,128)(2,1)S(1)} %all_to_all.10) | copy-start | bytes 1327108
  28.3 61.3 %collective-permute-start = (bf16[192,1152]{1,0:T(8,128)(2,1)S(1)}, bf16[192,1152]{1,0:T(8,128)(2,1)S(1)}, u32[]{:S(2)}, u32[]{:S(2)}) collective-permute-start(bf16[192,1152]{1,0:T(8,128)(2,1)S(1)} %bitcast.6), channel_id=1, source_target_pairs={{0,8},{8,0},{16,24},{24,16},{32,40},{40,32},{48,56},{56,48},{64,72... | collective-permute-start | bytes 1327112 | tf_op jit(solution)/shard_map/ppermute | solution.py:180
  68.4 15.8 %collective-permute-start.1 = (bf16[192,768]{1,0:T(8,128)(2,1)S(1)}, bf16[192,768]{1,0:T(8,128)(2,1)S(1)}, u32[]{:S(2)}, u32[]{:S(2)}) collective-permute-start(bf16[192,768]{1,0:T(8,128)(2,1)S(1)} %slice.18.refs_0_), channel_id=1, source_target_pairs={{0,16},{8,248},{16,32},{24,8},{32,48},{40,24},{48,64},{56,40},{64,... | collective-permute-start | bytes 884744 | tf_op jit(solution)/shard_map/ppermute | solution.py:187
  84.2 9.9 %collective-permute-start.2 = (bf16[192,768]{1,0:T(8,128)(2,1)S(1)}, bf16[192,768]{1,0:T(8,128)(2,1)S(1)}, u32[]{:S(2)}, u32[]{:S(2)}) collective-permute-start(bf16[192,768]{1,0:T(8,128)(2,1)S(1)} %collective-permute-done.1.refs_0_), channel_id=1, source_target_pairs={{0,16},{8,248},{16,32},{24,8},{32,48},{40,24},{48,64},{56,40},{64,... | collective-permute-start | bytes 884744 | tf_op jit(solution)/shard_map/ppermute | solution.py:187
  89.7 50.5 %copy-start.2 = (bf16[192,1152]{1,0:T(8,128)(2,1)}, bf16[192,1152]{1,0:T(8,128)(2,1)S(1)}, u32[]{:S(2)}) copy-start(bf16[192,1152]{1,0:T(8,128)(2,1)S(1)} %collective-permute-done) | copy-start | bytes 1327108
  89.7 9.9 %collective-permute-start.9 = (bf16[192,768]{1,0:T(8,128)(2,1)S(1)}, bf16[192,768]{1,0:T(8,128)(2,1)S(1)}, u32[]{:S(2)}, u32[]{:S(2)}) collective-permute-start(bf16[192,768]{1,0:T(8,128)(2,1)S(1)} %slice.19), channel_id=1, source_target_pairs={{0,16},{8,248},{16,32},{24,8},{32,48},{40,24},{48,64},{56,40},{64,... | collective-permute-start | bytes 884744 | tf_op jit(solution)/shard_map/ppermute | solution.py:189
  94.1 10.6 %collective-permute-start.3 = (bf16[192,768]{1,0:T(8,128)(2,1)S(1)}, bf16[192,768]{1,0:T(8,128)(2,1)S(1)}, u32[]{:S(2)}, u32[]{:S(2)}) collective-permute-start(bf16[192,768]{1,0:T(8,128)(2,1)S(1)} %collective-permute-done.2.refs_0_), channel_id=1, source_target_pairs={{0,16},{8,248},{16,32},{24,8},{32,48},{40,24},{48,64},{56,40},{64,... | collective-permute-start | bytes 884744 | tf_op jit(solution)/shard_map/ppermute | solution.py:187
  99.6 10.4 %collective-permute-start.10 = (bf16[192,768]{1,0:T(8,128)(2,1)S(1)}, bf16[192,768]{1,0:T(8,128)(2,1)S(1)}, u32[]{:S(2)}, u32[]{:S(2)}) collective-permute-start(bf16[192,768]{1,0:T(8,128)(2,1)S(1)} %collective-permute-done.9.refs_1_), channel_id=1, source_target_pairs={{0,16},{8,248},{16,32},{24,8},{32,48},{40,24},{48,64},{56,40},{64,... | collective-permute-start | bytes 884744 | tf_op jit(solution)/shard_map/ppermute | solution.py:189
  104.7 9.3 %collective-permute-start.4 = (bf16[192,768]{1,0:T(8,128)(2,1)S(1)}, bf16[192,768]{1,0:T(8,128)(2,1)S(1)}, u32[]{:S(2)}, u32[]{:S(2)}) collective-permute-start(bf16[192,768]{1,0:T(8,128)(2,1)S(1)} %collective-permute-done.3.refs_0_), channel_id=1, source_target_pairs={{0,16},{8,248},{16,32},{24,8},{32,48},{40,24},{48,64},{56,40},{64,... | collective-permute-start | bytes 884744 | tf_op jit(solution)/shard_map/ppermute | solution.py:187
  110.0 9.5 %collective-permute-start.11 = (bf16[192,768]{1,0:T(8,128)(2,1)S(1)}, bf16[192,768]{1,0:T(8,128)(2,1)S(1)}, u32[]{:S(2)}, u32[]{:S(2)}) collective-permute-start(bf16[192,768]{1,0:T(8,128)(2,1)S(1)} %collective-permute-done.10.refs_1_), channel_id=1, source_target_pairs={{0,16},{8,248},{16,32},{24,8},{32,48},{40,24},{48,64},{56,40},{64,... | collective-permute-start | bytes 884744 | tf_op jit(solution)/shard_map/ppermute | solution.py:189
  114.0 9.2 %collective-permute-start.5 = (bf16[192,768]{1,0:T(8,128)(2,1)S(1)}, bf16[192,768]{1,0:T(8,128)(2,1)S(1)}, u32[]{:S(2)}, u32[]{:S(2)}) collective-permute-start(bf16[192,768]{1,0:T(8,128)(2,1)S(1)} %collective-permute-done.4.refs_0_), channel_id=1, source_target_pairs={{0,16},{8,248},{16,32},{24,8},{32,48},{40,24},{48,64},{56,40},{64,... | collective-permute-start | bytes 884744 | tf_op jit(solution)/shard_map/ppermute | solution.py:187
  119.5 8.7 %collective-permute-start.12 = (bf16[192,768]{1,0:T(8,128)(2,1)S(1)}, bf16[192,768]{1,0:T(8,128)(2,1)S(1)}, u32[]{:S(2)}, u32[]{:S(2)}) collective-permute-start(bf16[192,768]{1,0:T(8,128)(2,1)S(1)} %collective-permute-done.11.refs_1_), channel_id=1, source_target_pairs={{0,16},{8,248},{16,32},{24,8},{32,48},{40,24},{48,64},{56,40},{64,... | collective-permute-start | bytes 884744 | tf_op jit(solution)/shard_map/ppermute | solution.py:189
  123.2 8.7 %collective-permute-start.6 = (bf16[192,768]{1,0:T(8,128)(2,1)S(1)}, bf16[192,768]{1,0:T(8,128)(2,1)S(1)}, u32[]{:S(2)}, u32[]{:S(2)}) collective-permute-start(bf16[192,768]{1,0:T(8,128)(2,1)S(1)} %collective-permute-done.5.refs_0_), channel_id=1, source_target_pairs={{0,16},{8,248},{16,32},{24,8},{32,48},{40,24},{48,64},{56,40},{64,... | collective-permute-start | bytes 884744 | tf_op jit(solution)/shard_map/ppermute | solution.py:187
  128.2 8.7 %collective-permute-start.13 = (bf16[192,768]{1,0:T(8,128)(2,1)S(1)}, bf16[192,768]{1,0:T(8,128)(2,1)}, u32[]{:S(2)}, u32[]{:S(2)}) collective-permute-start(bf16[192,768]{1,0:T(8,128)(2,1)S(1)} %collective-permute-done.12.refs_1_), channel_id=1, source_target_pairs={{0,16},{8,248},{16,32},{24,8},{32,48},{40,24},{48,64},{56,40},{64,... | collective-permute-start | bytes 884744 | tf_op jit(solution)/shard_map/ppermute | solution.py:189
  131.9 8.7 %collective-permute-start.7 = (bf16[192,768]{1,0:T(8,128)(2,1)S(1)}, bf16[192,768]{1,0:T(8,128)(2,1)S(1)}, u32[]{:S(2)}, u32[]{:S(2)}) collective-permute-start(bf16[192,768]{1,0:T(8,128)(2,1)S(1)} %collective-permute-done.6.refs_0_), channel_id=1, source_target_pairs={{0,16},{8,248},{16,32},{24,8},{32,48},{40,24},{48,64},{56,40},{64,... | collective-permute-start | bytes 884744 | tf_op jit(solution)/shard_map/ppermute | solution.py:187
  136.9 8.7 %collective-permute-start.14 = (bf16[192,768]{1,0:T(8,128)(2,1)}, bf16[192,768]{1,0:T(8,128)(2,1)}, u32[]{:S(2)}, u32[]{:S(2)}) collective-permute-start(bf16[192,768]{1,0:T(8,128)(2,1)} %collective-permute-done.13.refs_1_), channel_id=1, source_target_pairs={{0,16},{8,248},{16,32},{24,8},{32,48},{40,24},{48,64},{56,40},{64,... | collective-permute-start | bytes 884744 | tf_op jit(solution)/shard_map/ppermute | solution.py:189
  140.6 31.2 %collective-permute-start.8 = (bf16[192,768]{1,0:T(8,128)(2,1)S(1)}, bf16[192,768]{1,0:T(8,128)(2,1)S(1)}, u32[]{:S(2)}, u32[]{:S(2)}) collective-permute-start(bf16[192,768]{1,0:T(8,128)(2,1)S(1)} %collective-permute-done.7.refs_0_), channel_id=1, source_target_pairs={{0,16},{8,248},{16,32},{24,8},{32,48},{40,24},{48,64},{56,40},{64,... | collective-permute-start | bytes 884744 | tf_op jit(solution)/shard_map/ppermute | solution.py:187
  145.6 23.6 %collective-permute-start.15 = (bf16[192,768]{1,0:T(8,128)(2,1)}, bf16[192,768]{1,0:T(8,128)(2,1)S(1)}, u32[]{:S(2)}, u32[]{:S(2)}) collective-permute-start(bf16[192,768]{1,0:T(8,128)(2,1)} %collective-permute-done.14.refs_1_), channel_id=1, source_target_pairs={{0,16},{8,248},{16,32},{24,8},{32,48},{40,24},{48,64},{56,40},{64,... | collective-permute-start | bytes 884744 | tf_op jit(solution)/shard_map/ppermute | solution.py:189
  173.5 7.3 %collective-permute-start.16 = (f32[400,384]{1,0:T(8,128)S(1)}, f32[400,384]{1,0:T(8,128)S(1)}, u32[]{:S(2)}, u32[]{:S(2)}) collective-permute-start(f32[400,384]{1,0:T(8,128)S(1)} %shard_map.64.one_ref), channel_id=1, source_target_pairs={{0,8},{8,0},{16,24},{24,16},{32,40},{40,32},{48,56},{56,48},{64,72... | collective-permute-start | bytes 1843208 | tf_op jit(solution)/shard_map/ppermute | solution.py:191
  180.9 1.7 copy-start
  218.1 0.7 copy-start.3
Sparse Core Ops, SparseCore 0:
  9.5 110.0 all-gather.1
